TPU v7x, 32 devices: a whole 2x2x4 slice. The times are simulated.
32 devices in a mesh: fsdp: 2 (over x), blk: 4 (over y, core), uly: 4 (over z).
Axes of the slice: x: 2, y: 2, z: 4, core: 2. Of those that a mesh axis runs over, the one named last changes fastest.
Arguments:
- inputs: bfloat16 [4, 1024, 1024], P('fsdp', ('blk', 'uly')), may hold values from -36 to 36
- segments: int32 [4, 1024], P('fsdp'), may hold values from 0 to 3, never falling along the last dimension, each value on 1 to 512 neighbouring positions
- attn_gain: bfloat16 [1024], P(('fsdp', 'blk', 'uly')), may hold values from 0.5 to 1.5
- head_gains: bfloat16 [2, 128], replicated, may hold values from 0.5 to 1.5
- query_weight: bfloat16 [1024, 2048], P(('fsdp', 'blk', 'uly')), may hold values from -0.1875 to 0.1875
- key_matrix: bfloat16 [1024, 1024], P(('fsdp', 'blk', 'uly')), may hold values from -0.1875 to 0.1875
- value_matrix: bfloat16 [1024, 1024], P(('fsdp', 'blk', 'uly')), may hold values from -0.1875 to 0.1875
- out_weight: bfloat16 [2048, 1024], P(('fsdp', 'blk', 'uly')), may hold values from -1.5 to 1.5
- ffn_gain: bfloat16 [1024], P(('fsdp', 'blk', 'uly')), may hold values from 0.5 to 1.5
- gate_weight: bfloat16 [1024, 3072], P(('fsdp', 'blk', 'uly')), may hold values from -0.1875 to 0.1875
- up_weight: bfloat16 [1024, 3072], P(('fsdp', 'blk', 'uly')), may hold values from -0.1875 to 0.1875
- down_weight: bfloat16 [3072, 1024], P(('fsdp', 'blk', 'uly')), may hold values from -0.109375 to 0.109375
- cotangent: bfloat16 [4, 1024, 1024], P('fsdp', ('blk', 'uly')), may hold values from -6 to 6
Outputs:
- outputs: bfloat16 [4, 1024, 1024], P('fsdp', ('blk', 'uly'))
- grad_inputs: bfloat16 [4, 1024, 1024], P('fsdp', ('blk', 'uly'))
- grad_attn_gain: float32 [1024], P(('fsdp', 'blk', 'uly'))
- grad_head_gains: float32 [2, 128], P(None, ('fsdp', 'blk', 'uly'))
- grad_query_weight: float32 [1024, 2048], P(('fsdp', 'blk', 'uly'))
- grad_key_weight: float32 [1024, 1024], P(('fsdp', 'blk', 'uly'))
- grad_value_weight: float32 [1024, 1024], P(('fsdp', 'blk', 'uly'))
- grad_out_weight: float32 [2048, 1024], P(('fsdp', 'blk', 'uly'))
- grad_ffn_gain: float32 [1024], P(('fsdp', 'blk', 'uly'))
- grad_gate_weight: float32 [1024, 3072], P(('fsdp', 'blk', 'uly'))
- grad_up_weight: float32 [1024, 3072], P(('fsdp', 'blk', 'uly'))
- grad_down_weight: float32 [3072, 1024], P(('fsdp', 'blk', 'uly'))
Inputs may be any that keep to these rules, and one draw needn't show every extreme that they name: `segments`: document numbers never fall along a sequence; every document has 1 to 512 tokens, and one of each sequence has exactly 512.
All inputs are finite; a program needn't handle non-finite values.
Results may differ from a plain program's by a relative error of at most 0.017.
Values may be sent and summed in bfloat16 or wider, within the bound.
A program may use at most 192 MiB of HBM per device.

v0:
```python
import math

import jax
import jax.numpy as jnp
from jax import lax
from jax.sharding import PartitionSpec as P

DOCS = 4


EPSILON = 1e-06
THETA = 1000000.0


def passed_along(value, axis, steps):
    count = lax.axis_size(axis)
    first, last = (max(0, -steps), min(count, count - steps))
    return lax.ppermute(value, axis, [(source, source + steps) for source in range(first, last)])


def from_behind(value, axis, steps):
    count = lax.axis_size(axis)
    pairs = [(source, (source + steps) % count) for source in range(count)]
    return lax.ppermute(value, axis, pairs)


def rms_norm(vector, weight):
    mean_square = jnp.mean(vector * vector, axis=-1, keepdims=True)
    return vector * lax.rsqrt(mean_square + EPSILON) * weight


def rotate(vector, cosine, sine_table):
    half_width = vector.shape[-1] // 2
    turned = jnp.concatenate([-vector[..., half_width:], vector[..., :half_width]], axis=-1)
    return vector * cosine + turned * sine_table


def prepare(query_pre, key_before_rotate, gains, cosine, sine_table):
    cos_heads = cosine[:, :, None, :]
    sin_heads = sine_table[:, :, None, :]
    query_rot = rotate(rms_norm(query_pre, gains[0]), cos_heads, sin_heads)
    key_rot = rotate(rms_norm(key_before_rotate, gains[1]), cos_heads, sin_heads)
    return (query_rot, key_rot)


def swiglu(gate_rows, up_rows):
    return jax.nn.silu(gate_rows) * up_rows


def fetch_attention(attn_gain, query_weight, key_matrix, value_matrix, out_weight):
    return (
        lax.all_gather(attn_gain, ("fsdp", "blk", "uly"), axis=0, tiled=True),
        lax.all_gather(query_weight, ("fsdp", "blk", "uly"), axis=0, tiled=True),
        lax.all_gather(key_matrix, ("fsdp", "blk", "uly"), axis=0, tiled=True),
        lax.all_gather(value_matrix, ("fsdp", "blk", "uly"), axis=0, tiled=True),
        lax.all_gather(out_weight, ("fsdp", "blk", "uly"), axis=0, tiled=True),
    )


def fetch_feedforward(ffn_gain, gate_weight, up_weight, down_weight):
    return (
        lax.all_gather(ffn_gain, ("fsdp", "blk", "uly"), axis=0, tiled=True),
        lax.all_gather(gate_weight, ("fsdp", "blk", "uly"), axis=0, tiled=True),
        lax.all_gather(up_weight, ("fsdp", "blk", "uly"), axis=0, tiled=True),
        lax.all_gather(down_weight, ("fsdp", "blk", "uly"), axis=0, tiled=True),
    )


def body(
    inputs,
    segments,
    attn_gain,
    head_gains,
    query_weight,
    key_matrix,
    value_matrix,
    out_weight,
    ffn_gain,
    gate_weight,
    up_weight,
    down_weight,
    cotangent,
):
    seq_count, tok_count, model_width = inputs.shape
    head_dim = head_gains.shape[1]
    query_heads = query_weight.shape[1] // head_dim
    value_heads = key_matrix.shape[1] // head_dim
    heads_per_group = query_heads // value_heads
    uly_size = lax.axis_size("uly")
    blk_size = lax.axis_size("blk")
    blk_index = lax.axis_index("blk")
    uly_index = lax.axis_index("uly")
    offset = (blk_index * uly_size + uly_index) * tok_count
    doc_ids = jnp.arange(DOCS, dtype=jnp.int32)
    starts = jnp.sum((segments[:, None, :] < doc_ids[None, :, None]).astype(jnp.int32), axis=2)
    local_segs = lax.dynamic_slice_in_dim(segments, offset, tok_count, 1)
    doc_start = jnp.sum(
        jnp.where(local_segs[:, :, None] == doc_ids[None, None, :], starts[:, None, :], 0), axis=2
    )
    token_place = (offset + jnp.arange(tok_count, dtype=jnp.int32)[None, :] - doc_start).astype(
        jnp.float32
    )
    inverse = jnp.exp(
        jnp.arange(head_dim // 2, dtype=jnp.float32) * (-2.0 * math.log(THETA) / head_dim)
    )
    angles = token_place[..., None] * inverse
    cosine = jnp.concatenate([jnp.cos(angles), jnp.cos(angles)], axis=-1)
    sine_table = jnp.concatenate([jnp.sin(angles), jnp.sin(angles)], axis=-1)
    floats = inputs.astype(jnp.float32)
    gain_one, query_full, key_full, value_full, out_full = fetch_attention(
        attn_gain, query_weight, key_matrix, value_matrix, out_weight
    )
    normed_float, norm_pull_one = jax.vjp(rms_norm, floats, gain_one.astype(jnp.float32))
    normalized_input = normed_float.astype(jnp.bfloat16)
    query_pre = jnp.einsum(
        "std,de->ste", normalized_input, query_full, preferred_element_type=jnp.float32
    ).reshape(seq_count, tok_count, query_heads, head_dim)
    key_before_rotate = jnp.einsum(
        "std,de->ste", normalized_input, key_full, preferred_element_type=jnp.float32
    ).reshape(seq_count, tok_count, value_heads, head_dim)
    rows_of_value = (
        jnp.einsum("std,de->ste", normalized_input, value_full, preferred_element_type=jnp.float32)
        .astype(jnp.bfloat16)
        .reshape(seq_count, tok_count, value_heads, head_dim)
    )
    head_float = head_gains.astype(jnp.float32)

    def prepare_local(query_arg, key_arg, gains_arg):
        return prepare(query_arg, key_arg, gains_arg, cosine, sine_table)

    (query_rot, key_rot), prep_pull = jax.vjp(
        prepare_local, query_pre, key_before_rotate, head_float
    )
    query_local, key_local, value_local = (
        lax.all_to_all(
            query_rot.astype(jnp.bfloat16), "uly", split_axis=2, concat_axis=1, tiled=True
        ),
        lax.all_to_all(
            key_rot.astype(jnp.bfloat16), "uly", split_axis=2, concat_axis=1, tiled=True
        ),
        lax.all_to_all(rows_of_value, "uly", split_axis=2, concat_axis=1, tiled=True),
    )
    block_len = query_local.shape[1]
    local_kv = key_local.shape[2]
    query_group = query_local.reshape(seq_count, block_len, local_kv, heads_per_group, head_dim)
    bound = math.sqrt(head_dim) * jnp.max(jnp.abs(head_float[0])) * jnp.max(jnp.abs(head_float[1]))
    scale = head_dim ** (-0.5)
    query_index = blk_index * block_len + jnp.arange(block_len, dtype=jnp.int32)
    query_segs = lax.dynamic_slice_in_dim(segments, blk_index * block_len, block_len, 1)

    def block_weights(keys_in, source):
        key_index = source * block_len + jnp.arange(block_len, dtype=jnp.int32)
        key_segs = lax.dynamic_slice_in_dim(segments, source * block_len, block_len, 1)
        allowed = (key_index[None, None, :] <= query_index[None, :, None]) & (
            key_segs[:, None, :] == query_segs[:, :, None]
        )
        scores = (
            jnp.einsum(
                "sqhgd,skhd->shgqk", query_group, keys_in, preferred_element_type=jnp.float32
            )
            * scale
        )
        return jnp.where(allowed[:, None, None], jnp.exp(scores - bound), 0.0)

    def absorb(stats, key_value, source):
        row_sums, summed = stats
        weights = block_weights(key_value[0], source)
        row_sums = row_sums + jnp.sum(weights, axis=-1)
        summed = summed + jnp.einsum(
            "shgqk,skhd->sqhgd",
            weights.astype(jnp.bfloat16),
            key_value[1],
            preferred_element_type=jnp.float32,
        )
        return (row_sums, summed)

    own_pair = jnp.stack([key_local, value_local])
    start_stats = (
        jnp.zeros((seq_count, local_kv, heads_per_group, block_len), jnp.float32),
        jnp.zeros((seq_count, block_len, local_kv, heads_per_group, head_dim), jnp.float32),
    )
    first_stats = absorb(start_stats, own_pair, blk_index)

    def forward_turn(turn_index, carry):
        key_value, stats_in = carry
        key_value = passed_along(key_value, "blk", 1)
        stats_in = lax.cond(
            turn_index <= blk_index,
            lambda holding: absorb(holding, key_value, blk_index - turn_index),
            lambda holding: holding,
            stats_in,
        )
        return (key_value, stats_in)

    moved_pair, (row_totals, summed_all) = lax.fori_loop(
        1, blk_size, forward_turn, (own_pair, first_stats)
    )
    attended = summed_all / jnp.transpose(row_totals, (0, 3, 1, 2))[..., None]
    attended_tok = lax.all_to_all(
        attended.reshape(seq_count, block_len, local_kv * heads_per_group, head_dim).astype(
            jnp.bfloat16
        ),
        "uly",
        split_axis=1,
        concat_axis=2,
        tiled=True,
    ).reshape(seq_count, tok_count, query_heads * head_dim)
    middle = floats + jnp.einsum(
        "ste,ed->std", attended_tok, out_full, preferred_element_type=jnp.float32
    )
    gain_two, gate_full, up_full, down_full = fetch_feedforward(
        ffn_gain, gate_weight, up_weight, down_weight
    )
    normed_two_float, norm_pull_two = jax.vjp(rms_norm, middle, gain_two.astype(jnp.float32))
    normed_two = normed_two_float.astype(jnp.bfloat16)
    gate_rows = jnp.einsum("std,df->stf", normed_two, gate_full, preferred_element_type=jnp.float32)
    up_rows = jnp.einsum("std,df->stf", normed_two, up_full, preferred_element_type=jnp.float32)
    hidden_float, swiglu_pull = jax.vjp(swiglu, gate_rows, up_rows)
    hidden = hidden_float.astype(jnp.bfloat16)
    outputs = (
        middle + jnp.einsum("stf,fd->std", hidden, down_full, preferred_element_type=jnp.float32)
    ).astype(jnp.bfloat16)
    refetched = fetch_feedforward(ffn_gain, gate_weight, up_weight, down_weight)
    gate_back, up_back, down_back = (refetched[1], refetched[2], refetched[3])
    grad_out = cotangent.astype(jnp.float32)
    down_grad = jnp.einsum("stf,std->fd", hidden, cotangent, preferred_element_type=jnp.float32)
    grad_hidden = jnp.einsum(
        "std,fd->stf", cotangent, down_back, preferred_element_type=jnp.float32
    )
    grad_gate, grad_up = swiglu_pull(grad_hidden)
    grad_gate = grad_gate.astype(jnp.bfloat16)
    grad_up = grad_up.astype(jnp.bfloat16)
    gate_grad = jnp.einsum("std,stf->df", normed_two, grad_gate, preferred_element_type=jnp.float32)
    up_grad = jnp.einsum("std,stf->df", normed_two, grad_up, preferred_element_type=jnp.float32)
    grad_normed_two = jnp.einsum(
        "stf,df->std", grad_gate, gate_back, preferred_element_type=jnp.float32
    ) + jnp.einsum("stf,df->std", grad_up, up_back, preferred_element_type=jnp.float32)
    middle_part, gain_two_grad = norm_pull_two(grad_normed_two)
    grad_middle = grad_out + middle_part
    ffn_shares = (
        lax.psum_scatter(gain_two_grad, ("fsdp", "blk", "uly"), scatter_dimension=0, tiled=True),
        lax.psum_scatter(gate_grad, ("fsdp", "blk", "uly"), scatter_dimension=0, tiled=True),
        lax.psum_scatter(up_grad, ("fsdp", "blk", "uly"), scatter_dimension=0, tiled=True),
        lax.psum_scatter(down_grad, ("fsdp", "blk", "uly"), scatter_dimension=0, tiled=True),
    )
    fetched_again = fetch_attention(attn_gain, query_weight, key_matrix, value_matrix, out_weight)
    query_back, key_back, value_back, out_back = (
        fetched_again[1],
        fetched_again[2],
        fetched_again[3],
        fetched_again[4],
    )
    grad_middle_low = grad_middle.astype(jnp.bfloat16)
    out_grad = jnp.einsum(
        "ste,std->ed", attended_tok, grad_middle_low, preferred_element_type=jnp.float32
    )
    grad_att_tok = (
        jnp.einsum("std,ed->ste", grad_middle_low, out_back, preferred_element_type=jnp.float32)
        .astype(jnp.bfloat16)
        .reshape(seq_count, tok_count, query_heads, head_dim)
    )
    grad_att = lax.all_to_all(grad_att_tok, "uly", split_axis=2, concat_axis=1, tiled=True).reshape(
        seq_count, block_len, local_kv, heads_per_group, head_dim
    )
    delta = jnp.transpose(jnp.sum(grad_att.astype(jnp.float32) * attended, axis=-1), (0, 2, 3, 1))

    def block_grads(key_value, source):
        keys_in = key_value[0]
        values_in = key_value[1]
        probs = block_weights(keys_in, source) / row_totals[..., None]
        grad_probs = jnp.einsum(
            "sqhgd,skhd->shgqk", grad_att, values_in, preferred_element_type=jnp.float32
        )
        grad_scores = (probs * (grad_probs - delta[..., None])).astype(jnp.bfloat16)
        grad_query = (
            jnp.einsum(
                "shgqk,skhd->sqhgd", grad_scores, keys_in, preferred_element_type=jnp.float32
            )
            * scale
        )
        grad_keys = (
            jnp.einsum(
                "shgqk,sqhgd->skhd", grad_scores, query_group, preferred_element_type=jnp.float32
            )
            * scale
        )
        grad_values = jnp.einsum(
            "shgqk,sqhgd->skhd",
            probs.astype(jnp.bfloat16),
            grad_att,
            preferred_element_type=jnp.float32,
        )
        return (grad_query, jnp.stack([grad_keys, grad_values]))

    def pass_grads(moving):
        return from_behind(moving.astype(jnp.bfloat16), "blk", 1).astype(moving.dtype)

    query_start, pair_start = block_grads(own_pair, blk_index)

    def backward_turn(turn_index, carry):
        key_value, query_acc, pair_acc = carry
        key_value = passed_along(key_value, "blk", 1)
        pair_acc = pass_grads(pair_acc)

        def accumulate(holding):
            part_query, part_pair = block_grads(key_value, blk_index - turn_index)
            return (holding[0] + part_query, holding[1] + part_pair)

        query_acc, pair_acc = lax.cond(
            turn_index <= blk_index, accumulate, lambda holding: holding, (query_acc, pair_acc)
        )
        return (key_value, query_acc, pair_acc)

    spent_pair, query_total, pair_total = lax.fori_loop(
        1, blk_size, backward_turn, (own_pair, query_start, pair_start)
    )
    pair_total = pass_grads(pair_total)
    grad_query_low = query_total.reshape(
        seq_count, block_len, local_kv * heads_per_group, head_dim
    ).astype(jnp.bfloat16)
    grad_query_tok, grad_key_tok, grad_value_tok = (
        lax.all_to_all(grad_query_low, "uly", split_axis=1, concat_axis=2, tiled=True),
        lax.all_to_all(
            pair_total[0].astype(jnp.bfloat16), "uly", split_axis=1, concat_axis=2, tiled=True
        ),
        lax.all_to_all(
            pair_total[1].astype(jnp.bfloat16), "uly", split_axis=1, concat_axis=2, tiled=True
        ),
    )
    grad_query_pre, grad_key_pre, heads_grad = prep_pull(
        (grad_query_tok.astype(jnp.float32), grad_key_tok.astype(jnp.float32))
    )
    grad_query_flat = grad_query_pre.astype(jnp.bfloat16).reshape(
        seq_count, tok_count, query_heads * head_dim
    )
    grad_key_flat = grad_key_pre.astype(jnp.bfloat16).reshape(
        seq_count, tok_count, value_heads * head_dim
    )
    grad_value_flat = grad_value_tok.reshape(seq_count, tok_count, value_heads * head_dim)
    query_grad = jnp.einsum(
        "std,ste->de", normalized_input, grad_query_flat, preferred_element_type=jnp.float32
    )
    key_grad = jnp.einsum(
        "std,ste->de", normalized_input, grad_key_flat, preferred_element_type=jnp.float32
    )
    value_grad = jnp.einsum(
        "std,ste->de", normalized_input, grad_value_flat, preferred_element_type=jnp.float32
    )
    grad_normed = jnp.einsum(
        "ste,de->std", grad_query_flat, query_back, preferred_element_type=jnp.float32
    )
    grad_normed = grad_normed + jnp.einsum(
        "ste,de->std", grad_key_flat, key_back, preferred_element_type=jnp.float32
    )
    grad_normed = grad_normed + jnp.einsum(
        "ste,de->std", grad_value_flat, value_back, preferred_element_type=jnp.float32
    )
    input_part, gain_one_grad = norm_pull_one(grad_normed)
    input_grad = (grad_middle + input_part).astype(jnp.bfloat16)
    attn_shares = (
        lax.psum_scatter(gain_one_grad, ("fsdp", "blk", "uly"), scatter_dimension=0, tiled=True),
        lax.psum_scatter(heads_grad, ("fsdp", "blk", "uly"), scatter_dimension=1, tiled=True),
        lax.psum_scatter(query_grad, ("fsdp", "blk", "uly"), scatter_dimension=0, tiled=True),
        lax.psum_scatter(key_grad, ("fsdp", "blk", "uly"), scatter_dimension=0, tiled=True),
        lax.psum_scatter(value_grad, ("fsdp", "blk", "uly"), scatter_dimension=0, tiled=True),
        lax.psum_scatter(out_grad, ("fsdp", "blk", "uly"), scatter_dimension=0, tiled=True),
    )
    return (
        outputs,
        input_grad,
        attn_shares[0],
        attn_shares[1],
        attn_shares[2],
        attn_shares[3],
        attn_shares[4],
        attn_shares[5],
        ffn_shares[0],
        ffn_shares[1],
        ffn_shares[2],
        ffn_shares[3],
    )


def solution(mesh):
    return jax.shard_map(
        body,
        mesh=mesh,
        in_specs=(
            P("fsdp", ("blk", "uly"), None),
            P("fsdp", None),
            P(("fsdp", "blk", "uly")),
            P(),
            P(("fsdp", "blk", "uly"), None),
            P(("fsdp", "blk", "uly"), None),
            P(("fsdp", "blk", "uly"), None),
            P(("fsdp", "blk", "uly"), None),
            P(("fsdp", "blk", "uly")),
            P(("fsdp", "blk", "uly"), None),
            P(("fsdp", "blk", "uly"), None),
            P(("fsdp", "blk", "uly"), None),
            P("fsdp", ("blk", "uly"), None),
        ),
        out_specs=(
            P("fsdp", ("blk", "uly"), None),
            P("fsdp", ("blk", "uly"), None),
            P(("fsdp", "blk", "uly")),
            P(None, ("fsdp", "blk", "uly")),
            P(("fsdp", "blk", "uly"), None),
            P(("fsdp", "blk", "uly"), None),
            P(("fsdp", "blk", "uly"), None),
            P(("fsdp", "blk", "uly"), None),
            P(("fsdp", "blk", "uly")),
            P(("fsdp", "blk", "uly"), None),
            P(("fsdp", "blk", "uly"), None),
            P(("fsdp", "blk", "uly"), None),
        ),
        check_vma=False,
    )
```

profile of v0, /device:TPU:0, one launch (start us, length us, event | category | flops | bytes accessed | tf_op | source)
XLA Modules:
  0.0 1771.8 jit_solution(2439551218924024467)
XLA Ops:
  13.6 42.1 %all-reduce.12 = (bf16[1024]{0:T(1024)(128)(2,1)S(1)}, bf16[1024]{0:T(1024)(128)(2,1)}) all-reduce(bf16[1024]{0:T(1024)(128)(2,1)S(1)} %dynamic-update-slice, bf16[1024]{0:T(1024)(128)(2,1)S(1)} %dynamic-update-slice.1), channel_id=1, replica_groups=mesh['fsdp'=2,'blk'=4,'uly'=4] {'fsdp','blk','uly'}, use_global_device_ids=true, to_apply=%add.6 | all-reduce | flops 2048 | bytes 8192
  76.5 52.2 %all-gather.8.cloned.1.call-done = bf16[1024,1024]{1,0:T(8,128)(2,1)} async-done(((bf16[32,1024]{1,0:T(8,128)(2,1)}), bf16[1024,1024]{1,0:T(8,128)(2,1)}) %all-gather.8.cloned.1.call-update) | async-done | bytes 2097168 | tf_op jit(solution)/shard_map/all_gather | solution.py:54
  132.7 59.5 %all-gather.12.cloned.1.call-done = bf16[1024,2048]{1,0:T(8,128)(2,1)} async-done(((bf16[32,2048]{1,0:T(8,128)(2,1)}), bf16[1024,2048]{1,0:T(8,128)(2,1)}) %all-gather.12.cloned.1.call-update) | async-done | bytes 4194320 | tf_op jit(solution)/shard_map/all_gather | solution.py:53
  215.9 15.9 all-to-all-done.2
  236.4 35.8 %while.36 = (s32[]{:T(128)}, bf16[2,2,256,2,128]{4,2,3,1,0:T(8,128)(2,1)}, f32[2,2,2,256]{3,2,1,0:T(2,128)S(1)}, f32[2,256,2,2,128]{4,1,3,2,0:T(8,128)S(1)}, s32...) while((s32[]{:T(128)}, ...), condition=%wide.region_12.13_spmd.clone, body=%wide.region_8.12_spmd.clone.sunk | while | flops 271647232 | bytes 8829293 | solution.py:195
  241.0 17.1 collective-permute-start
  277.7 10.3 all-to-all-done.3
  292.3 44.3 %all-gather.20.cloned.1.call-done = bf16[3072,1024]{1,0:T(8,128)(2,1)} async-done(((bf16[96,1024]{1,0:T(8,128)(2,1)}), bf16[3072,1024]{1,0:T(8,128)(2,1)}) %all-gather.20.cloned.1.call-update) | async-done | bytes 6291472 | tf_op jit(solution)/shard_map/all_gather | solution.py:65
  342.8 64.4 %all-gather.18.cloned.1.call-done = bf16[1024,3072]{1,0:T(8,128)(2,1)} async-done(((bf16[32,3072]{1,0:T(8,128)(2,1)}), bf16[1024,3072]{1,0:T(8,128)(2,1)}) %all-gather.18.cloned.1.call-update) | async-done | bytes 6291472 | tf_op jit(solution)/shard_map/all_gather | solution.py:64
  412.1 65.8 %all-gather.16.cloned.1.call-done = bf16[1024,3072]{1,0:T(8,128)(2,1)} async-done(((bf16[32,3072]{1,0:T(8,128)(2,1)}), bf16[1024,3072]{1,0:T(8,128)(2,1)}) %all-gather.16.cloned.1.call-update) | async-done | bytes 6291472 | tf_op jit(solution)/shard_map/all_gather | solution.py:63
  492.6 18.2 %all_to_all.114 = bf16[2,64,16,128]{3,1,0,2:T(8,128)(2,1)S(1)} all-to-all(bf16[2,64,16,128]{3,1,0,2:T(8,128)(2,1)S(1)} %bitcast.400), channel_id=1, replica_groups=mesh['fsdp'=2,'blk'=4,'uly'=4] {'uly'}, dimensions={2} | all-to-all | bytes 1048576 | tf_op jit(solution)/shard_map/all_to_all | solution.py:262
  519.1 54.2 %while.37 = (s32[]{:T(128)}, bf16[2,2,256,2,128]{4,2,3,1,0:T(8,128)(2,1)}, f32[2,256,2,2,128]{4,1,3,2,0:T(8,128)S(1)}, f32[2,2,256,2,128]{4,2,3,1,0:T(8,128)S(1)...) while((s32[]{:T(128)}, ...), condition=%wide.region_19.20_spmd.clone, body=%wide.region_16.19_spmd.clone.sunk | while | flops 677315072 | bytes 27458016 | solution.py:314
  532.3 10.3 collective-permute-start.2
  559.3 11.0 collective-permute-start.1
  602.6 13.1 all_to_all.116
  648.0 30.7 %all_to_all.117 = bf16[2,256,4,128]{3,2,0,1:T(4,128)(2,1)S(1)} all-to-all(bf16[2,256,4,128]{3,2,0,1:T(4,128)(2,1)S(1)} %bitcast.402), channel_id=1, replica_groups=mesh['fsdp'=2,'blk'=4,'uly'=4] {'uly'}, dimensions={1} | all-to-all | bytes 1048576 | tf_op jit(solution)/shard_map/all_to_all | solution.py:322
  696.4 38.6 %all-reduce.11 = (f32[1024]{0:T(1024)S(1)}, f32[2,128]{1,0:T(2,128)S(1)}, f32[1024]{0:T(1024)S(1)}) all-reduce(f32[1024]{0:T(1024)S(1)} %get-tuple-element.788, f32[2,128]{1,0:T(2,128)S(1)} %pad_add_fusion, f32[1024]{0:T(1024)S(1)} %copy-done.41), channel_id=2, replica_groups=mesh['fsdp'=2,'blk'=4,'uly'=4] {'fsdp','blk','uly'}, use_global_device_ids=true, to_apply=%region_24.25.clone | all-reduce | flops 2304 | bytes 18432
  737.7 21.2 %reduce-scatter.11.cloned.1.call-done = f32[32,1024]{1,0:T(8,128)} async-done(((f32[1024,1024]{1,0:T(8,128)}), f32[32,1024]{1,0:T(8,128)}) %reduce-scatter.11.cloned.1.call-update) | async-done | bytes 131088 | tf_op jit(solution)/shard_map/reduce_scatter | solution.py:364
  758.9 151.4 %reduce-scatter.13.cloned.1.call-done = f32[32,1024]{1,0:T(8,128)} async-done(((f32[1024,1024]{1,0:T(8,128)}), f32[32,1024]{1,0:T(8,128)}) %reduce-scatter.13.cloned.1.call-update) | async-done | bytes 131088 | tf_op jit(solution)/shard_map/reduce_scatter | solution.py:365
  910.3 187.1 %reduce-scatter.15.cloned.1.call-done = f32[64,1024]{1,0:T(8,128)} async-done(((f32[2048,1024]{1,0:T(8,128)}), f32[64,1024]{1,0:T(8,128)}) %reduce-scatter.15.cloned.1.call-update) | async-done | bytes 262160 | tf_op jit(solution)/shard_map/reduce_scatter | solution.py:366
  1097.4 159.1 %reduce-scatter.17.cloned.1.call-done = f32[32,3072]{1,0:T(8,128)} async-done(((f32[1024,3072]{1,0:T(8,128)}), f32[32,3072]{1,0:T(8,128)}) %reduce-scatter.17.cloned.1.call-update) | async-done | bytes 393232 | tf_op jit(solution)/shard_map/reduce_scatter | solution.py:242
  1256.6 160.4 %reduce-scatter.19.cloned.1.call-done = f32[32,3072]{1,0:T(8,128)} async-done(((f32[1024,3072]{1,0:T(8,128)}), f32[32,3072]{1,0:T(8,128)}) %reduce-scatter.19.cloned.1.call-update) | async-done | bytes 393232 | tf_op jit(solution)/shard_map/reduce_scatter | solution.py:243
  1417.0 160.4 %reduce-scatter.21.cloned.1.call-done = f32[96,1024]{1,0:T(8,128)} async-done(((f32[3072,1024]{1,0:T(8,128)}), f32[96,1024]{1,0:T(8,128)}) %reduce-scatter.21.cloned.1.call-update) | async-done | bytes 393232 | tf_op jit(solution)/shard_map/reduce_scatter | solution.py:244
  1577.4 187.4 %reduce-scatter.9.cloned.1.call-done = f32[32,2048]{1,0:T(8,128)} async-done(((f32[1024,2048]{1,0:T(8,128)}), f32[32,2048]{1,0:T(8,128)}) %reduce-scatter.9.cloned.1.call-update) | async-done | bytes 262160 | tf_op jit(solution)/shard_map/reduce_scatter | solution.py:363
  (290 shorter events, 234.5 us)
Async XLA Ops:
  7.2 63.0 %all-gather.10.cloned.1.call-start = ((), (), s32[]{:S(2)}) async-start(), calls=%async_computation.16 | async-start | bytes 2162688 | tf_op jit(solution)/shard_map/all_gather | solution.py:55
  7.9 120.8 %all-gather.8.cloned.1.call-start = ((), (), s32[]{:S(2)}) async-start(), calls=%async_computation.15 | async-start | bytes 2162688 | tf_op jit(solution)/shard_map/all_gather | solution.py:54
  8.7 183.6 %all-gather.12.cloned.1.call-start = ((), (), s32[]{:S(2)}) async-start(), calls=%async_computation.17 | async-start | bytes 4325376 | tf_op jit(solution)/shard_map/all_gather | solution.py:53
  9.4 279.5 %all-gather.14.cloned.1.call-start = ((), (), s32[]{:S(2)}) async-start(), calls=%async_computation.18 | async-start | bytes 4325376 | tf_op jit(solution)/shard_map/all_gather | solution.py:56
  10.0 326.6 %all-gather.20.cloned.1.call-start = ((), (), s32[]{:S(2)}) async-start(), calls=%async_computation.21 | async-start | bytes 6488064 | tf_op jit(solution)/shard_map/all_gather | solution.py:65
  10.6 396.6 %all-gather.18.cloned.1.call-start = ((), (), s32[]{:S(2)}) async-start(), calls=%async_computation.20 | async-start | bytes 6488064 | tf_op jit(solution)/shard_map/all_gather | solution.py:64
  11.1 466.7 %all-gather.16.cloned.1.call-start = ((), (), s32[]{:S(2)}) async-start(), calls=%async_computation.19 | async-start | bytes 6488064 | tf_op jit(solution)/shard_map/all_gather | solution.py:63
  73.1 123.1 %all-to-all-start.1 = ((bf16[2,64,8,128]{3,1,0,2:T(8,128)(2,1)}), bf16[2,64,8,128]{3,1,0,2:T(8,128)(2,1)S(1)}, u32[]{:S(2)}, u32[]{:S(2)}) async-start(bf16[2,64,8,128]{3,1,0,2:T(8,128)(2,1)} %bitcast.379), calls=%async_computation.1 | async-start | bytes 524288 | tf_op jit(solution)/shard_map/all_to_all | solution.py:141
  196.2 14.2 all-to-all-start
  210.5 21.4 %all-to-all-start.2 = ((bf16[2,64,16,128]{3,1,0,2:T(8,128)(2,1)}), bf16[2,64,16,128]{3,1,0,2:T(8,128)(2,1)S(1)}, u32[]{:S(2)}, u32[]{:S(2)}) async-start(bf16[2,64,16,128]{3,1,0,2:T(8,128)(2,1)} %fusion.95), calls=%async_computation.2 | async-start | bytes 1048576 | tf_op jit(solution)/shard_map/all_to_all | solution.py:135
  241.0 18.8 %collective-permute-start = (bf16[2,2,256,2,128]{4,2,3,1,0:T(8,128)(2,1)}, bf16[2,2,256,2,128]{4,2,3,1,0:T(8,128)(2,1)S(1)}, u32[]{:S(2)}, u32[]{:S(2)}) collective-permute-start(bf16[2,2,256,2,128]{4,2,3,1,0:T(8,128)(2,1)} %get-tuple-element.1044), channel_id=1, source_target_pairs={{0,4},{4,8},{8,12},{1,5},{5,9},{9,13},{2,6},{6,10},{10,14},{3,7},{... | collective-permute-start | bytes 1572872 | tf_op jit(solution)/shard_map/while/body/eval_jaxpr/ppermute | solution.py:18
  260.6 10.7 collective-permute-start
  273.8 14.2 all-to-all-start.3
  277.5 481.4 %reduce-scatter.11.cloned.1.call-start = ((), (), s32[]{:S(2)}) async-start(), calls=%async_computation.23 | async-start | bytes 4325376 | tf_op jit(solution)/shard_map/reduce_scatter | solution.py:364
  532.3 14.6 collective-permute-start.2
  550.9 19.4 %collective-permute-start.2 = (bf16[2,2,256,2,128]{4,2,3,1,0:T(8,128)(2,1)}, bf16[2,2,256,2,128]{4,2,3,1,0:T(8,128)(2,1)}, u32[]{:S(2)}, u32[]{:S(2)}) collective-permute-start(bf16[2,2,256,2,128]{4,2,3,1,0:T(8,128)(2,1)} %convert_element_type.292), channel_id=1, source_target_pairs={{0,4},{4,8},{8,12},{12,0},{1,5},{5,9},{9,13},{13,1},{2,6},{6,10},{... | collective-permute-start | bytes 1572872 | tf_op jit(solution)/shard_map/while/body/eval_jaxpr/ppermute | solution.py:24
  559.3 12.7 collective-permute-start.1
  574.2 13.5 collective-permute-start.3
  602.5 307.8 %reduce-scatter.13.cloned.1.call-start = ((), (), s32[]{:S(2)}) async-start(), calls=%async_computation.24 | async-start | bytes 4325376 | tf_op jit(solution)/shard_map/reduce_scatter | solution.py:365
  618.9 478.5 %reduce-scatter.15.cloned.1.call-start = ((), (), s32[]{:S(2)}) async-start(), calls=%async_computation.25 | async-start | bytes 8650752 | tf_op jit(solution)/shard_map/reduce_scatter | solution.py:366
  624.6 631.9 %reduce-scatter.17.cloned.1.call-start = ((), (), s32[]{:S(2)}) async-start(), calls=%async_computation.26 | async-start | bytes 12976128 | tf_op jit(solution)/shard_map/reduce_scatter | solution.py:242
  632.2 784.8 %reduce-scatter.19.cloned.1.call-start = ((), (), s32[]{:S(2)}) async-start(), calls=%async_computation.27 | async-start | bytes 12976128 | tf_op jit(solution)/shard_map/reduce_scatter | solution.py:243
  639.7 937.7 %reduce-scatter.21.cloned.1.call-start = ((), (), s32[]{:S(2)}) async-start(), calls=%async_computation.28 | async-start | bytes 12976128 | tf_op jit(solution)/shard_map/reduce_scatter | solution.py:244
  647.3 1117.5 %reduce-scatter.9.cloned.1.call-start = ((), (), s32[]{:S(2)}) async-start(), calls=%async_computation.22 | async-start | bytes 8650752 | tf_op jit(solution)/shard_map/reduce_scatter | solution.py:363
  (52 other events, 1098.9 us)
Sparse Core Ops, SparseCore 0:
  10.9 59.1 all-gather.9
  73.1 55.5 all-gather.7
  131.7 60.4 all-gather.11
  195.1 62.0 all-gather.13
  259.9 76.6 all-gather.19
  339.3 67.7 all-gather.17
  410.0 67.7 all-gather.15
  602.6 156.2 reduce-scatter.10
  761.8 148.5 reduce-scatter.12
  913.0 184.3 reduce-scatter.14
  1104.0 152.4 reduce-scatter.16
  1263.0 153.8 reduce-scatter.18
  1423.5 153.7 reduce-scatter.20
  1580.1 184.6 reduce-scatter.8
where the time goes:
time: 1780 us; the launch traced here: 1770 us
  waiting for transfers between devices  1380 us (78%)
  blocking collectives  152 us (9%)
  starting transfers between devices  88.4 us (5%)
  matrix products  82.4 us (5%)
  local copies, waits for them, and re-layouts  30.9 us (2%)
  other arithmetic  22.1 us (1%)
    reduce_scatter x1, waiting for transfers between devices, body(): lax.psum_scatter(query_grad, ('fsdp', 'blk', 'uly'), scatter_dimension=0,...  187 us
    reduce_scatter x1, waiting for transfers between devices, body(): lax.psum_scatter(out_grad, ('fsdp', 'blk', 'uly'), scatter_dimension=0, t...  187 us
    reduce_scatter x1, waiting for transfers between devices, body(): lax.psum_scatter(down_grad, ('fsdp', 'blk', 'uly'), scatter_dimension=0,...  160 us
    reduce_scatter x1, waiting for transfers between devices, body(): lax.psum_scatter(up_grad, ('fsdp', 'blk', 'uly'), scatter_dimension=0, ti...  160 us
    reduce_scatter x1, waiting for transfers between devices, body(): lax.psum_scatter(gate_grad, ('fsdp', 'blk', 'uly'), scatter_dimension=0,...  159 us
    reduce_scatter x1, waiting for transfers between devices, body(): lax.psum_scatter(value_grad, ('fsdp', 'blk', 'uly'), scatter_dimension=0,...  151 us
    unnamed x2, blocking collectives  80.7 us
    all_gather x1, waiting for transfers between devices, fetch_feedforward(): lax.all_gather(gate_weight, ('fsdp', 'blk', 'uly'), axis=0, tiled=True)  65.8 us
  transfers between devices with their start and end apart: 28, of which 23 were waited for; matrix products, arithmetic and copies ran while one was open for 5% of the time, Pallas kernels for 0%

commit v1 on v0

--- a/solution.py
+++ b/solution.py
@@ -1,8 +1,11 @@
+import functools
 import math
 
 import jax
 import jax.numpy as jnp
 from jax import lax
+from jax.experimental import pallas as pl
+from jax.experimental.pallas import tpu as pltpu
 from jax.sharding import PartitionSpec as P
 
 DOCS = 4
@@ -381,9 +384,713 @@
     )
 
 
+MESH = pl.DeviceIdType.MESH
+ANY = pl.BlockSpec(memory_space=pl.ANY)
+VMEM = pl.BlockSpec(memory_space=pltpu.VMEM)
+PLANE = [(dx, dy, dc) for dx in (0, 1) for dy in (0, 1) for dc in (0, 1)]
+FAR = [(1, 1, 0), (1, 0, 0), (0, 1, 0)]
+TURNS = (1, 2, 3)
+SEM = pltpu.SemaphoreType.DMA
+
+
+class Place:
+    def __init__(self):
+        self.x = lax.axis_index("fsdp")
+        self.block = lax.axis_index("blk")
+        self.z = lax.axis_index("uly")
+        self.y, self.c = (self.block // 2, self.block % 2)
+        self.head = 4 * self.x + self.block
+        self.here = (self.x, self.block, self.z)
+
+    def coords(self, dx, dy, dc):
+        return ((self.x + dx) % 2, (self.y + dy) % 2, (self.c + dc) % 2)
+
+    def peer(self, dx, dy, dc):
+        x, y, c = self.coords(dx, dy, dc)
+        return (x, 2 * y + c, self.z)
+
+    def index(self, dx, dy, dc):
+        x, y, c = self.coords(dx, dy, dc)
+        return 4 * x + 2 * y + c
+
+    def shard(self, ref, dx=0, dy=0, dc=0):
+        x, y, c = self.coords(dx, dy, dc)
+        return ref.at[2 * y + c, :, x]
+
+    def behind(self, turn):
+        return (self.z + 4 - turn) % 4
+
+    def ahead(self, turn):
+        return (self.z + turn) % 4
+
+    def line(self, turn):
+        return (self.x, self.block, self.ahead(turn))
+
+
+def remote(src, dst, send_sem, recv_sem, device):
+    return pltpu.make_async_remote_copy(
+        src_ref=src,
+        dst_ref=dst,
+        send_sem=send_sem,
+        recv_sem=recv_sem,
+        device_id=device,
+        device_id_type=MESH,
+    )
+
+
+def arrived(ref, sem):
+    pltpu.make_async_copy(ref, ref, sem).wait()
+
+
+def meet(peers):
+    barrier = pltpu.get_barrier_semaphore()
+    for peer in peers:
+        pl.semaphore_signal(barrier, inc=1, device_id=peer, device_id_type=MESH)
+    pl.semaphore_wait(barrier, len(peers))
+
+
+class Sends:
+    def __init__(self):
+        self.pending = []
+
+    def go(self, *args):
+        copy = remote(*args)
+        copy.start()
+        self.pending.append(copy)
+
+    def drain(self):
+        for copy in self.pending:
+            copy.wait_send()
+
+
+def spread_start(me, sends, src, full, send_sems, recv_sems):
+    for i, d in enumerate(FAR + [(0, 0, 1)]):
+        sends.go(src, me.shard(full), send_sems.at[i], recv_sems.at[i], me.peer(*d))
+
+
+def spread_forward(me, sends, full, send_sems, recv_sems):
+    for i in (1, 2, 0):
+        part = me.shard(full, *FAR[i])
+        arrived(part, recv_sems.at[i])
+        sends.go(part, part, send_sems.at[4 + i], recv_sems.at[4 + i], me.peer(0, 0, 1))
+
+
+def spread_finish(me, full, recv_sems):
+    for i, (dx, dy, _) in enumerate([(0, 0, 0)] + FAR):
+        arrived(me.shard(full, dx, dy, 1), recv_sems.at[3 + i])
+
+
+def gather_kernel(
+    x_ref, cot_ref, seg_ref, q_ref, k_ref, v_ref, g_ref, u_ref, gain_ref,
+    xf_ref, cf_ref, segf_ref, w_ref, gu_ref, gains_ref,
+    ps, pr, as_, ar, ws, wr, zs, zr, us, ur, gs, gr, ls,
+):
+    me = Place()
+    x, z, p = (me.x, me.z, me.head)
+    across = [((x + 1) % 2, me.block, me.ahead(turn)) for turn in TURNS]
+    meet([me.peer(*d) for d in PLANE[1:]] + [me.line(turn) for turn in TURNS] + across)
+    sends = Sends()
+    half = x_ref.shape[1] // 2
+    own_gain = pltpu.make_async_copy(gain_ref, gains_ref.at[p, z], ls.at[0])
+    own_gain.start()
+    own_seg = pltpu.make_async_copy(seg_ref, segf_ref.at[x], ls.at[1])
+    own_seg.start()
+    sends.go(seg_ref, segf_ref.at[x], ls.at[2], ls.at[3], me.peer(1, 0, 0))
+    for turn in TURNS:
+        sends.go(gain_ref, gains_ref.at[p, z], gs.at[turn], gr.at[turn], me.line(turn))
+
+    def permute(src_ref, full_ref, o, wait=False):
+        for j in (0, 1):
+            for to in (0, 1):
+                src = src_ref.at[j, pl.ds(half * to, half)]
+                dst = full_ref.at[me.block, z, to]
+                target = (to, me.block, 2 * x + j)
+                mine = jnp.logical_and(x == to, z == 2 * x + j)
+                copy = remote(src, dst, ps.at[o + 2 * j + to], pr.at[o + z], target)
+
+                @pl.when(jnp.logical_not(mine))
+                def _():
+                    if wait:
+                        copy.wait_send()
+                    else:
+                        copy.start()
+
+                if not wait:
+
+                    @pl.when(mine)
+                    def _():
+                        pltpu.make_async_copy(src, dst, pr.at[o + z]).start()
+
+    def permuted(full_ref, o):
+        for k in range(4):
+            arrived(full_ref.at[me.block, k, x], pr.at[o + k])
+
+    permute(x_ref, xf_ref, 0)
+    wide, narrow = (q_ref.shape[1] // 8, k_ref.shape[1] // 8)
+    cuts = ((q_ref, wide, 0), (k_ref, narrow, wide), (v_ref, narrow, wide + narrow))
+    for i, d in enumerate(PLANE):
+        t = me.index(*d)
+        for n, (ref, width, off) in enumerate(cuts):
+            src = ref.at[:, pl.ds(pl.multiple_of(t * width, 128), width)]
+            dst = w_ref.at[p, z, :, pl.ds(off, width)]
+            if i == 0:
+                pltpu.make_async_copy(src, dst, wr.at[n]).start()
+            else:
+                sends.go(src, dst, ws.at[3 * i + n], wr.at[3 * i + n], me.peer(*d))
+    permute(cot_ref, cf_ref, 4)
+    permuted(xf_ref, 0)
+    spread_start(me, sends, me.shard(xf_ref), xf_ref, as_, ar)
+    for i, d in enumerate(PLANE):
+        t = me.index(*d)
+        for n, (ref, width, off) in enumerate(cuts):
+            arrived(w_ref.at[t, z, :, pl.ds(off, width)], wr.at[3 * i + n])
+        for turn in TURNS:
+            s = 3 * i + turn - 1
+            sends.go(w_ref.at[t, z], w_ref.at[t, z], zs.at[s], zr.at[s], me.line(turn))
+    width = g_ref.shape[1] // 8
+    for i, d in enumerate(PLANE):
+        t = me.index(*d)
+        for n, ref in enumerate((g_ref, u_ref)):
+            src = ref.at[:, pl.ds(pl.multiple_of(t * width, 128), width)]
+            dst = gu_ref.at[p, :, pl.ds(n * width, width)]
+            if i == 0:
+                pltpu.make_async_copy(src, dst, ur.at[n]).start()
+            else:
+                sends.go(src, dst, us.at[2 * i + n], ur.at[2 * i + n], me.peer(*d))
+    permuted(cf_ref, 4)
+    spread_start(me, sends, me.shard(cf_ref), cf_ref, as_.at[pl.ds(7, 7)], ar.at[pl.ds(7, 7)])
+    own_gain.wait()
+    own_seg.wait()
+    arrived(segf_ref.at[(x + 1) % 2], ls.at[3])
+    for turn in TURNS:
+        arrived(gains_ref.at[p, me.behind(turn)], gr.at[turn])
+    for i, d in enumerate(PLANE[1:]):
+        sends.go(gains_ref.at[p], gains_ref.at[p], gs.at[4 + i], gr.at[4 + i], me.peer(*d))
+    spread_forward(me, sends, xf_ref, as_, ar)
+    spread_finish(me, xf_ref, ar)
+    for i, d in enumerate(PLANE[1:]):
+        arrived(gains_ref.at[me.index(*d)], gr.at[4 + i])
+    for i, d in enumerate(PLANE):
+        for turn in TURNS:
+            arrived(w_ref.at[me.index(*d), me.behind(turn)], zr.at[3 * i + turn - 1])
+    for i, d in enumerate(PLANE):
+        for n in (0, 1):
+            arrived(gu_ref.at[me.index(*d), :, pl.ds(n * width, width)], ur.at[2 * i + n])
+    spread_forward(me, sends, cf_ref, as_.at[pl.ds(7, 7)], ar.at[pl.ds(7, 7)])
+    spread_finish(me, cf_ref, ar.at[pl.ds(7, 7)])
+    permute(x_ref, xf_ref, 0, wait=True)
+    permute(cot_ref, cf_ref, 4, wait=True)
+    sends.drain()
+
+
+def full_shape(tokens, width):
+    return (4, 4, 2, tokens // 32, width)
+
+
+def gather_all(x, cot, seg, q, k, v, g, u, gain):
+    tokens, width = (16 * x.shape[1], x.shape[2])
+    rows = q.shape[0]
+    cols = (q.shape[1] + 2 * k.shape[1]) // 8
+    full = jax.ShapeDtypeStruct(full_shape(tokens, width), jnp.bfloat16)
+    return pl.pallas_call(
+        gather_kernel,
+        name="gather_all",
+        out_shape=(
+            full,
+            full,
+            jax.ShapeDtypeStruct((2,) + seg.shape, seg.dtype),
+            jax.ShapeDtypeStruct((8, 4, rows, cols), jnp.bfloat16),
+            jax.ShapeDtypeStruct((8, rows, g.shape[1] // 4), jnp.bfloat16),
+            jax.ShapeDtypeStruct((8, 4, 8, 128), jnp.float32),
+        ),
+        in_specs=[ANY] * 9,
+        out_specs=(ANY,) * 6,
+        scratch_shapes=[SEM((8,)), SEM((8,)), SEM((14,)), SEM((14,))]
+        + [SEM((24,))] * 4
+        + [SEM((16,))] * 2
+        + [SEM((11,))] * 2
+        + [SEM((4,))],
+        compiler_params=pltpu.CompilerParams(collective_id=0, has_side_effects=True),
+    )(x, cot, seg, q, k, v, g, u, gain)
+
+
+def half_start(me, sends, part, kept, sibling, keep_sems, send_sems, recv_sems):
+    for i, (dx, dy, _) in enumerate(FAR + [(0, 0, 0)]):
+        src = me.shard(part, dx, dy, 1)
+        sends.go(src, sibling.at[i], send_sems.at[i], recv_sems.at[i], me.peer(0, 0, 1))
+        pltpu.make_async_copy(me.shard(part, dx, dy, 0), kept.at[i], keep_sems.at[i]).start()
+
+
+def half_send(me, sends, kept, sibling, out, came, keep_sems, send_sems, recv_sems):
+    for i, d in enumerate(FAR):
+        arrived(kept.at[i], keep_sems.at[i])
+        arrived(sibling.at[i], recv_sems.at[i])
+        out[i] = (
+            kept[i].astype(jnp.float32) + sibling[i].astype(jnp.float32)
+        ).astype(jnp.bfloat16)
+        sends.go(out.at[i], came.at[i], send_sems.at[4 + i], recv_sems.at[4 + i], me.peer(*d))
+
+
+def half_sum(kept, sibling, came, keep_sems, recv_sems):
+    arrived(kept.at[3], keep_sems.at[3])
+    arrived(sibling.at[3], recv_sems.at[3])
+    total = kept[3].astype(jnp.float32) + sibling[3].astype(jnp.float32)
+    for i in (1, 2, 0):
+        arrived(came.at[i], recv_sems.at[4 + i])
+        total = total + came[i].astype(jnp.float32)
+    return total
+
+
+def quarter_scratch(tokens, width):
+    piece = (4, tokens // 32, width)
+    return [
+        pltpu.VMEM((4,) + piece, jnp.bfloat16),
+        pltpu.VMEM((4,) + piece, jnp.bfloat16),
+        pltpu.VMEM((3,) + piece, jnp.bfloat16),
+        pltpu.VMEM((3,) + piece, jnp.bfloat16),
+        SEM((4,)),
+        SEM((7,)),
+        SEM((7,)),
+    ]
+
+
+def near(me):
+    return [me.peer(*d) for d in FAR + [(0, 0, 1)]]
+
+
+def middle_kernel(
+    part_ref, xf_ref, gain_ref, mid_ref, nf_ref,
+    kept, sibling, out, came, ks, ss, rs, xs_ref, n_ref, as_, ar, ls,
+):
+    me = Place()
+    meet(near(me))
+    sends = Sends()
+    half_start(me, sends, part_ref, kept, sibling, ks, ss, rs)
+    own_x = pltpu.make_async_copy(me.shard(xf_ref), xs_ref, ls.at[0])
+    own_x.start()
+    half_send(me, sends, kept, sibling, out, came, ks, ss, rs)
+    own_x.wait()
+    middle = xs_ref[...].astype(jnp.float32) + half_sum(kept, sibling, came, ks, rs)
+    mid_ref[...] = middle
+    scale = lax.rsqrt(jnp.mean(middle * middle, axis=-1, keepdims=True) + EPSILON)
+    n_ref[...] = (middle * scale * gain_ref[...]).astype(jnp.bfloat16)
+    own_n = pltpu.make_async_copy(n_ref, me.shard(nf_ref), ls.at[1])
+    own_n.start()
+    spread_start(me, sends, n_ref, nf_ref, as_, ar)
+    spread_forward(me, sends, nf_ref, as_, ar)
+    spread_finish(me, nf_ref, ar)
+    own_n.wait()
+    sends.drain()
+
+
+def middle_step(part, xf, gain):
+    tokens, width = (part.shape[0], part.shape[1])
+    piece = (4, tokens // 32, width)
+    return pl.pallas_call(
+        middle_kernel,
+        name="middle_step",
+        out_shape=(
+            jax.ShapeDtypeStruct(piece, jnp.float32),
+            jax.ShapeDtypeStruct(full_shape(tokens, width), jnp.bfloat16),
+        ),
+        in_specs=[ANY, ANY, VMEM],
+        out_specs=(VMEM, ANY),
+        scratch_shapes=quarter_scratch(tokens, width)
+        + [pltpu.VMEM(piece, jnp.bfloat16)] * 2
+        + [SEM((7,)), SEM((7,)), SEM((2,))],
+        compiler_params=pltpu.CompilerParams(collective_id=1, has_side_effects=True),
+    )(part.reshape(full_shape(tokens, width)), xf, gain)
+
+
+def norm_back(grad, vector, gain, scale):
+    weighted = grad * gain
+    inner = jnp.mean(weighted * vector, axis=-1, keepdims=True)
+    return scale * weighted - vector * (scale * scale * scale * inner)
+
+
+def turn_kernel(
+    part_ref, down_ref, cf_ref, mid_ref, gain_ref, gmid_ref, gf_ref, out_ref, gg_ref,
+    kept, sibling, out, came, ks, ss, rs, kept2, sibling2, out2, came2, ks2, ss2, rs2,
+    cs_ref, n_ref, as_, ar, ls,
+):
+    me = Place()
+    meet(near(me))
+    sends = Sends()
+    half_start(me, sends, part_ref, kept, sibling, ks, ss, rs)
+    own_c = pltpu.make_async_copy(me.shard(cf_ref), cs_ref, ls.at[0])
+    own_c.start()
+    half_start(me, sends, down_ref, kept2, sibling2, ks2, ss2, rs2)
+    half_send(me, sends, kept, sibling, out, came, ks, ss, rs)
+    half_send(me, sends, kept2, sibling2, out2, came2, ks2, ss2, rs2)
+    own_c.wait()
+    grad = half_sum(kept, sibling, came, ks, rs)
+    middle = mid_ref[...]
+    scale = lax.rsqrt(jnp.mean(middle * middle, axis=-1, keepdims=True) + EPSILON)
+    total = cs_ref[...].astype(jnp.float32) + norm_back(grad, middle, gain_ref[...], scale)
+    gmid_ref[...] = total
+    n_ref[...] = total.astype(jnp.bfloat16)
+    own_n = pltpu.make_async_copy(n_ref, me.shard(gf_ref), ls.at[1])
+    own_n.start()
+    spread_start(me, sends, n_ref, gf_ref, as_, ar)
+    share = grad * middle * scale
+    gg_ref[...] = jnp.sum(jnp.sum(share, axis=0), axis=0, keepdims=True)
+    out_ref[...] = (middle + half_sum(kept2, sibling2, came2, ks2, rs2)).astype(jnp.bfloat16)
+    spread_forward(me, sends, gf_ref, as_, ar)
+    spread_finish(me, gf_ref, ar)
+    own_n.wait()
+    sends.drain()
+
+
+def turn_step(part, down, cf, middle, gain):
+    tokens, width = (part.shape[0], part.shape[1])
+    piece = (4, tokens // 32, width)
+    full = full_shape(tokens, width)
+    return pl.pallas_call(
+        turn_kernel,
+        name="turn_step",
+        out_shape=(
+            jax.ShapeDtypeStruct(piece, jnp.float32),
+            jax.ShapeDtypeStruct(full, jnp.bfloat16),
+            jax.ShapeDtypeStruct(piece, jnp.bfloat16),
+            jax.ShapeDtypeStruct((1, width), jnp.float32),
+        ),
+        in_specs=[ANY, ANY, ANY, VMEM, VMEM],
+        out_specs=(VMEM, ANY, VMEM, VMEM),
+        scratch_shapes=quarter_scratch(tokens, width) * 2
+        + [pltpu.VMEM(piece, jnp.bfloat16)] * 2
+        + [SEM((7,)), SEM((7,)), SEM((2,))],
+        compiler_params=pltpu.CompilerParams(collective_id=2, has_side_effects=True),
+    )(part.reshape(full), down.reshape(full), cf, middle, gain)
+
+
+def last_kernel(
+    part_ref, xf_ref, gmid_ref, out_ref, gain_ref, small_ref, dw_ref, dgu_ref,
+    y_ref, gx_ref, q_ref, k_ref, v_ref, g_ref, u_ref, sums_ref,
+    kept, sibling, out, came, ks, ss, rs, xs_ref, gi_ref, ps, pr, ls,
+    wown, wcame, wsum, zs, zr, ws, wr, us, ur, pack, packs, lines, gs, gr,
+):
+    me = Place()
+    x, z, p = (me.x, me.z, me.head)
+    across = [((x + 1) % 2, me.block, me.ahead(turn)) for turn in TURNS]
+    meet([me.peer(*d) for d in PLANE[1:]] + [me.line(turn) for turn in TURNS] + across)
+    sends = Sends()
+    half_start(me, sends, part_ref, kept, sibling, ks, ss, rs)
+    for turn in TURNS:
+        sends.go(
+            dw_ref.at[:, me.ahead(turn)], wcame.at[turn - 1],
+            zs.at[turn - 1], zr.at[turn - 1], me.line(turn),
+        )
+    own_w = pltpu.make_async_copy(dw_ref.at[:, z], wown, ls.at[2])
+    own_w.start()
+    own_x = pltpu.make_async_copy(me.shard(xf_ref), xs_ref, ls.at[0])
+    own_x.start()
+    half_send(me, sends, kept, sibling, out, came, ks, ss, rs)
+    half = y_ref.shape[1] // 2
+
+    def permute(src_ref, dst_ref, o, wait=False):
+        for k in range(4):
+            dst = dst_ref.at[z % 2, pl.ds(half * x, half)]
+            src = src_ref.at[k]
+            mine = jnp.logical_and(x == z // 2, z == k)
+            copy = remote(src, dst, ps.at[o + k], pr.at[o + 2 * (z % 2) + x], (z // 2, me.block, k))
+
+            @pl.when(jnp.logical_not(mine))
+            def _():
+                if wait:
+                    copy.wait_send()
+                else:
+                    copy.start()
+
+            if not wait:
+
+                @pl.when(mine)
+                def _():
+                    pltpu.make_async_copy(src, dst, pr.at[o + 2 * (z % 2) + x]).start()
+
+    def permuted(dst_ref, o):
+        for j in (0, 1):
+            for to in (0, 1):
+                arrived(dst_ref.at[j, pl.ds(half * to, half)], pr.at[o + 2 * j + to])
+
+    permute(out_ref, y_ref, 0)
+    width = g_ref.shape[1] // 8
+    for i, d in enumerate(PLANE):
+        t = me.index(*d)
+        for n, ref in enumerate((g_ref, u_ref)):
+            src = dgu_ref.at[t, :, pl.ds(n * width, width)]
+            dst = ref.at[:, pl.ds(pl.multiple_of(p * width, 128), width)]
+            if i == 0:
+                pltpu.make_async_copy(src, dst, ur.at[n]).start()
+            else:
+                sends.go(src, dst, us.at[2 * i + n], ur.at[2 * i + n], me.peer(*d))
+    own_x.wait()
+    grad = half_sum(kept, sibling, came, ks, rs)
+    rows = xs_ref[...].astype(jnp.float32)
+    scale = lax.rsqrt(jnp.mean(rows * rows, axis=-1, keepdims=True) + EPSILON)
+    gi_ref[...] = (gmid_ref[...] + norm_back(grad, rows, gain_ref[...], scale)).astype(jnp.bfloat16)
+    permute(gi_ref, gx_ref, 4)
+    share = jnp.sum(jnp.sum(grad * rows * scale, axis=0), axis=0, keepdims=True)
+    for i in range(8):
+        pack[pl.ds(i, 1)] = share[:, 128 * i : 128 * i + 128]
+    pack[pl.ds(8, 16)] = small_ref[...]
+    for i, d in enumerate(PLANE[1:]):
+        sends.go(pack, packs.at[i], gs.at[i], gr.at[i], me.peer(*d))
+    own_w.wait()
+    for turn in TURNS:
+        arrived(wcame.at[turn - 1], zr.at[turn - 1])
+    wsum[...] = (
+        wown[...].astype(jnp.float32)
+        + wcame[0].astype(jnp.float32)
+        + wcame[1].astype(jnp.float32)
+        + wcame[2].astype(jnp.float32)
+    ).astype(jnp.bfloat16)
+    wide, narrow = (q_ref.shape[1] // 8, k_ref.shape[1] // 8)
+    cuts = ((q_ref, wide, 0), (k_ref, narrow, wide), (v_ref, narrow, wide + narrow))
+    for i, d in enumerate(PLANE):
+        t = me.index(*d)
+        for n, (ref, cols, off) in enumerate(cuts):
+            src = wsum.at[t, :, pl.ds(off, cols)]
+            dst = ref.at[:, pl.ds(pl.multiple_of(p * cols, 128), cols)]
+            if i == 0:
+                pltpu.make_async_copy(src, dst, wr.at[n]).start()
+            else:
+                sends.go(src, dst, ws.at[3 * i + n], wr.at[3 * i + n], me.peer(*d))
+    total = pack[...]
+    for i in range(7):
+        arrived(packs.at[i], gr.at[i])
+        total = total + packs[i]
+    sums_ref[...] = total
+    packs[7] = total
+    for turn in TURNS:
+        sends.go(packs.at[7], lines.at[turn - 1], gs.at[6 + turn], gr.at[6 + turn], me.line(turn))
+    for turn in TURNS:
+        arrived(lines.at[turn - 1], gr.at[6 + turn])
+    sums_ref[...] = ((sums_ref[...] + lines[0]) + lines[1]) + lines[2]
+    for i, d in enumerate(PLANE):
+        t = me.index(*d)
+        for n, ref in enumerate((g_ref, u_ref)):
+            arrived(ref.at[:, pl.ds(pl.multiple_of(t * width, 128), width)], ur.at[2 * i + n])
+        for n, (ref, cols, off) in enumerate(cuts):
+            arrived(ref.at[:, pl.ds(pl.multiple_of(t * cols, 128), cols)], wr.at[3 * i + n])
+    permuted(y_ref, 0)
+    permuted(gx_ref, 4)
+    permute(out_ref, y_ref, 0, wait=True)
+    permute(gi_ref, gx_ref, 4, wait=True)
+    sends.drain()
+
+
+def last_step(part, xf, gmid, out, gain, small, dw, dgu, per_device):
+    tokens, width = (part.shape[0], part.shape[1])
+    piece = (4, tokens // 32, width)
+    rows, cols = (dw.shape[2], dw.shape[3])
+    token_shape, q_cols, k_cols, f_cols = per_device
+    back = jax.ShapeDtypeStruct(token_shape, jnp.bfloat16)
+    weights = [jax.ShapeDtypeStruct((rows, n), jnp.bfloat16) for n in (q_cols, k_cols, k_cols, f_cols, f_cols)]
+    return pl.pallas_call(
+        last_kernel,
+        name="last_step",
+        out_shape=(back, back, *weights, jax.ShapeDtypeStruct((24, 128), jnp.float32)),
+        in_specs=[ANY, ANY, VMEM, ANY, VMEM, VMEM, ANY, ANY],
+        out_specs=(ANY,) * 7 + (VMEM,),
+        scratch_shapes=quarter_scratch(tokens, width)
+        + [pltpu.VMEM(piece, jnp.bfloat16)] * 2
+        + [SEM((8,)), SEM((8,)), SEM((3,))]
+        + [
+            pltpu.VMEM((8, rows, cols), jnp.bfloat16),
+            pltpu.VMEM((3, 8, rows, cols), jnp.bfloat16),
+            pltpu.VMEM((8, rows, cols), jnp.bfloat16),
+            SEM((3,)), SEM((3,)), SEM((24,)), SEM((24,)), SEM((16,)), SEM((16,)),
+            pltpu.VMEM((24, 128), jnp.float32),
+            pltpu.VMEM((8, 24, 128), jnp.float32),
+            pltpu.VMEM((3, 24, 128), jnp.float32),
+            SEM((10,)), SEM((10,)),
+        ],
+        compiler_params=pltpu.CompilerParams(collective_id=3, has_side_effects=True),
+    )(part.reshape(full_shape(tokens, width)), xf, gmid, out, gain, small, dw, dgu)
+
+
+def rope_tables(segs, head_dim):
+    count = segs.shape[0]
+    doc_ids = jnp.arange(DOCS, dtype=jnp.int32)
+    starts = jnp.sum((segs[None, :] < doc_ids[:, None]).astype(jnp.int32), axis=1)
+    inverse = jnp.exp(
+        jnp.arange(head_dim // 2, dtype=jnp.float32) * (-2.0 * math.log(THETA) / head_dim)
+    )
+    inverse = jnp.concatenate([inverse, inverse])
+    low = jnp.arange(32, dtype=jnp.float32)[:, None] * inverse
+    high = jnp.arange(count // 32, dtype=jnp.float32)[:, None] * (32.0 * inverse)
+    first = starts.astype(jnp.float32)[:, None] * inverse
+    cl, sl, ch, sh, cf, sf = (
+        f(v) for v in (low, high, first) for f in (jnp.cos, jnp.sin)
+    )
+    cos_at = (ch[:, None] * cl - sh[:, None] * sl).reshape(count, head_dim)
+    sin_at = (sh[:, None] * cl + ch[:, None] * sl).reshape(count, head_dim)
+    chosen_cos = jnp.broadcast_to(cf[0], (count, head_dim))
+    chosen_sin = jnp.broadcast_to(sf[0], (count, head_dim))
+    for doc in range(1, DOCS):
+        here = (segs == doc)[:, None]
+        chosen_cos = jnp.where(here, cf[doc], chosen_cos)
+        chosen_sin = jnp.where(here, sf[doc], chosen_sin)
+    return (
+        cos_at * chosen_cos + sin_at * chosen_sin,
+        sin_at * chosen_cos - cos_at * chosen_sin,
+    )
+
+
+def dot(a, b, kind=jnp.float32):
+    return jnp.dot(a, b, preferred_element_type=jnp.float32).astype(kind)
+
+
+def dot_left(a, b, kind=jnp.float32):
+    return lax.dot_general(
+        a, b, (((0,), (0,)), ((), ())), preferred_element_type=jnp.float32
+    ).astype(kind)
+
+
+def dot_right(a, b, kind=jnp.float32):
+    return lax.dot_general(
+        a, b, (((1,), (1,)), ((), ())), preferred_element_type=jnp.float32
+    ).astype(kind)
+
+
+def plane_body(
+    inputs, segments, attn_gain, head_gains, query_weight, key_matrix, value_matrix, out_weight,
+    ffn_gain, gate_weight, up_weight, down_weight, cotangent,
+):
+    low = jnp.bfloat16
+    width = inputs.shape[2]
+    head_dim = head_gains.shape[1]
+    z = lax.axis_index("uly")
+    head = 4 * lax.axis_index("fsdp") + lax.axis_index("blk")
+    out_full = lax.all_gather(out_weight, "uly", axis=0, tiled=True)
+    down_full = lax.all_gather(down_weight, "uly", axis=0, tiled=True)
+    piece = attn_gain.shape[0]
+    gains_own = jnp.zeros((8, 128), jnp.float32)
+    gains_own = gains_own.at[0, :piece].set(attn_gain.astype(jnp.float32))
+    gains_own = gains_own.at[1, :piece].set(ffn_gain.astype(jnp.float32))
+    xf, cf, segf, w_qkv, gu_part, gains = gather_all(
+        inputs, cotangent, segments, query_weight, key_matrix, value_matrix, gate_weight,
+        up_weight, gains_own,
+    )
+    gate_up = lax.all_gather(gu_part, "uly", axis=1, tiled=False)
+    gate_up = gate_up.reshape(width, gu_part.shape[2])
+    w_qkv = w_qkv.reshape(width, w_qkv.shape[3])
+    gain_one = gains[:, :, 0, :piece].reshape(1, width)
+    gain_two = gains[:, :, 1, :piece].reshape(1, width)
+    tokens = xf.shape[0] * xf.shape[1] * xf.shape[2] * xf.shape[3]
+    x_all = xf.reshape(tokens, width)
+    cot_all = cf.reshape(tokens, width)
+    segs = lax.dynamic_index_in_dim(segf.reshape(-1, tokens), z, 0, keepdims=False)
+    normed = rms_norm(x_all.astype(jnp.float32), gain_one).astype(low)
+    pre = dot(normed, w_qkv).reshape(tokens, -1, head_dim)
+    groups = pre.shape[1] - 2
+    cosine, sine = rope_tables(segs, head_dim)
+    head_float = head_gains.astype(jnp.float32)
+
+    def prepare_local(query_arg, key_arg, gains_arg):
+        return prepare(query_arg[None], key_arg[None], gains_arg, cosine[None], sine[None])
+
+    (query_rot, key_rot), prep_pull = jax.vjp(
+        prepare_local, pre[:, :groups], pre[:, groups : groups + 1], head_float
+    )
+    query = query_rot[0].astype(low)
+    key = key_rot[0, :, 0].astype(low)
+    value = pre[:, groups + 1].astype(low)
+    bound = math.sqrt(head_dim) * jnp.max(jnp.abs(head_float[0])) * jnp.max(jnp.abs(head_float[1]))
+    scale = head_dim ** (-0.5)
+    index = jnp.arange(tokens, dtype=jnp.int32)
+    allowed = (index[None, :] <= index[:, None]) & (segs[None, :] == segs[:, None])
+    scores = jnp.einsum("qgd,kd->gqk", query, key, preferred_element_type=jnp.float32) * scale
+    weights = jnp.where(allowed[None], jnp.exp(scores - bound), 0.0)
+    totals = jnp.sum(weights, axis=-1)
+    mixed = jnp.einsum("gqk,kd->qgd", weights.astype(low), value, preferred_element_type=jnp.float32)
+    attended = mixed / jnp.transpose(totals)[..., None]
+    attended_low = attended.astype(low).reshape(tokens, groups * head_dim)
+    middle, nf = middle_step(dot(attended_low, out_full, low), xf, gain_two)
+    normed_two = nf.reshape(tokens, width)
+    hidden_width = gate_up.shape[1] // 2
+    both = dot(normed_two, gate_up)
+    gate_rows, up_rows = (both[:, :hidden_width], both[:, hidden_width:])
+    hidden_float, swiglu_pull = jax.vjp(swiglu, gate_rows, up_rows)
+    hidden = hidden_float.astype(low)
+    down_part = dot(hidden, down_full, low)
+    grad_hidden = dot_right(cot_all, down_full)
+    grad_gate, grad_up = swiglu_pull(grad_hidden)
+    grad_both = jnp.concatenate([grad_gate.astype(low), grad_up.astype(low)], axis=1)
+    gmid, gf, out_own, gain_two_grad = turn_step(
+        dot_right(grad_both, gate_up, low), down_part, cf, middle, gain_two
+    )
+    down_grad = lax.psum_scatter(
+        dot_left(hidden, cot_all, low), "uly", scatter_dimension=0, tiled=True
+    )
+    both_grad = dot_left(normed_two, grad_both, low).reshape(8, 4, -1, 2 * hidden_width)
+    both_grad = lax.psum_scatter(both_grad, "uly", scatter_dimension=1, tiled=False)
+    grad_mid = gf.reshape(tokens, width)
+    out_grad = lax.psum_scatter(
+        dot_left(attended_low, grad_mid, low), "uly", scatter_dimension=0, tiled=True
+    )
+    grad_att = dot_right(grad_mid, out_full, low).reshape(tokens, groups, head_dim)
+    delta = jnp.transpose(jnp.sum(grad_att.astype(jnp.float32) * attended, axis=-1))
+    probs = weights / totals[..., None]
+    grad_probs = jnp.einsum("qgd,kd->gqk", grad_att, value, preferred_element_type=jnp.float32)
+    grad_scores = (probs * (grad_probs - delta[..., None])).astype(low)
+    grad_query = (
+        jnp.einsum("gqk,kd->qgd", grad_scores, key, preferred_element_type=jnp.float32) * scale
+    )
+    grad_key = (
+        jnp.einsum("gqk,qgd->kd", grad_scores, query, preferred_element_type=jnp.float32) * scale
+    )
+    grad_value = jnp.einsum(
+        "gqk,qgd->kd", probs.astype(low), grad_att, preferred_element_type=jnp.float32
+    )
+    grad_query_pre, grad_key_pre, heads_grad = prep_pull(
+        (
+            grad_query.astype(low).astype(jnp.float32)[None],
+            grad_key.astype(low).astype(jnp.float32)[None, :, None],
+        )
+    )
+    grad_pre = jnp.concatenate(
+        [
+            grad_query_pre.astype(low).reshape(tokens, groups * head_dim),
+            grad_key_pre.astype(low).reshape(tokens, head_dim),
+            grad_value.astype(low),
+        ],
+        axis=1,
+    )
+    dw = dot_left(normed, grad_pre, low).reshape(8, 4, -1, grad_pre.shape[1])
+    small = jnp.concatenate(
+        [gain_two_grad.reshape(8, 128), heads_grad, jnp.zeros((6, 128), jnp.float32)], axis=0
+    )
+    per_device = (inputs.shape, query_weight.shape[1], key_matrix.shape[1], gate_weight.shape[1])
+    outputs, grad_inputs, q_grad, k_grad, v_grad, g_grad, u_grad, sums = last_step(
+        dot_right(grad_pre, w_qkv, low), xf, gmid, out_own, gain_one, small, dw, both_grad, per_device
+    )
+    floats = lambda v: v.astype(jnp.float32)
+    attn_gain_grad = lax.dynamic_slice(sums, (head, z * piece), (1, piece))[0]
+    ffn_gain_grad = lax.dynamic_slice(sums, (8 + head, z * piece), (1, piece))[0]
+    share = head_dim // 32
+    head_gain_grad = lax.dynamic_slice(sums, (16, (4 * head + z) * share), (2, share))
+    return (
+        outputs, grad_inputs, attn_gain_grad, head_gain_grad, floats(q_grad), floats(k_grad),
+        floats(v_grad), floats(out_grad), ffn_gain_grad, floats(g_grad), floats(u_grad),
+        floats(down_grad),
+    )
+
+
+def fits_plane(mesh, seq_count, heads):
+    shape = mesh.shape
+    return (shape["fsdp"], shape["blk"], shape["uly"]) == (2, 4, 4) and seq_count == 4 and heads == 8
+
+
 def solution(mesh):
-    return jax.shard_map(
-        body,
+    def step(*arrays):
+        seq_count = arrays[0].shape[0]
+        heads = arrays[5].shape[1] // arrays[3].shape[1]
+        chosen = plane_body if fits_plane(mesh, seq_count, heads) else body
+        return mapped(chosen)(*arrays)
+
+    mapped = functools.partial(
+        jax.shard_map,
         mesh=mesh,
         in_specs=(
             P("fsdp", ("blk", "uly"), None),
@@ -416,3 +1123,4 @@
         ),
         check_vma=False,
     )
+    return step

time: 1780 us -> 402 us (0.23)
  waiting for transfers between devices: 1380 us -> 46.5 us
  Pallas kernels: 0 us -> 177 us
  blocking collectives: 152 us -> 45.4 us
  starting transfers between devices: 88.4 us -> 0.16 us
  matrix products: 82.4 us -> 57.4 us
    reduce_scatter x7 -> x3, waiting for transfers between devices: 1030 us -> 46.4 us  [the longest x1 35.4 us: plane_body(): lax.psum_scatter(both_grad, 'uly', scatter_dimension=1, tiled=False)]
    all_gather x7 -> x1, waiting for transfers between devices: 295 us -> 0.01 us  [plane_body(): gate_up = lax.all_gather(gu_part, 'uly', axis=1, tiled=False)]
    pallas_call x0 -> x4, Pallas kernels: none -> 177 us  [the longest x1 57.1 us: gather_all(): pl.pallas_call(gather_kernel, name='gather_all', out_shape=(full, full, j...]
    unnamed x2 -> x0, blocking collectives: 80.7 us -> none
    ppermute x10 -> x0, starting transfers between devices: 73.4 us -> none  [the longest x6 46.2 us: passed_along(): lax.ppermute(value, axis, [(source, source + steps) for source in range(f...]
    all_to_all x4 -> x0, blocking collectives: 71.7 us -> none  [the longest x1 30.7 us: body(): lax.all_to_all(grad_query_low, 'uly', split_axis=1, concat_axis=2, tiled=...]
    all_gather x0 -> x2, blocking collectives: none -> 45.4 us  [the longest x1 25.4 us: plane_body(): out_full = lax.all_gather(out_weight, 'uly', axis=0, tiled=True)]
    all_to_all x4 -> x0, waiting for transfers between devices: 35.1 us -> none  [the longest x1 15.9 us: body(): lax.all_to_all(query_rot.astype(jnp.bfloat16), 'uly', split_axis=2, conca...]
  transfers between devices with their start and end apart: 28 -> 4, of which waited for: 23 -> 2; matrix products, arithmetic and copies ran while one was open for 5% -> 17% of each run, Pallas kernels for 0% -> 9%
where the time goes in v1:
time: 402 us; the launch traced here: 396 us
  Pallas kernels  177 us (44%)
  matrix products  57.4 us (14%)
  waiting for transfers between devices  46.5 us (12%)
  blocking collectives  45.4 us (11%)
  other arithmetic  34.3 us (9%)
  local copies, waits for them, and re-layouts  19.3 us (5%)
  between operations  15.9 us (4%)
    pallas_call x1, Pallas kernels, gather_all(): pl.pallas_call(gather_kernel, name='gather_all', out_shape=(full, full, j...  57.1 us
    pallas_call x1, Pallas kernels, turn_step(): pl.pallas_call(turn_kernel, name='turn_step', out_shape=(jax.ShapeDtypeSt...  43.2 us
    pallas_call x1, Pallas kernels, last_step(): pl.pallas_call(last_kernel, name='last_step', out_shape=(back, back, *wei...  42.7 us
    reduce_scatter x1, waiting for transfers between devices, plane_body(): lax.psum_scatter(both_grad, 'uly', scatter_dimension=1, tiled=False)  35.4 us
    pallas_call x1, Pallas kernels, middle_step(): pl.pallas_call(middle_kernel, name='middle_step', out_shape=(jax.ShapeDty...  34 us
    all_gather x1, blocking collectives, plane_body(): out_full = lax.all_gather(out_weight, 'uly', axis=0, tiled=True)  25.4 us
    all_gather x1, blocking collectives, plane_body(): down_full = lax.all_gather(down_weight, 'uly', axis=0, tiled=True)  20 us
    dot_general x4, matrix products, dot_left(): lax.dot_general(a, b, (((0,), (0,)), ((), ())), preferred_element_type=jn...  12.2 us
  transfers between devices with their start and end apart: 4, of which 2 were waited for; matrix products, arithmetic and copies ran while one was open for 17% of the time, Pallas kernels for 9%

profile of v1, /device:TPU:0, one launch (start us, length us, event | category | flops | bytes accessed | tf_op | source)
XLA Modules:
  0.0 395.9 jit_solution(4916504882209953207)
XLA Ops:
  9.2 57.1 %gather_all.1 = (bf16[4,4,2,32,1024]{4,3,2,1,0:T(8,128)(2,1)}, bf16[4,4,2,32,1024]{4,3,2,1,0:T(8,128)(2,1)}, s32[2,2,1024]{2,1,0:T(2,128)}, bf16[8,4,32,512]{3,2...) custom-call(bf16[2,64,1024]{2,1,0:T(8,128)(2,1)} %x_ref.1, bf16[2,64,1024]{2,1,0:T(8,128)(2,1)} %cot_ref.1, ...), custom_call_target="tpu_custom_call" | custom-call | tf_op jit(solution)/shard_map/gather_all/pallas_call | solution.py:595
  71.4 2.2 multiply_reduce_fusion
  85.0 25.4 %all_gather.13 = bf16[256,1024]{1,0:T(8,128)(2,1)} all-gather(bf16[64,1024]{1,0:T(8,128)(2,1)S(1)} %copy-done.29), channel_id=1, replica_groups=mesh['fsdp'=2,'blk'=4,'uly'=4] {'uly'}, dimensions={0}, use_global_device_ids=true | all-gather | bytes 655360 | tf_op jit(solution)/shard_map/all_gather | solution.py:965
  116.7 2.9 fusion.4
  119.6 3.6 fusion.97
  125.3 34.0 %middle_step.1 = (f32[4,32,1024]{2,1,0:T(8,128)}, bf16[4,4,2,32,1024]{4,3,2,1,0:T(8,128)(2,1)}) custom-call(bf16[4,4,2,32,1024]{4,3,2,1,0:T(8,128)(2,1)} %bitcast.225, bf16[4,4,2,32,1024]{4,3,2,1,0:T(8,128)(2,1)} %get-tuple-element.56.xf_ref, f32[1,1024]{1,0:T(1,128)} %reshape_squeeze.6.gain_ref), custom_call_target="tpu_custom_call" | custom-call | tf_op jit(solution)/shard_map/middle_step/pallas_call | solution.py:689
  159.4 20.0 %all_gather.12 = bf16[384,1024]{1,0:T(8,128)(2,1)} all-gather(bf16[96,1024]{1,0:T(8,128)(2,1)} %param.28), channel_id=1, replica_groups=mesh['fsdp'=2,'blk'=4,'uly'=4] {'uly'}, dimensions={0}, use_global_device_ids=true | all-gather | bytes 983040 | tf_op jit(solution)/shard_map/all_gather | solution.py:966
  181.3 4.1 %fusion.99 = f32[1024,768]{0,1:T(8,128)S(1)} fusion(bf16[1024,1024]{1,0:T(8,128)(2,1)} %bitcast.254, bf16[1024,768]{1,0:T(8,128)(2,1)} %bitcast.258), kind=kOutput, calls=%fused_computation.179 | convolution fusion | flops 1610612736 | bytes 6815744 | tf_op jit(solution)/shard_map/dot_general | solution.py:941
  187.1 2.7 convolution_convert_fusion
  189.8 3.3 convolution_convert_fusion.3
  193.0 43.2 %turn_step.1 = (f32[4,32,1024]{2,1,0:T(8,128)}, bf16[4,4,2,32,1024]{4,3,2,1,0:T(8,128)(2,1)}, bf16[4,32,1024]{2,1,0:T(8,128)(2,1)}, f32[1,1024]{1,0:T(1,128)}) custom-call(bf16[4,4,2,32,1024]{4,3,2,1,0:T(8,128)(2,1)} %bitcast.233, bf16[4,4,2,32,1024]{4,3,2,1,0:T(8,128)(2,1)} %bitcast.232, bf16[4,4,2,32,1024]{4,3,2,1,0:T(8,128)(2,1)} %get-tuple-element.60.cf_ref, ...), custom_call_target="tpu_custom_call" | custom-call | tf_op jit(solution)/shard_map/turn_step/pallas_call | solution.py:748
  236.2 3.1 convolution_convert_fusion.7
  239.3 2.9 multiply_reduce_fusion.1
  242.3 6.0 %fusion.1 = bf16[2,1024,1024]{1,2,0:T(8,128)(2,1)S(1)} fusion(f32[2,1024]{1,0:T(2,128)S(1)} %bitcast.263, bf16[1024,2,128]{0,2,1:T(8,128)(2,1)S(1)} %bitcast.260, f32[2,1024]{1,0:T(2,128)S(1)} %get-tuple-element.127, f32[]{:T(128)S(6)} %mul.706, f32[1024,1024,2]{1,0,2:T(8,128)} %copy-done.37, pred[1024,1024]{0,1:T(8,128)(4,1)S(1)} %copy-done.15, ...), kind=kOutput, calls=%fused_computation.2 | convolution fusion | flops 551550976 | bytes 14434308 | tf_op jit(solution)/shard_map/qgd,kd->gqk/dot_general | solution.py:1035
  250.3 2.3 fusion.31
  252.7 3.7 convolution_convert_fusion.6
  256.4 4.4 %fusion.22 = f32[1024,2,128]{0,2,1:T(8,128)} fusion(bf16[2,1024,1024]{1,2,0:T(8,128)(2,1)} %copy-done.5, f32[1024,128]{0,1:T(8,128)S(1)} %get-tuple-element.90, f32[1024,64]{0,1:T(8,128)} %get-tuple-element.98, f32[1024,64]{0,1:T(8,128)S(1)} %get-tuple-element.95, f32[1024,128]{0,1:T(8,128)S(1)} %get-tuple-element.89, f32[1024,4,128]{0,2,1:T(8,128)S(1)} %copy-done.3, ...), kind=kOutput, calls=%fused_computation.39 | convolution fusion | flops 538574848 | bytes 7344640 | tf_op jit(solution)/shard_map/gqk,kd->qgd/dot_general | solution.py:1038
  260.8 3.0 convolution_convert_fusion.4
  274.0 5.5 %fusion.27 = bf16[1024,128]{0,1:T(8,128)(2,1)S(1)} fusion(bf16[1024,2,128]{0,2,1:T(8,128)(2,1)S(1)} %bitcast.261, f32[1024,1024,2]{1,0,2:T(8,128)} %copy-done.37, f32[2,1024]{1,0:T(2,128)S(1)} %get-tuple-element.127, f32[]{:T(128)S(6)} %mul.706, pred[1024,1024]{0,1:T(8,128)(4,1)S(1)} %copy-done.16), kind=kOutput, calls=%fused_computation.45 | convolution fusion | flops 547487744 | bytes 10231812 | tf_op jit(solution)/shard_map/gqk,qgd->kd/dot_general | solution.py:1043
  279.6 2.6 convolution_convert_fusion.1
  282.2 2.3 convolution_convert_fusion.5
  286.1 11.0 %reduce-scatter.8.cloned.1.call-done = bf16[96,1024]{1,0:T(8,128)(2,1)} async-done(((bf16[384,1024]{1,0:T(8,128)(2,1)}), bf16[96,1024]{1,0:T(8,128)(2,1)}) %reduce-scatter.8.cloned.1.call-update) | async-done | bytes 196624 | tf_op jit(solution)/shard_map/reduce_scatter | solution.py:1023
  298.9 35.4 %reduce-scatter.4.cloned.1.call-done = bf16[8,1,32,768]{3,2,0,1:T(8,128)(2,1)} async-done(((bf16[8,4,32,768]{3,2,0,1:T(8,128)(2,1)}), bf16[8,1,32,768]{3,2,0,1:T(8,128)(2,1)}) %reduce-scatter.4.cloned.1.call-update) | async-done | bytes 393232 | tf_op jit(solution)/shard_map/reduce_scatter | solution.py:1027
  334.3 42.7 %last_step.1 = (bf16[2,64,1024]{2,1,0:T(8,128)(2,1)}, bf16[2,64,1024]{2,1,0:T(8,128)(2,1)}, bf16[32,2048]{1,0:T(8,128)(2,1)}, bf16[32,1024]{1,0:T(8,128)(2,1)}, ...) custom-call(bf16[4,4,2,32,1024]{4,3,2,1,0:T(8,128)(2,1)} %bitcast.235, ...), custom_call_target="tpu_custom_call" | custom-call | tf_op jit(solution)/shard_map/last_step/pallas_call | solution.py:889
  (164 shorter events, 56.6 us)
Async XLA Ops:
  7.2 174.1 %all-gather.3.cloned.1.call-start = ((), (), s32[]{:S(2)}) async-start(), calls=%async_computation.6 | async-start | bytes 1966080 | tf_op jit(solution)/shard_map/all_gather | solution.py:975
  66.3 7.4 %copy-start.12 = (bf16[8,4,32,512]{3,2,1,0:T(8,128)(2,1)S(1)}, bf16[8,4,32,512]{3,2,1,0:T(8,128)(2,1)}, u32[]{:S(2)}) copy-start(bf16[8,4,32,512]{3,2,1,0:T(8,128)(2,1)} %get-tuple-element.58) | copy-start | bytes 3145732
  66.4 218.1 %reduce-scatter.6.cloned.1.call-start = ((), (), s32[]{:S(2)}) async-start(), calls=%async_computation.4 | async-start | bytes 655360 | tf_op jit(solution)/shard_map/reduce_scatter | solution.py:1029
  71.4 3.6 copy-start
  77.7 41.9 %copy-start.2 = (f32[1024,4,128]{0,2,1:T(8,128)}, f32[1024,4,128]{0,2,1:T(8,128)S(1)}, u32[]{:S(2)}) copy-start(f32[1024,4,128]{0,2,1:T(8,128)S(1)} %fusion.98) | copy-start | bytes 6291460
  116.5 3.1 copy-start.21
  119.6 3.6 copy-start.37
  119.6 3.6 copy-start.10
  125.3 54.1 %copy-start.1 = (bf16[4,4,2,32,1024]{4,3,2,1,0:T(8,128)(2,1)S(1)}, bf16[4,4,2,32,1024]{4,3,2,1,0:T(8,128)(2,1)}, u32[]{:S(2)}) copy-start(bf16[4,4,2,32,1024]{4,3,2,1,0:T(8,128)(2,1)} %get-tuple-element.56.xf_ref) | copy-start | bytes 6291460
  181.3 4.1 %copy-start.7 = (bf16[4,4,2,32,1024]{4,3,2,1,0:T(8,128)(2,1)S(1)}, bf16[4,4,2,32,1024]{4,3,2,1,0:T(8,128)(2,1)}, u32[]{:S(2)}) copy-start(bf16[4,4,2,32,1024]{4,3,2,1,0:T(8,128)(2,1)} %get-tuple-element.60.cf_ref) | copy-start | bytes 6291460
  181.3 4.1 %copy-start.18 = (bf16[384,1024]{1,0:T(8,128)(2,1)S(1)}, bf16[384,1024]{1,0:T(8,128)(2,1)}, u32[]{:S(2)}) copy-start(bf16[384,1024]{1,0:T(8,128)(2,1)} %all_gather.12) | copy-start | bytes 2359300
  193.0 43.2 %copy-start.24 = (bf16[1024,2,128]{0,2,1:T(8,128)(2,1)S(1)}, bf16[1024,2,128]{0,2,1:T(8,128)(2,1)}, u32[]{:S(2)}) copy-start(bf16[1024,2,128]{0,2,1:T(8,128)(2,1)} %copy-done.23) | copy-start | bytes 1572868
  239.3 2.9 copy-start.3
  239.3 3.0 copy-start.15
  242.3 6.0 %copy-start.34 = (bf16[1024,256]{0,1:T(8,128)(2,1)}, bf16[1024,256]{0,1:T(8,128)(2,1)S(1)}, u32[]{:S(2)}) copy-start(bf16[1024,256]{0,1:T(8,128)(2,1)S(1)} %get-tuple-element.132) | copy-start | bytes 1572868
  242.3 8.0 %copy-start.22 = (bf16[1024,2,128]{0,2,1:T(8,128)(2,1)S(1)}, bf16[1024,2,128]{0,2,1:T(8,128)(2,1)}, u32[]{:S(2)}) copy-start(bf16[1024,2,128]{0,2,1:T(8,128)(2,1)} %copy-done.21) | copy-start | bytes 1572868
  252.6 44.5 %reduce-scatter.8.cloned.1.call-start = ((), (), s32[]{:S(2)}) async-start(), calls=%async_computation.5 | async-start | bytes 983040 | tf_op jit(solution)/shard_map/reduce_scatter | solution.py:1023
  256.4 4.4 %copy-start.32 = (bf16[4,4,2,32,1024]{4,3,2,1,0:T(8,128)(2,1)S(1)}, bf16[4,4,2,32,1024]{4,3,2,1,0:T(8,128)(2,1)}, u32[]{:S(2)}) copy-start(bf16[4,4,2,32,1024]{4,3,2,1,0:T(8,128)(2,1)} %get-tuple-element.61) | copy-start | bytes 6291460
  256.4 4.4 %copy-start.39 = (bf16[1024,384]{0,1:T(8,128)(2,1)S(1)}, bf16[1024,384]{0,1:T(8,128)(2,1)}, u32[]{:S(2)}) copy-start(bf16[1024,384]{0,1:T(8,128)(2,1)} %copy-done.38) | copy-start | bytes 2359300
  256.4 4.4 %copy-start.41 = (bf16[1024,384]{0,1:T(8,128)(2,1)S(1)}, bf16[1024,384]{0,1:T(8,128)(2,1)}, u32[]{:S(2)}) copy-start(bf16[1024,384]{0,1:T(8,128)(2,1)} %copy-done.40) | copy-start | bytes 2359300
  263.9 70.4 %reduce-scatter.4.cloned.1.call-start = ((), (), s32[]{:S(2)}) async-start(), calls=%async_computation.3 | async-start | bytes 1966080 | tf_op jit(solution)/shard_map/reduce_scatter | solution.py:1027
  274.0 5.5 %copy-start.13 = (bf16[8,4,32,512]{3,2,1,0:T(8,128)(2,1)S(1)}, bf16[8,4,32,512]{3,2,1,0:T(8,128)(2,1)}, u32[]{:S(2)}) copy-start(bf16[8,4,32,512]{3,2,1,0:T(8,128)(2,1)} %get-tuple-element.58) | copy-start | bytes 3145732
  377.0 10.7 %copy-start.26 = (bf16[2,64,1024]{2,1,0:T(8,128)(2,1)S(1)}, bf16[2,64,1024]{2,1,0:T(8,128)(2,1)}, u32[]{:S(2)}) copy-start(bf16[2,64,1024]{2,1,0:T(8,128)(2,1)} %get-tuple-element.151) | copy-start | bytes 786436
  377.0 11.4 %copy-start.25 = (bf16[2,64,1024]{2,1,0:T(8,128)(2,1)S(1)}, bf16[2,64,1024]{2,1,0:T(8,128)(2,1)}, u32[]{:S(2)}) copy-start(bf16[2,64,1024]{2,1,0:T(8,128)(2,1)} %get-tuple-element.152) | copy-start | bytes 786436
  (22 other events, 41.3 us)
Sparse Core Ops, SparseCore 0:
  66.5 46.2 all-gather.2
  252.8 20.6 reduce-scatter.5
  275.8 21.3 reduce-scatter.7
  299.3 34.9 reduce-scatter.3

commit v2 on v1

--- a/solution.py
+++ b/solution.py
@@ -456,11 +456,19 @@
     def go(self, *args):
         copy = remote(*args)
         copy.start()
-        self.pending.append(copy)
+        self.pending.append((None, copy))
+
+    def go_if(self, condition, *args):
+        copy = remote(*args)
+        pl.when(condition)(lambda: copy.start())
+        self.pending.append((condition, copy))
 
     def drain(self):
-        for copy in self.pending:
-            copy.wait_send()
+        for condition, copy in self.pending:
+            if condition is None:
+                copy.wait_send()
+            else:
+                pl.when(condition)(lambda copy=copy: copy.wait_send())
 
 
 def spread_start(me, sends, src, full, send_sems, recv_sems):
@@ -480,138 +488,8 @@
         arrived(me.shard(full, dx, dy, 1), recv_sems.at[3 + i])
 
 
-def gather_kernel(
-    x_ref, cot_ref, seg_ref, q_ref, k_ref, v_ref, g_ref, u_ref, gain_ref,
-    xf_ref, cf_ref, segf_ref, w_ref, gu_ref, gains_ref,
-    ps, pr, as_, ar, ws, wr, zs, zr, us, ur, gs, gr, ls,
-):
-    me = Place()
-    x, z, p = (me.x, me.z, me.head)
-    across = [((x + 1) % 2, me.block, me.ahead(turn)) for turn in TURNS]
-    meet([me.peer(*d) for d in PLANE[1:]] + [me.line(turn) for turn in TURNS] + across)
-    sends = Sends()
-    half = x_ref.shape[1] // 2
-    own_gain = pltpu.make_async_copy(gain_ref, gains_ref.at[p, z], ls.at[0])
-    own_gain.start()
-    own_seg = pltpu.make_async_copy(seg_ref, segf_ref.at[x], ls.at[1])
-    own_seg.start()
-    sends.go(seg_ref, segf_ref.at[x], ls.at[2], ls.at[3], me.peer(1, 0, 0))
-    for turn in TURNS:
-        sends.go(gain_ref, gains_ref.at[p, z], gs.at[turn], gr.at[turn], me.line(turn))
-
-    def permute(src_ref, full_ref, o, wait=False):
-        for j in (0, 1):
-            for to in (0, 1):
-                src = src_ref.at[j, pl.ds(half * to, half)]
-                dst = full_ref.at[me.block, z, to]
-                target = (to, me.block, 2 * x + j)
-                mine = jnp.logical_and(x == to, z == 2 * x + j)
-                copy = remote(src, dst, ps.at[o + 2 * j + to], pr.at[o + z], target)
-
-                @pl.when(jnp.logical_not(mine))
-                def _():
-                    if wait:
-                        copy.wait_send()
-                    else:
-                        copy.start()
-
-                if not wait:
-
-                    @pl.when(mine)
-                    def _():
-                        pltpu.make_async_copy(src, dst, pr.at[o + z]).start()
-
-    def permuted(full_ref, o):
-        for k in range(4):
-            arrived(full_ref.at[me.block, k, x], pr.at[o + k])
-
-    permute(x_ref, xf_ref, 0)
-    wide, narrow = (q_ref.shape[1] // 8, k_ref.shape[1] // 8)
-    cuts = ((q_ref, wide, 0), (k_ref, narrow, wide), (v_ref, narrow, wide + narrow))
-    for i, d in enumerate(PLANE):
-        t = me.index(*d)
-        for n, (ref, width, off) in enumerate(cuts):
-            src = ref.at[:, pl.ds(pl.multiple_of(t * width, 128), width)]
-            dst = w_ref.at[p, z, :, pl.ds(off, width)]
-            if i == 0:
-                pltpu.make_async_copy(src, dst, wr.at[n]).start()
-            else:
-                sends.go(src, dst, ws.at[3 * i + n], wr.at[3 * i + n], me.peer(*d))
-    permute(cot_ref, cf_ref, 4)
-    permuted(xf_ref, 0)
-    spread_start(me, sends, me.shard(xf_ref), xf_ref, as_, ar)
-    for i, d in enumerate(PLANE):
-        t = me.index(*d)
-        for n, (ref, width, off) in enumerate(cuts):
-            arrived(w_ref.at[t, z, :, pl.ds(off, width)], wr.at[3 * i + n])
-        for turn in TURNS:
-            s = 3 * i + turn - 1
-            sends.go(w_ref.at[t, z], w_ref.at[t, z], zs.at[s], zr.at[s], me.line(turn))
-    width = g_ref.shape[1] // 8
-    for i, d in enumerate(PLANE):
-        t = me.index(*d)
-        for n, ref in enumerate((g_ref, u_ref)):
-            src = ref.at[:, pl.ds(pl.multiple_of(t * width, 128), width)]
-            dst = gu_ref.at[p, :, pl.ds(n * width, width)]
-            if i == 0:
-                pltpu.make_async_copy(src, dst, ur.at[n]).start()
-            else:
-                sends.go(src, dst, us.at[2 * i + n], ur.at[2 * i + n], me.peer(*d))
-    permuted(cf_ref, 4)
-    spread_start(me, sends, me.shard(cf_ref), cf_ref, as_.at[pl.ds(7, 7)], ar.at[pl.ds(7, 7)])
-    own_gain.wait()
-    own_seg.wait()
-    arrived(segf_ref.at[(x + 1) % 2], ls.at[3])
-    for turn in TURNS:
-        arrived(gains_ref.at[p, me.behind(turn)], gr.at[turn])
-    for i, d in enumerate(PLANE[1:]):
-        sends.go(gains_ref.at[p], gains_ref.at[p], gs.at[4 + i], gr.at[4 + i], me.peer(*d))
-    spread_forward(me, sends, xf_ref, as_, ar)
-    spread_finish(me, xf_ref, ar)
-    for i, d in enumerate(PLANE[1:]):
-        arrived(gains_ref.at[me.index(*d)], gr.at[4 + i])
-    for i, d in enumerate(PLANE):
-        for turn in TURNS:
-            arrived(w_ref.at[me.index(*d), me.behind(turn)], zr.at[3 * i + turn - 1])
-    for i, d in enumerate(PLANE):
-        for n in (0, 1):
-            arrived(gu_ref.at[me.index(*d), :, pl.ds(n * width, width)], ur.at[2 * i + n])
-    spread_forward(me, sends, cf_ref, as_.at[pl.ds(7, 7)], ar.at[pl.ds(7, 7)])
-    spread_finish(me, cf_ref, ar.at[pl.ds(7, 7)])
-    permute(x_ref, xf_ref, 0, wait=True)
-    permute(cot_ref, cf_ref, 4, wait=True)
-    sends.drain()
-
-
 def full_shape(tokens, width):
     return (4, 4, 2, tokens // 32, width)
-
-
-def gather_all(x, cot, seg, q, k, v, g, u, gain):
-    tokens, width = (16 * x.shape[1], x.shape[2])
-    rows = q.shape[0]
-    cols = (q.shape[1] + 2 * k.shape[1]) // 8
-    full = jax.ShapeDtypeStruct(full_shape(tokens, width), jnp.bfloat16)
-    return pl.pallas_call(
-        gather_kernel,
-        name="gather_all",
-        out_shape=(
-            full,
-            full,
-            jax.ShapeDtypeStruct((2,) + seg.shape, seg.dtype),
-            jax.ShapeDtypeStruct((8, 4, rows, cols), jnp.bfloat16),
-            jax.ShapeDtypeStruct((8, rows, g.shape[1] // 4), jnp.bfloat16),
-            jax.ShapeDtypeStruct((8, 4, 8, 128), jnp.float32),
-        ),
-        in_specs=[ANY] * 9,
-        out_specs=(ANY,) * 6,
-        scratch_shapes=[SEM((8,)), SEM((8,)), SEM((14,)), SEM((14,))]
-        + [SEM((24,))] * 4
-        + [SEM((16,))] * 2
-        + [SEM((11,))] * 2
-        + [SEM((4,))],
-        compiler_params=pltpu.CompilerParams(collective_id=0, has_side_effects=True),
-    )(x, cot, seg, q, k, v, g, u, gain)
 
 
 def half_start(me, sends, part, kept, sibling, keep_sems, send_sems, recv_sems):
@@ -658,48 +536,372 @@
     return [me.peer(*d) for d in FAR + [(0, 0, 1)]]
 
 
-def middle_kernel(
-    part_ref, xf_ref, gain_ref, mid_ref, nf_ref,
-    kept, sibling, out, came, ks, ss, rs, xs_ref, n_ref, as_, ar, ls,
+def line_spread(me, sends, src, part, sems):
+    for dz in (1, 2):
+        sends.go_if(me.z < 4 - dz, src, part(me.z), sems.at[0, dz - 1], sems.at[1, dz - 1], me.line(dz))
+        sends.go_if(me.z >= dz, src, part(me.z), sems.at[0, dz + 1], sems.at[1, dz + 1], me.line(4 - dz))
+
+
+def line_forward(me, sends, part, sems):
+    inner = jnp.logical_or(me.z == 1, me.z == 2)
+    ref = part((me.z + 2) % 4)
+    pl.when(me.z == 1)(lambda: arrived(ref, sems.at[1, 3]))
+    pl.when(me.z == 2)(lambda: arrived(ref, sems.at[1, 1]))
+    target = (me.x, me.block, (3 * me.z + 1) % 4)
+    sends.go_if(inner, ref, ref, sems.at[0, 4], sems.at[1, 4], target)
+
+
+def line_finish(me, part, sems):
+    z = me.z
+    pl.when(z > 0)(lambda: arrived(part((z + 3) % 4), sems.at[1, 0]))
+    pl.when(z < 3)(lambda: arrived(part((z + 1) % 4), sems.at[1, 2]))
+
+    @pl.when(z == 3)
+    def _():
+        arrived(part((z + 2) % 4), sems.at[1, 1])
+        arrived(part((z + 1) % 4), sems.at[1, 4])
+
+    @pl.when(z == 0)
+    def _():
+        arrived(part((z + 2) % 4), sems.at[1, 3])
+        arrived(part((z + 3) % 4), sems.at[1, 4])
+
+
+def lanes(shape):
+    return lax.broadcasted_iota(jnp.int32, shape, len(shape) - 1)
+
+
+def turned(vector):
+    half = vector.shape[-1] // 2
+    sign = jnp.where(lanes((1, 2 * half)) < half, -1.0, 1.0)
+    return pltpu.roll(vector, half, 1) * sign
+
+
+def head_scale(vector):
+    return lax.rsqrt(jnp.mean(vector * vector, axis=-1, keepdims=True) + EPSILON)
+
+
+def mat(a, b):
+    return jnp.dot(a, b, preferred_element_type=jnp.float32)
+
+
+def mat_right(a, b):
+    return lax.dot_general(a, b, (((1,), (1,)), ((), ())), preferred_element_type=jnp.float32)
+
+
+def mat_left(a, b):
+    return lax.dot_general(a, b, (((0,), (0,)), ((), ())), preferred_element_type=jnp.float32)
+
+
+def permute_in(me, src_ref, full_ref, send_sems, recv_sems, wait=False):
+    half = src_ref.shape[1] // 2
+    for j in (0, 1):
+        for to in (0, 1):
+            src = src_ref.at[j, pl.ds(half * to, half)]
+            dst = full_ref.at[me.block, me.z, to]
+            mine = jnp.logical_and(me.x == to, me.z == 2 * me.x + j)
+            copy = remote(
+                src, dst, send_sems.at[2 * j + to], recv_sems.at[me.z], (to, me.block, 2 * me.x + j)
+            )
+            if wait:
+                pl.when(jnp.logical_not(mine))(lambda copy=copy: copy.wait_send())
+                continue
+            pl.when(jnp.logical_not(mine))(lambda copy=copy: copy.start())
+            own = pltpu.make_async_copy(src, dst, recv_sems.at[me.z])
+            pl.when(mine)(lambda own=own: own.start())
+
+
+def permuted_in(me, full_ref, recv_sems):
+    for k in range(4):
+        arrived(full_ref.at[me.block, k, me.x], recv_sems.at[k])
+
+
+def half_block(me, sends, part, sibling, send_sems, recv_sems, b):
+    other = me.c != b % 2
+    dy = (me.y + b // 2) % 2
+    for to in (0, 1):
+        slot = 3 - 2 * ((me.x + to) % 2) - dy
+        sends.go_if(
+            other, part.at[b, :, to], sibling.at[slot], send_sems.at[slot], recv_sems.at[slot],
+            me.peer(0, 0, 1),
+        )
+
+
+def half_out(me, sends, part, sibling, out, came, send_sems, recv_sems):
+    for i, d in enumerate(FAR):
+        x, y, c = me.coords(*d)
+        arrived(sibling.at[i], recv_sems.at[i])
+        own = part[2 * y + c, :, x].astype(jnp.float32)
+        out[i] = (own + sibling[i].astype(jnp.float32)).astype(jnp.bfloat16)
+        sends.go(out.at[i], came.at[i], send_sems.at[4 + i], recv_sems.at[4 + i], me.peer(*d))
+
+
+def half_in(me, part, sibling, came, recv_sems):
+    arrived(sibling.at[3], recv_sems.at[3])
+    total = part[me.block, :, me.x].astype(jnp.float32) + sibling[3].astype(jnp.float32)
+    for i in (1, 2, 0):
+        arrived(came.at[i], recv_sems.at[4 + i])
+        total = total + came[i].astype(jnp.float32)
+    return total
+
+
+def half_scratch(tokens, width):
+    piece = (4, tokens // 32, width)
+    return [
+        pltpu.VMEM((4,) + piece, jnp.bfloat16),
+        pltpu.VMEM((3,) + piece, jnp.bfloat16),
+        pltpu.VMEM((3,) + piece, jnp.bfloat16),
+        SEM((7,)),
+        SEM((7,)),
+    ]
+
+
+def gain_row(gains_ref, kind):
+    rows = [jnp.sum(gains_ref[p, :, kind, :], axis=0, keepdims=True) for p in range(8)]
+    return jnp.concatenate(rows, axis=1)
+
+
+def allowed_keys(segcol, segrow, b, kb):
+    same = segcol[b] == segrow[:, 256 * kb : 256 * kb + 256]
+    if kb < b:
+        return same
+    rows = lax.broadcasted_iota(jnp.int32, (256, 256), 0)
+    return jnp.logical_and(same, lanes((256, 256)) <= rows)
+
+
+def forward_kernel(
+    x_ref, cot_ref, seg_ref, q_ref, k_ref, v_ref, g_ref, u_ref, o_ref, d_ref, gain_ref, hg_ref,
+    cf_ref, nf_ref, guf_ref, df_ref, segf_ref, wq_out, of_out, n1_out, xs_out, pre_out, qkv_out,
+    att_out, cos_out, sin_out, mid_ref, grow_ref,
+    xf, wf, of, segs, gains, n1, pre, qkv, segcol, cos_s, sin_s, att, attlow, part, n2,
+    sibling, out, came, hs, hr, ps, pr, as_, ar, ws, wr, us, ur, gs, gr, zq, zo, zd, zg, ls,
 ):
     me = Place()
-    meet(near(me))
+    x, z, p = (me.x, me.z, me.head)
+    across = [((x + 1) % 2, me.block, me.ahead(turn)) for turn in TURNS]
+    meet([me.peer(*d) for d in PLANE[1:]] + [me.line(turn) for turn in TURNS] + across)
     sends = Sends()
-    half_start(me, sends, part_ref, kept, sibling, ks, ss, rs)
-    own_x = pltpu.make_async_copy(me.shard(xf_ref), xs_ref, ls.at[0])
-    own_x.start()
-    half_send(me, sends, kept, sibling, out, came, ks, ss, rs)
-    own_x.wait()
-    middle = xs_ref[...].astype(jnp.float32) + half_sum(kept, sibling, came, ks, rs)
+
+    def local(src, dst, sem):
+        copy = pltpu.make_async_copy(src, dst, sem)
+        copy.start()
+        return copy
+
+    own_gain = local(gain_ref, gains.at[p, z], ls.at[0])
+    own_seg = local(seg_ref, segs.at[x], ls.at[1])
+    sends.go(seg_ref, segs.at[x], ls.at[2], ls.at[3], me.peer(1, 0, 0))
+    for turn in TURNS:
+        sends.go(gain_ref, gains.at[p, z], gs.at[turn], gr.at[turn], me.line(turn))
+    permute_in(me, x_ref, xf, ps.at[0], pr.at[0])
+    own_o = local(o_ref, of.at[z], ls.at[4])
+    own_d = local(d_ref, df_ref.at[z], ls.at[5])
+    wide, narrow = (q_ref.shape[1] // 8, k_ref.shape[1] // 8)
+    cuts = ((q_ref, wide, 0), (k_ref, narrow, wide), (v_ref, narrow, wide + narrow))
+    for i, d in enumerate(PLANE):
+        t = me.index(*d)
+        for n, (ref, width, off) in enumerate(cuts):
+            src = ref.at[:, pl.ds(pl.multiple_of(t * width, 128), width)]
+            dst = wf.at[p, z, :, pl.ds(off, width)]
+            if i == 0:
+                local(src, dst, wr.at[n])
+            else:
+                sends.go(src, dst, ws.at[3 * i + n], wr.at[3 * i + n], me.peer(*d))
+    permuted_in(me, xf, pr.at[0])
+    spread_start(me, sends, me.shard(xf), xf, as_.at[0], ar.at[0])
+    for i, d in enumerate(PLANE):
+        t = me.index(*d)
+        for n, (ref, width, off) in enumerate(cuts):
+            arrived(wf.at[t, z, :, pl.ds(off, width)], wr.at[3 * i + n])
+    qkv_part = lambda k: wf.at[:, k]
+    o_part = lambda k: of.at[k]
+    d_part = lambda k: df_ref.at[k]
+    gu_part = lambda k: guf_ref.at[:, k]
+    line_spread(me, sends, qkv_part(z), qkv_part, zq)
+    permute_in(me, cot_ref, cf_ref, ps.at[1], pr.at[1])
+    line_spread(me, sends, o_ref, o_part, zo)
+    width = g_ref.shape[1] // 8
+    for i, d in enumerate(PLANE):
+        t = me.index(*d)
+        for n, ref in enumerate((g_ref, u_ref)):
+            src = ref.at[:, pl.ds(pl.multiple_of(t * width, 128), width)]
+            dst = guf_ref.at[p, z, :, pl.ds(n * width, width)]
+            if i == 0:
+                local(src, dst, ur.at[n])
+            else:
+                sends.go(src, dst, us.at[2 * i + n], ur.at[2 * i + n], me.peer(*d))
+    own_gain.wait()
+    for turn in TURNS:
+        arrived(gains.at[p, me.behind(turn)], gr.at[turn])
+    for i, d in enumerate(PLANE[1:]):
+        sends.go(gains.at[p], gains.at[p], gs.at[4 + i], gr.at[4 + i], me.peer(*d))
+    own_seg.wait()
+    arrived(segs.at[(x + 1) % 2], ls.at[3])
+    local(segs, segf_ref, ls.at[6])
+    head_dim = hg_ref.shape[1]
+    segrow = segs[z // 2, pl.ds(z % 2, 1), :]
+    tokens = segrow.shape[1]
+    column = jnp.transpose(jnp.broadcast_to(segrow.astype(jnp.float32), (8, tokens)))[:, :1]
+    segcol[...] = column.astype(jnp.int32).reshape(4, 256, 1)
+    half_lane = (lanes((1, head_dim)) % (head_dim // 2)).astype(jnp.float32)
+    inverse = jnp.exp(half_lane * (-2.0 * math.log(THETA) / head_dim))
+    steps = lax.broadcasted_iota(jnp.int32, (32, head_dim), 0).astype(jnp.float32) * inverse
+    cl, sl = (jnp.cos(steps), jnp.sin(steps))
+    ch, sh = (jnp.cos(steps * 32.0), jnp.sin(steps * 32.0))
+    doc_cos, doc_sin = ([], [])
+    for doc in range(DOCS):
+        start = jnp.sum((segrow < doc).astype(jnp.float32), axis=1, keepdims=True)
+        doc_cos.append(jnp.cos(start * inverse))
+        doc_sin.append(jnp.sin(start * inverse))
+    for b in range(4):
+        hi_c, hi_s = (ch[8 * b : 8 * b + 8][:, None, :], sh[8 * b : 8 * b + 8][:, None, :])
+        cos_at = (hi_c * cl[None] - hi_s * sl[None]).reshape(256, head_dim)
+        sin_at = (hi_s * cl[None] + hi_c * sl[None]).reshape(256, head_dim)
+        column = segcol[b]
+        cd, sd = (jnp.broadcast_to(v[0], (256, head_dim)) for v in (doc_cos, doc_sin))
+        for doc in range(1, DOCS):
+            cd = jnp.where(column == doc, doc_cos[doc], cd)
+            sd = jnp.where(column == doc, doc_sin[doc], sd)
+        cos_s[b] = cos_at * cd + sin_at * sd
+        sin_s[b] = sin_at * cd - cos_at * sd
+    local(cos_s, cos_out, ls.at[7])
+    local(sin_s, sin_out, ls.at[8])
+    for i, d in enumerate(PLANE[1:]):
+        arrived(gains.at[me.index(*d)], gr.at[4 + i])
+    gain_one, gain_two = (gain_row(gains, 0), gain_row(gains, 1))
+    grow_ref[0:1] = gain_one
+    grow_ref[1:2] = gain_two
+    line_forward(me, sends, qkv_part, zq)
+    spread_forward(me, sends, xf, as_.at[0], ar.at[0])
+    spread_finish(me, xf, ar.at[0])
+    xs_copy = local(me.shard(xf), xs_out, ls.at[9])
+
+    def norm_block(b, carry):
+        rows = xf[b].reshape(256, -1).astype(jnp.float32)
+        n1[b] = (rows * head_scale(rows) * gain_one).astype(jnp.bfloat16)
+        return carry
+
+    lax.fori_loop(0, 4, norm_block, 0)
+    local(n1, n1_out, ls.at[10])
+    for i, d in enumerate(PLANE):
+        t = me.index(*d)
+        for n in (0, 1):
+            arrived(guf_ref.at[t, z, :, pl.ds(n * width, width)], ur.at[2 * i + n])
+    line_spread(me, sends, gu_part(z), gu_part, zg)
+    line_spread(me, sends, d_ref, d_part, zd)
+    line_finish(me, qkv_part, zq)
+    local(wf, wq_out, ls.at[11])
+
+    def qkv_block(b, carry):
+        w = wf[...].reshape(-1, wf.shape[3])
+        rows = mat(n1[b], w)
+        pre[b] = rows
+        cosine, sine = (cos_s[b], sin_s[b])
+        for h in range(3):
+            v = rows[:, head_dim * h : head_dim * (h + 1)]
+            n = v * head_scale(v) * hg_ref[pl.ds(h // 2, 1), :]
+            qkv[b, :, pl.ds(head_dim * h, head_dim)] = (n * cosine + turned(n) * sine).astype(jnp.bfloat16)
+        qkv[b, :, pl.ds(3 * head_dim, head_dim)] = rows[:, 3 * head_dim :].astype(jnp.bfloat16)
+        return carry
+
+    lax.fori_loop(0, 4, qkv_block, 0)
+    local(pre, pre_out, ls.at[12])
+    local(qkv, qkv_out, ls.at[13])
+    own_o.wait()
+    line_forward(me, sends, o_part, zo)
+    top = lambda r: jnp.max(jnp.abs(hg_ref[pl.ds(r, 1), :]), axis=1, keepdims=True)
+    bound = math.sqrt(head_dim) * top(0) * top(1)
+    scale = head_dim ** (-0.5)
+    for b in range(4):
+        for h in (0, 1):
+            qb = qkv[b, :, pl.ds(head_dim * h, head_dim)]
+            total, mixed = (None, None)
+            for kb in range(b + 1):
+                s = mat_right(qb, qkv[kb, :, pl.ds(2 * head_dim, head_dim)]) * scale
+                w = jnp.where(allowed_keys(segcol, segrow, b, kb), jnp.exp(s - bound), 0.0)
+                t = jnp.sum(w, axis=1, keepdims=True)
+                m = mat(w.astype(jnp.bfloat16), qkv[kb, :, pl.ds(3 * head_dim, head_dim)])
+                total = t if kb == 0 else total + t
+                mixed = m if kb == 0 else mixed + m
+            mixed = mixed / total
+            att[b, :, pl.ds(head_dim * h, head_dim)] = mixed
+            attlow[b, :, pl.ds(head_dim * h, head_dim)] = mixed.astype(jnp.bfloat16)
+        if b == 2:
+            permuted_in(me, cf_ref, pr.at[1])
+            spread_start(me, sends, me.shard(cf_ref), cf_ref, as_.at[1], ar.at[1])
+    local(att, att_out, ls.at[14])
+    line_finish(me, o_part, zo)
+    local(of, of_out, ls.at[15])
+    for b in range(4):
+        rows = mat(attlow[b], of[...].reshape(-1, of.shape[2])).astype(jnp.bfloat16)
+        part[b] = rows.reshape(part.shape[1:])
+        half_block(me, sends, part, sibling, hs, hr, b)
+    half_out(me, sends, part, sibling, out, came, hs, hr)
+    spread_forward(me, sends, cf_ref, as_.at[1], ar.at[1])
+    middle = xf[me.block, :, x].astype(jnp.float32) + half_in(me, part, sibling, came, hr)
     mid_ref[...] = middle
-    scale = lax.rsqrt(jnp.mean(middle * middle, axis=-1, keepdims=True) + EPSILON)
-    n_ref[...] = (middle * scale * gain_ref[...]).astype(jnp.bfloat16)
-    own_n = pltpu.make_async_copy(n_ref, me.shard(nf_ref), ls.at[1])
-    own_n.start()
-    spread_start(me, sends, n_ref, nf_ref, as_, ar)
-    spread_forward(me, sends, nf_ref, as_, ar)
-    spread_finish(me, nf_ref, ar)
+    n2[...] = (middle * head_scale(middle) * gain_two).astype(jnp.bfloat16)
+    own_n = local(n2, me.shard(nf_ref), ls.at[16])
+    spread_start(me, sends, n2, nf_ref, as_.at[2], ar.at[2])
+    line_forward(me, sends, gu_part, zg)
+    line_forward(me, sends, d_part, zd)
+    spread_forward(me, sends, nf_ref, as_.at[2], ar.at[2])
+    spread_finish(me, nf_ref, ar.at[2])
+    spread_finish(me, cf_ref, ar.at[1])
+    own_d.wait()
     own_n.wait()
+    line_finish(me, gu_part, zg)
+    line_finish(me, d_part, zd)
+    permute_in(me, x_ref, xf, ps.at[0], pr.at[0], wait=True)
+    permute_in(me, cot_ref, cf_ref, ps.at[1], pr.at[1], wait=True)
+    xs_copy.wait()
+    for src, dst, i in (
+        (segs, segf_ref, 6), (cos_s, cos_out, 7), (sin_s, sin_out, 8), (n1, n1_out, 10),
+        (wf, wq_out, 11), (pre, pre_out, 12), (qkv, qkv_out, 13), (att, att_out, 14), (of, of_out, 15),
+    ):
+        pltpu.make_async_copy(src, dst, ls.at[i]).wait()
     sends.drain()
 
 
-def middle_step(part, xf, gain):
-    tokens, width = (part.shape[0], part.shape[1])
+def forward_step(x, cot, seg, q, k, v, g, u, o, d, gain, head_gains):
+    tokens, width = (16 * x.shape[1], x.shape[2])
+    rows, low, wide = (q.shape[0], jnp.bfloat16, jnp.float32)
+    cols = (q.shape[1] + 2 * k.shape[1]) // 8
+    att_cols, head_dim = (q.shape[1] // 8, k.shape[1] // 8)
+    full = full_shape(tokens, width)
     piece = (4, tokens // 32, width)
+    quarter = tokens // 4
+    S = jax.ShapeDtypeStruct
     return pl.pallas_call(
-        middle_kernel,
-        name="middle_step",
+        forward_kernel,
+        name="forward_step",
         out_shape=(
-            jax.ShapeDtypeStruct(piece, jnp.float32),
-            jax.ShapeDtypeStruct(full_shape(tokens, width), jnp.bfloat16),
+            S(full, low), S(full, low), S((8, 4, rows, g.shape[1] // 4), low), S((4,) + d.shape, low),
+            S((2,) + seg.shape, seg.dtype), S((8, 4, rows, cols), low), S((4,) + o.shape, low),
+            S((4, quarter, width), low), S(piece, low), S((4, quarter, cols), wide),
+            S((4, quarter, cols), low), S((4, quarter, att_cols), wide),
+            S((4, quarter, head_dim), wide), S((4, quarter, head_dim), wide),
+            S(piece, wide), S((2, width), wide),
         ),
-        in_specs=[ANY, ANY, VMEM],
-        out_specs=(VMEM, ANY),
-        scratch_shapes=quarter_scratch(tokens, width)
-        + [pltpu.VMEM(piece, jnp.bfloat16)] * 2
-        + [SEM((7,)), SEM((7,)), SEM((2,))],
-        compiler_params=pltpu.CompilerParams(collective_id=1, has_side_effects=True),
-    )(part.reshape(full_shape(tokens, width)), xf, gain)
+        in_specs=[ANY] * 11 + [VMEM],
+        out_specs=(ANY,) * 14 + (VMEM,) * 2,
+        scratch_shapes=[
+            pltpu.VMEM(full, low), pltpu.VMEM((8, 4, rows, cols), low), pltpu.VMEM((4,) + o.shape, low),
+            pltpu.VMEM((2,) + seg.shape, seg.dtype), pltpu.VMEM((8, 4, 8, 128), wide),
+            pltpu.VMEM((4, quarter, width), low), pltpu.VMEM((4, quarter, cols), wide),
+            pltpu.VMEM((4, quarter, cols), low), pltpu.VMEM((4, quarter, 1), jnp.int32),
+            pltpu.VMEM((4, quarter, head_dim), wide), pltpu.VMEM((4, quarter, head_dim), wide),
+            pltpu.VMEM((4, quarter, att_cols), wide), pltpu.VMEM((4, quarter, att_cols), low),
+            pltpu.VMEM(full, low), pltpu.VMEM(piece, low),
+        ]
+        + half_scratch(tokens, width)
+        + [SEM((2, 4)), SEM((2, 4)), SEM((3, 7)), SEM((3, 7)), SEM((24,)), SEM((24,)), SEM((16,)), SEM((16,))]
+        + [SEM((11,)), SEM((11,))]
+        + [SEM((2, 5))] * 4
+        + [SEM((17,))],
+        compiler_params=pltpu.CompilerParams(
+            collective_id=0, has_side_effects=True, vmem_limit_bytes=60 * 1024 * 1024
+        ),
+    )(x, cot, seg, q, k, v, g, u, o, d, gain, head_gains)
 
 
 def norm_back(grad, vector, gain, scale):
@@ -782,7 +984,7 @@
         )
     own_w = pltpu.make_async_copy(dw_ref.at[:, z], wown, ls.at[2])
     own_w.start()
-    own_x = pltpu.make_async_copy(me.shard(xf_ref), xs_ref, ls.at[0])
+    own_x = pltpu.make_async_copy(xf_ref, xs_ref, ls.at[0])
     own_x.start()
     half_send(me, sends, kept, sibling, out, came, ks, ss, rs)
     half = y_ref.shape[1] // 2
@@ -909,34 +1111,6 @@
     )(part.reshape(full_shape(tokens, width)), xf, gmid, out, gain, small, dw, dgu)
 
 
-def rope_tables(segs, head_dim):
-    count = segs.shape[0]
-    doc_ids = jnp.arange(DOCS, dtype=jnp.int32)
-    starts = jnp.sum((segs[None, :] < doc_ids[:, None]).astype(jnp.int32), axis=1)
-    inverse = jnp.exp(
-        jnp.arange(head_dim // 2, dtype=jnp.float32) * (-2.0 * math.log(THETA) / head_dim)
-    )
-    inverse = jnp.concatenate([inverse, inverse])
-    low = jnp.arange(32, dtype=jnp.float32)[:, None] * inverse
-    high = jnp.arange(count // 32, dtype=jnp.float32)[:, None] * (32.0 * inverse)
-    first = starts.astype(jnp.float32)[:, None] * inverse
-    cl, sl, ch, sh, cf, sf = (
-        f(v) for v in (low, high, first) for f in (jnp.cos, jnp.sin)
-    )
-    cos_at = (ch[:, None] * cl - sh[:, None] * sl).reshape(count, head_dim)
-    sin_at = (sh[:, None] * cl + ch[:, None] * sl).reshape(count, head_dim)
-    chosen_cos = jnp.broadcast_to(cf[0], (count, head_dim))
-    chosen_sin = jnp.broadcast_to(sf[0], (count, head_dim))
-    for doc in range(1, DOCS):
-        here = (segs == doc)[:, None]
-        chosen_cos = jnp.where(here, cf[doc], chosen_cos)
-        chosen_sin = jnp.where(here, sf[doc], chosen_sin)
-    return (
-        cos_at * chosen_cos + sin_at * chosen_sin,
-        sin_at * chosen_cos - cos_at * chosen_sin,
-    )
-
-
 def dot(a, b, kind=jnp.float32):
     return jnp.dot(a, b, preferred_element_type=jnp.float32).astype(kind)
 
@@ -962,40 +1136,40 @@
     head_dim = head_gains.shape[1]
     z = lax.axis_index("uly")
     head = 4 * lax.axis_index("fsdp") + lax.axis_index("blk")
-    out_full = lax.all_gather(out_weight, "uly", axis=0, tiled=True)
-    down_full = lax.all_gather(down_weight, "uly", axis=0, tiled=True)
     piece = attn_gain.shape[0]
-    gains_own = jnp.zeros((8, 128), jnp.float32)
-    gains_own = gains_own.at[0, :piece].set(attn_gain.astype(jnp.float32))
-    gains_own = gains_own.at[1, :piece].set(ffn_gain.astype(jnp.float32))
-    xf, cf, segf, w_qkv, gu_part, gains = gather_all(
-        inputs, cotangent, segments, query_weight, key_matrix, value_matrix, gate_weight,
-        up_weight, gains_own,
-    )
-    gate_up = lax.all_gather(gu_part, "uly", axis=1, tiled=False)
-    gate_up = gate_up.reshape(width, gu_part.shape[2])
-    w_qkv = w_qkv.reshape(width, w_qkv.shape[3])
-    gain_one = gains[:, :, 0, :piece].reshape(1, width)
-    gain_two = gains[:, :, 1, :piece].reshape(1, width)
-    tokens = xf.shape[0] * xf.shape[1] * xf.shape[2] * xf.shape[3]
-    x_all = xf.reshape(tokens, width)
+    pair = jnp.stack([attn_gain, ffn_gain]).astype(jnp.float32)
+    spot = (jnp.arange(128, dtype=jnp.int32) // piece == z)[None]
+    gains_own = jnp.where(spot, jnp.tile(pair, (1, 128 // piece)), 0.0)
+    gains_own = jnp.concatenate([gains_own, jnp.zeros((6, 128), jnp.float32)], axis=0)
+    head_float = head_gains.astype(jnp.float32)
+    (
+        cf, nf, gate_up, down_full, segf, w_qkv, out_full, normed, xs, pre, qkv, attended, cosine,
+        sine, middle, gain_rows,
+    ) = forward_step(
+        inputs, cotangent, segments, query_weight, key_matrix, value_matrix, gate_weight, up_weight,
+        out_weight, down_weight, gains_own, head_float,
+    )
+    gain_one, gain_two = (gain_rows[0:1], gain_rows[1:2])
+    tokens = normed.shape[0] * normed.shape[1]
+    normed = normed.reshape(tokens, width)
+    w_qkv = w_qkv.reshape(width, -1)
+    out_full = out_full.reshape(-1, width)
+    down_full = down_full.reshape(-1, width)
+    gate_up = gate_up.reshape(width, -1)
     cot_all = cf.reshape(tokens, width)
     segs = lax.dynamic_index_in_dim(segf.reshape(-1, tokens), z, 0, keepdims=False)
-    normed = rms_norm(x_all.astype(jnp.float32), gain_one).astype(low)
-    pre = dot(normed, w_qkv).reshape(tokens, -1, head_dim)
-    groups = pre.shape[1] - 2
-    cosine, sine = rope_tables(segs, head_dim)
-    head_float = head_gains.astype(jnp.float32)
+    groups = query_weight.shape[1] // 8 // head_dim
+    pre = pre.reshape(tokens, -1, head_dim)
+    qkv = qkv.reshape(tokens, -1, head_dim)
+    query, key, value = (qkv[:, :groups], qkv[:, groups], qkv[:, groups + 1])
+    cosine, sine = (cosine.reshape(tokens, head_dim), sine.reshape(tokens, head_dim))
 
     def prepare_local(query_arg, key_arg, gains_arg):
         return prepare(query_arg[None], key_arg[None], gains_arg, cosine[None], sine[None])
 
-    (query_rot, key_rot), prep_pull = jax.vjp(
+    _, prep_pull = jax.vjp(
         prepare_local, pre[:, :groups], pre[:, groups : groups + 1], head_float
     )
-    query = query_rot[0].astype(low)
-    key = key_rot[0, :, 0].astype(low)
-    value = pre[:, groups + 1].astype(low)
     bound = math.sqrt(head_dim) * jnp.max(jnp.abs(head_float[0])) * jnp.max(jnp.abs(head_float[1]))
     scale = head_dim ** (-0.5)
     index = jnp.arange(tokens, dtype=jnp.int32)
@@ -1003,10 +1177,8 @@
     scores = jnp.einsum("qgd,kd->gqk", query, key, preferred_element_type=jnp.float32) * scale
     weights = jnp.where(allowed[None], jnp.exp(scores - bound), 0.0)
     totals = jnp.sum(weights, axis=-1)
-    mixed = jnp.einsum("gqk,kd->qgd", weights.astype(low), value, preferred_element_type=jnp.float32)
-    attended = mixed / jnp.transpose(totals)[..., None]
+    attended = attended.reshape(tokens, groups, head_dim)
     attended_low = attended.astype(low).reshape(tokens, groups * head_dim)
-    middle, nf = middle_step(dot(attended_low, out_full, low), xf, gain_two)
     normed_two = nf.reshape(tokens, width)
     hidden_width = gate_up.shape[1] // 2
     both = dot(normed_two, gate_up)
@@ -1063,7 +1235,7 @@
     )
     per_device = (inputs.shape, query_weight.shape[1], key_matrix.shape[1], gate_weight.shape[1])
     outputs, grad_inputs, q_grad, k_grad, v_grad, g_grad, u_grad, sums = last_step(
-        dot_right(grad_pre, w_qkv, low), xf, gmid, out_own, gain_one, small, dw, both_grad, per_device
+        dot_right(grad_pre, w_qkv, low), xs, gmid, out_own, gain_one, small, dw, both_grad, per_device
     )
     floats = lambda v: v.astype(jnp.float32)
     attn_gain_grad = lax.dynamic_slice(sums, (head, z * piece), (1, piece))[0]

time: 402 us -> 326 us (0.81)
  blocking collectives: 45.4 us -> 0 us
  waiting for transfers between devices: 46.5 us -> 26.8 us
  Pallas kernels: 177 us -> 193 us
  matrix products: 57.4 us -> 43 us
  other arithmetic: 34.3 us -> 20.7 us
    all_gather x2 -> x0, blocking collectives: 45.4 us -> none  [the longest x1 25.4 us: plane_body(): out_full = lax.all_gather(out_weight, 'uly', axis=0, tiled=True)]
    pallas_call x2 -> x1, Pallas kernels: 91.1 us -> 106 us  [forward_step(): pl.pallas_call(forward_kernel, name='forward_step', out_shape=(S(full, lo...]
    reduce_scatter x1, waiting for transfers between devices: 11 us -> 0.01 us  [plane_body(): lax.psum_scatter(dot_left(hidden, cot_all, low), 'uly', scatter_dimension...]
    reduce_scatter x1, waiting for transfers between devices: 35.4 us -> 26.8 us  [plane_body(): lax.psum_scatter(both_grad, 'uly', scatter_dimension=1, tiled=False)]
    slice x1 -> x6, local copies, waits for them, and re-layouts: 1.08 us -> 6.01 us  [the longest x2 3.12 us: plane_body(): query, key, value = (qkv[:, :groups], qkv[:, groups], qkv[:, groups + 1])]
    reshape x0 -> x4, local copies, waits for them, and re-layouts: none -> 4.1 us  [the longest x1 1.94 us: plane_body(): pre = pre.reshape(tokens, -1, head_dim)]
    dot_general x4 -> x2, matrix products: 10.1 us -> 6.68 us  [dot(): return jnp.dot(a, b, preferred_element_type=jnp.float32).astype(kind)]
  transfers between devices with their start and end apart: 4 -> 3, of which waited for: 2 -> 1; matrix products, arithmetic and copies ran while one was open for 17% -> 16% of each run, Pallas kernels for 9% -> 0%
where the time goes in v2:
time: 326 us; the launch traced here: 322 us
  Pallas kernels  193 us (59%)
  matrix products  43 us (13%)
  waiting for transfers between devices  26.8 us (8%)
  local copies, waits for them, and re-layouts  22.3 us (7%)
  other arithmetic  20.7 us (6%)
  between operations  16 us (5%)
    pallas_call x1, Pallas kernels, forward_step(): pl.pallas_call(forward_kernel, name='forward_step', out_shape=(S(full, lo...  106 us
    pallas_call x1, Pallas kernels, turn_step(): pl.pallas_call(turn_kernel, name='turn_step', out_shape=(jax.ShapeDtypeSt...  44.3 us
    pallas_call x1, Pallas kernels, last_step(): pl.pallas_call(last_kernel, name='last_step', out_shape=(back, back, *wei...  42.7 us
    reduce_scatter x1, waiting for transfers between devices, plane_body(): lax.psum_scatter(both_grad, 'uly', scatter_dimension=1, tiled=False)  26.8 us
    convert_element_type x7, other arithmetic, plane_body(): floats = lambda v: v.astype(jnp.float32)  11.5 us
    dot_general x4, matrix products, dot_left(): lax.dot_general(a, b, (((0,), (0,)), ((), ())), preferred_element_type=jn...  11.3 us
    dot_general x4, matrix products, dot_right(): lax.dot_general(a, b, (((1,), (1,)), ((), ())), preferred_element_type=jn...  10.4 us
    dot_general x2, matrix products, dot(): return jnp.dot(a, b, preferred_element_type=jnp.float32).astype(kind)  6.68 us
  transfers between devices with their start and end apart: 3, of which 1 were waited for; matrix products, arithmetic and copies ran while one was open for 16% of the time, Pallas kernels for 0%

profile of v2, /device:TPU:0, one launch (start us, length us, event | category | flops | bytes accessed | tf_op | source)
XLA Modules:
  0.0 322.5 jit_solution(11674819707521068083)
XLA Ops:
  9.8 106.4 %forward_step.1 = (bf16[4,4,2,32,1024]{4,3,2,1,0:T(8,128)(2,1)}, bf16[4,4,2,32,1024]{4,3,2,1,0:T(8,128)(2,1)}, bf16[8,4,32,768]{3,2,1,0:T(8,128)(2,1)}, bf16[4,9...) custom-call(bf16[2,64,1024]{2,1,0:T(8,128)(2,1)} %x_ref.1, ...), custom_call_target="tpu_custom_call" | custom-call | tf_op jit(solution)/shard_map/forward_step/pallas_call | solution.py:874
  118.9 4.1 %fusion.52 = f32[1024,768]{0,1:T(8,128)S(1)} fusion(bf16[1024,1024]{1,0:T(8,128)(2,1)} %bitcast.165, bf16[1024,768]{1,0:T(8,128)(2,1)} %bitcast.167), kind=kOutput, calls=%fused_computation.102 | convolution fusion | flops 1610612736 | bytes 6815744 | tf_op jit(solution)/shard_map/dot_general | solution.py:1115
  123.0 1.7 fusion.9
  124.7 2.6 convolution_convert_fusion
  127.4 3.2 convolution_convert_fusion.2
  130.6 44.3 %turn_step.1 = (f32[4,32,1024]{2,1,0:T(8,128)}, bf16[4,4,2,32,1024]{4,3,2,1,0:T(8,128)(2,1)}, bf16[4,32,1024]{2,1,0:T(8,128)(2,1)}, f32[1,1024]{1,0:T(1,128)}) custom-call(bf16[4,4,2,32,1024]{4,3,2,1,0:T(8,128)(2,1)} %bitcast.146, bf16[4,4,2,32,1024]{4,3,2,1,0:T(8,128)(2,1)} %bitcast.145, bf16[4,4,2,32,1024]{4,3,2,1,0:T(8,128)(2,1)} %get-tuple-element.42.cf_ref, ...), custom_call_target="tpu_custom_call" | custom-call | tf_op jit(solution)/shard_map/turn_step/pallas_call | solution.py:950
  174.9 3.3 %convolution_convert_fusion.6 = bf16[256,1024]{1,0:T(8,128)(2,1)} fusion(bf16[1024,256]{1,0:T(8,128)(2,1)S(1)} %bitcast.149, bf16[1024,1024]{1,0:T(8,128)(2,1)} %bitcast.147), kind=kOutput, calls=%fused_computation.30 | convolution fusion | flops 537133056 | bytes 3145728 | tf_op jit(solution)/shard_map/dot_general | solution.py:1119
  178.3 1.9 convolution_convert_fusion.5
  180.3 3.8 %convolution_convert_fusion.3 = bf16[1024,768]{1,0:T(8,128)(2,1)S(1)} fusion(bf16[1024,1024]{1,0:T(8,128)(2,1)} %bitcast.166, bf16[1024,384]{0,1:T(8,128)(2,1)} %copy-done.30, bf16[1024,384]{0,1:T(8,128)(2,1)} %copy-done.29), kind=kOutput, calls=%fused_computation.14 | convolution fusion | flops 1614544896 | bytes 5242880 | tf_op jit(solution)/shard_map/dot_general | solution.py:1119
  187.5 2.0 fusion.49
  190.0 1.9 reshape.343
  196.8 2.9 multiply_reduce_fusion.1
  199.8 2.6 fusion.3
  202.4 3.6 %fusion.1 = bf16[2,1024,1024]{1,2,0:T(8,128)(2,1)S(1)} fusion(f32[2,1024]{1,0:T(2,128)S(1)} %bitcast.175, bf16[1024,2,128]{0,2,1:T(8,128)(2,1)S(1)} %bitcast.173, f32[2,1024]{1,0:T(2,128)S(1)} %get-tuple-element.91, f32[]{:T(128)S(6)} %mul.243, f32[1024,1024,2]{1,0,2:T(8,128)S(1)} %get-tuple-element.92, pred[1024,1024]{0,1:T(8,128)(4,1)S(1)} %fusion.6, ...), kind=kOutput, calls=%fused_computation.2 | convolution fusion | flops 551550976 | bytes 14434308 | tf_op jit(solution)/shard_map/qgd,kd->gqk/dot_general | solution.py:1207
  206.0 2.3 fusion.22
  220.2 5.3 %fusion.18 = bf16[1024,128]{0,1:T(8,128)(2,1)S(1)} fusion(bf16[1024,2,128]{0,2,1:T(8,128)(2,1)S(1)} %bitcast.174, f32[1024,1024,2]{1,0,2:T(8,128)} %copy-done.28, f32[2,1024]{1,0:T(2,128)S(1)} %get-tuple-element.91, f32[]{:T(128)S(6)} %mul.243, pred[1024,1024]{0,1:T(8,128)(4,1)S(1)} %copy-done.12), kind=kOutput, calls=%fused_computation.35 | convolution fusion | flops 547487744 | bytes 10231812 | tf_op jit(solution)/shard_map/gqk,qgd->kd/dot_general | solution.py:1215
  225.6 2.6 convolution_convert_fusion.1
  228.2 2.3 convolution_convert_fusion.4
  230.5 1.7 convert_element_type.145
  232.2 1.7 convert_element_type.149
  233.9 26.8 %reduce-scatter.4.cloned.1.call-done = bf16[8,1,32,768]{3,2,0,1:T(8,128)(2,1)} async-done(((bf16[8,4,32,768]{3,2,0,1:T(8,128)(2,1)}), bf16[8,1,32,768]{3,2,0,1:T(8,128)(2,1)}) %reduce-scatter.4.cloned.1.call-update) | async-done | bytes 393232 | tf_op jit(solution)/shard_map/reduce_scatter | solution.py:1199
  260.7 42.7 %last_step.1 = (bf16[2,64,1024]{2,1,0:T(8,128)(2,1)}, bf16[2,64,1024]{2,1,0:T(8,128)(2,1)}, bf16[32,2048]{1,0:T(8,128)(2,1)}, bf16[32,1024]{1,0:T(8,128)(2,1)}, ...) custom-call(bf16[4,4,2,32,1024]{4,3,2,1,0:T(8,128)(2,1)} %bitcast.150, ...), custom_call_target="tpu_custom_call" | custom-call | tf_op jit(solution)/shard_map/last_step/pallas_call | solution.py:1091
  308.1 1.7 convert_element_type.146
  309.8 1.7 convert_element_type.147
  (122 shorter events, 33.3 us)
Async XLA Ops:
  7.2 223.4 %reduce-scatter.6.cloned.1.call-start = ((), (), s32[]{:S(2)}) async-start(), calls=%async_computation.4 | async-start | bytes 655360 | tf_op jit(solution)/shard_map/reduce_scatter | solution.py:1201
  118.9 4.1 %copy-start.6 = (bf16[4,4,2,32,1024]{4,3,2,1,0:T(8,128)(2,1)S(1)}, bf16[4,4,2,32,1024]{4,3,2,1,0:T(8,128)(2,1)}, u32[]{:S(2)}) copy-start(bf16[4,4,2,32,1024]{4,3,2,1,0:T(8,128)(2,1)} %get-tuple-element.42.cf_ref) | copy-start | bytes 6291460
  118.9 4.1 %copy-start.25 = (bf16[4,96,1024]{2,1,0:T(8,128)(2,1)S(1)}, bf16[4,96,1024]{2,1,0:T(8,128)(2,1)}, u32[]{:S(2)}) copy-start(bf16[4,96,1024]{2,1,0:T(8,128)(2,1)} %get-tuple-element.43) | copy-start | bytes 2359300
  124.7 2.7 copy-start.29
  124.7 2.6 copy-start.30
  124.7 2.6 copy-start.23
  174.9 3.4 %copy-start.7 = (bf16[4,4,2,32,1024]{4,3,2,1,0:T(8,128)(2,1)S(1)}, bf16[4,4,2,32,1024]{4,3,2,1,0:T(8,128)(2,1)}, u32[]{:S(2)}) copy-start(bf16[4,4,2,32,1024]{4,3,2,1,0:T(8,128)(2,1)} %get-tuple-element.42.cf_ref) | copy-start | bytes 6291460
  178.2 54.0 %reduce-scatter.8.cloned.1.call-start = ((), (), s32[]{:S(2)}) async-start(), calls=%async_computation.5 | async-start | bytes 983040 | tf_op jit(solution)/shard_map/reduce_scatter | solution.py:1195
  180.2 80.4 %reduce-scatter.4.cloned.1.call-start = ((), (), s32[]{:S(2)}) async-start(), calls=%async_computation.3 | async-start | bytes 1966080 | tf_op jit(solution)/shard_map/reduce_scatter | solution.py:1199
  186.4 3.1 copy-start.4
  192.0 2.9 copy-start
  195.5 6.8 %copy-start.11 = (pred[1024,1024]{0,1:T(8,128)(4,1)}, pred[1024,1024]{0,1:T(8,128)(4,1)S(1)}, u32[]{:S(2)}) copy-start(pred[1024,1024]{0,1:T(8,128)(4,1)S(1)} %fusion.6) | copy-start | bytes 3145732
  196.8 2.9 copy-start.9
  196.8 2.9 copy-start.10
  199.7 2.6 copy-start.26
  199.8 2.6 copy-start.16
  202.3 3.7 %copy-start.28 = (f32[1024,1024,2]{1,0,2:T(8,128)}, f32[1024,1024,2]{1,0,2:T(8,128)S(1)}, u32[]{:S(2)}) copy-start(f32[1024,1024,2]{1,0,2:T(8,128)S(1)} %get-tuple-element.92) | copy-start | bytes 25165828
  208.3 2.1 copy-start.14
  209.1 2.3 slice-start
  216.9 2.0 copy-start.8
  220.2 5.3 %copy-start.24 = (bf16[8,4,32,512]{3,2,1,0:T(8,128)(2,1)S(1)}, bf16[8,4,32,512]{3,2,1,0:T(8,128)(2,1)}, u32[]{:S(2)}) copy-start(bf16[8,4,32,512]{3,2,1,0:T(8,128)(2,1)} %get-tuple-element.54) | copy-start | bytes 3145732
  225.6 2.7 copy-start.22
  303.4 10.7 %copy-start.18 = (bf16[2,64,1024]{2,1,0:T(8,128)(2,1)S(1)}, bf16[2,64,1024]{2,1,0:T(8,128)(2,1)}, u32[]{:S(2)}) copy-start(bf16[2,64,1024]{2,1,0:T(8,128)(2,1)} %get-tuple-element.107) | copy-start | bytes 786436
  303.4 11.4 %copy-start.17 = (bf16[2,64,1024]{2,1,0:T(8,128)(2,1)S(1)}, bf16[2,64,1024]{2,1,0:T(8,128)(2,1)}, u32[]{:S(2)}) copy-start(bf16[2,64,1024]{2,1,0:T(8,128)(2,1)} %get-tuple-element.108) | copy-start | bytes 786436
  (11 other events, 15.3 us)
Sparse Core Ops, SparseCore 0:
  178.3 21.2 reduce-scatter.5
  201.9 21.4 reduce-scatter.7
  225.7 34.9 reduce-scatter.3

commit v3 on v0

--- a/solution.py
+++ b/solution.py
@@ -1,8 +1,11 @@
+import functools
 import math
 
 import jax
 import jax.numpy as jnp
 from jax import lax
+from jax.experimental import pallas as pl
+from jax.experimental.pallas import tpu as pltpu
 from jax.sharding import PartitionSpec as P
 
 DOCS = 4
@@ -381,9 +384,818 @@
     )
 
 
+MESH = pl.DeviceIdType.MESH
+ANY = pl.BlockSpec(memory_space=pl.ANY)
+VMEM = pl.BlockSpec(memory_space=pltpu.VMEM)
+PLANE = [(dx, dy, dc) for dx in (0, 1) for dy in (0, 1) for dc in (0, 1)]
+FAR = [(1, 1, 0), (1, 0, 0), (0, 1, 0)]
+TURNS = (1, 2, 3)
+SEM = pltpu.SemaphoreType.DMA
+
+
+class Place:
+    def __init__(self):
+        self.x = lax.axis_index("fsdp")
+        self.block = lax.axis_index("blk")
+        self.z = lax.axis_index("uly")
+        self.y, self.c = (self.block // 2, self.block % 2)
+        self.head = 4 * self.x + self.block
+        self.here = (self.x, self.block, self.z)
+
+    def coords(self, dx, dy, dc):
+        return ((self.x + dx) % 2, (self.y + dy) % 2, (self.c + dc) % 2)
+
+    def peer(self, dx, dy, dc):
+        x, y, c = self.coords(dx, dy, dc)
+        return (x, 2 * y + c, self.z)
+
+    def index(self, dx, dy, dc):
+        x, y, c = self.coords(dx, dy, dc)
+        return 4 * x + 2 * y + c
+
+    def shard(self, ref, dx=0, dy=0, dc=0):
+        x, y, c = self.coords(dx, dy, dc)
+        return ref.at[2 * y + c, :, x]
+
+    def behind(self, turn):
+        return (self.z + 4 - turn) % 4
+
+    def ahead(self, turn):
+        return (self.z + turn) % 4
+
+    def line(self, turn):
+        return (self.x, self.block, self.ahead(turn))
+
+
+def remote(src, dst, send_sem, recv_sem, device):
+    return pltpu.make_async_remote_copy(
+        src_ref=src,
+        dst_ref=dst,
+        send_sem=send_sem,
+        recv_sem=recv_sem,
+        device_id=device,
+        device_id_type=MESH,
+    )
+
+
+def arrived(ref, sem):
+    pltpu.make_async_copy(ref, ref, sem).wait()
+
+
+def meet(peers):
+    barrier = pltpu.get_barrier_semaphore()
+    for peer in peers:
+        pl.semaphore_signal(barrier, inc=1, device_id=peer, device_id_type=MESH)
+    pl.semaphore_wait(barrier, len(peers))
+
+
+class Sends:
+    def __init__(self):
+        self.pending = []
+
+    def go(self, *args):
+        copy = remote(*args)
+        copy.start()
+        self.pending.append((None, copy))
+
+    def go_if(self, condition, *args):
+        copy = remote(*args)
+        pl.when(condition)(lambda: copy.start())
+        self.pending.append((condition, copy))
+
+    def drain(self):
+        for condition, copy in self.pending:
+            if condition is None:
+                copy.wait_send()
+            else:
+                pl.when(condition)(lambda copy=copy: copy.wait_send())
+
+
+def spread_start(me, sends, src, full, send_sems, recv_sems):
+    for i, d in enumerate(FAR + [(0, 0, 1)]):
+        sends.go(src, me.shard(full), send_sems.at[i], recv_sems.at[i], me.peer(*d))
+
+
+def spread_forward(me, sends, full, send_sems, recv_sems):
+    for i in (1, 2, 0):
+        part = me.shard(full, *FAR[i])
+        arrived(part, recv_sems.at[i])
+        sends.go(part, part, send_sems.at[4 + i], recv_sems.at[4 + i], me.peer(0, 0, 1))
+
+
+def spread_finish(me, full, recv_sems):
+    for i, (dx, dy, _) in enumerate([(0, 0, 0)] + FAR):
+        arrived(me.shard(full, dx, dy, 1), recv_sems.at[3 + i])
+
+
+def full_shape(tokens, width):
+    return (4, 4, 2, tokens // 32, width)
+
+
+def line_spread(me, sends, src, part, sems):
+    for dz in (1, 2):
+        sends.go_if(me.z < 4 - dz, src, part(me.z), sems.at[0, dz - 1], sems.at[1, dz - 1], me.line(dz))
+        sends.go_if(me.z >= dz, src, part(me.z), sems.at[0, dz + 1], sems.at[1, dz + 1], me.line(4 - dz))
+
+
+def line_forward(me, sends, part, sems):
+    inner = jnp.logical_or(me.z == 1, me.z == 2)
+    ref = part((me.z + 2) % 4)
+    pl.when(me.z == 1)(lambda: arrived(ref, sems.at[1, 3]))
+    pl.when(me.z == 2)(lambda: arrived(ref, sems.at[1, 1]))
+    target = (me.x, me.block, (3 * me.z + 1) % 4)
+    sends.go_if(inner, ref, ref, sems.at[0, 4], sems.at[1, 4], target)
+
+
+def line_finish(me, part, sems):
+    z = me.z
+    pl.when(z > 0)(lambda: arrived(part((z + 3) % 4), sems.at[1, 0]))
+    pl.when(z < 3)(lambda: arrived(part((z + 1) % 4), sems.at[1, 2]))
+
+    @pl.when(z == 3)
+    def _():
+        arrived(part((z + 2) % 4), sems.at[1, 1])
+        arrived(part((z + 1) % 4), sems.at[1, 4])
+
+    @pl.when(z == 0)
+    def _():
+        arrived(part((z + 2) % 4), sems.at[1, 3])
+        arrived(part((z + 3) % 4), sems.at[1, 4])
+
+
+def line_to(me, z):
+    return (me.x, me.block, z)
+
+
+def outer_inner(me):
+    outer = jnp.logical_or(me.z == 0, me.z == 3)
+    return (outer, jnp.logical_not(outer))
+
+
+def reduce_start(me, sends, own, came, sems):
+    z = me.z
+    outer, _ = outer_inner(me)
+    sends.go_if(z < 3, own((z + 1) % 4), came.at[0], sems.at[0, 0], sems.at[1, 0], me.line(1))
+    sends.go_if(z > 0, own((z + 3) % 4), came.at[1], sems.at[0, 1], sems.at[1, 1], me.line(3))
+    nearer = line_to(me, 1 + z // 3)
+    sends.go_if(outer, own((7 - z) % 4), came.at[3], sems.at[0, 3], sems.at[1, 3], nearer)
+    far = (z + 2) % 4
+    sends.go_if(outer, own(far), came.at[2], sems.at[0, 2], sems.at[1, 2], line_to(me, far))
+
+
+def reduce_join(me, sends, own, came, buf, sems):
+    _, inner = outer_inner(me)
+    far = (me.z + 2) % 4
+
+    @pl.when(inner)
+    def _():
+        arrived(came.at[3], sems.at[1, 3])
+        buf[...] = (own(far)[...].astype(jnp.float32) + came[3].astype(jnp.float32)).astype(buf.dtype)
+
+    sends.go_if(inner, buf, came.at[2], sems.at[0, 2], sems.at[1, 2], line_to(me, far))
+
+
+def reduce_total(me, own, came, total, sems):
+    arrived(came.at[2], sems.at[1, 2])
+    total[...] = own(me.z)[...].astype(jnp.float32) + came[2].astype(jnp.float32)
+
+    @pl.when(me.z > 0)
+    def _():
+        arrived(came.at[0], sems.at[1, 0])
+        total[...] = total[...] + came[0].astype(jnp.float32)
+
+    @pl.when(me.z < 3)
+    def _():
+        arrived(came.at[1], sems.at[1, 1])
+        total[...] = total[...] + came[1].astype(jnp.float32)
+
+
+def lanes(shape):
+    return lax.broadcasted_iota(jnp.int32, shape, len(shape) - 1)
+
+
+def turned(vector):
+    half = vector.shape[-1] // 2
+    sign = jnp.where(lanes((1, 2 * half)) < half, -1.0, 1.0)
+    return pltpu.roll(vector, half, 1) * sign
+
+
+def head_scale(vector):
+    return lax.rsqrt(jnp.mean(vector * vector, axis=-1, keepdims=True) + EPSILON)
+
+
+def mat(a, b):
+    return jnp.dot(a, b, preferred_element_type=jnp.float32)
+
+
+def mat_right(a, b):
+    return lax.dot_general(a, b, (((1,), (1,)), ((), ())), preferred_element_type=jnp.float32)
+
+
+def mat_left(a, b):
+    return lax.dot_general(a, b, (((0,), (0,)), ((), ())), preferred_element_type=jnp.float32)
+
+
+def permute_in(me, src_ref, full_ref, send_sems, recv_sems, wait=False):
+    half = src_ref.shape[1] // 2
+    for j in (0, 1):
+        for to in (0, 1):
+            src = src_ref.at[j, pl.ds(half * to, half)]
+            dst = full_ref.at[me.block, me.z, to]
+            mine = jnp.logical_and(me.x == to, me.z == 2 * me.x + j)
+            copy = remote(
+                src, dst, send_sems.at[2 * j + to], recv_sems.at[me.z], (to, me.block, 2 * me.x + j)
+            )
+            if wait:
+                pl.when(jnp.logical_not(mine))(lambda copy=copy: copy.wait_send())
+                continue
+            pl.when(jnp.logical_not(mine))(lambda copy=copy: copy.start())
+            own = pltpu.make_async_copy(src, dst, recv_sems.at[me.z])
+            pl.when(mine)(lambda own=own: own.start())
+
+
+def permuted_in(me, full_ref, recv_sems):
+    for k in range(4):
+        arrived(full_ref.at[me.block, k, me.x], recv_sems.at[k])
+
+
+def half_block(me, part, sibling, send_sems, recv_sems, b, sends=None):
+    other = me.c != b % 2
+    dy = (me.y + b // 2) % 2
+    for to in (0, 1):
+        slot = 3 - 2 * ((me.x + to) % 2) - dy
+        copy = remote(
+            part.at[b, :, to], sibling.at[slot], send_sems.at[slot], recv_sems.at[slot],
+            me.peer(0, 0, 1),
+        )
+        if sends is None:
+            pl.when(other)(lambda copy=copy: copy.start())
+        else:
+            sends.pending.append((other, copy))
+
+
+def half_out(me, sends, part, sibling, out, came, send_sems, recv_sems):
+    for i, d in enumerate(FAR):
+        x, y, c = me.coords(*d)
+        arrived(sibling.at[i], recv_sems.at[i])
+        own = part[2 * y + c, :, x].astype(jnp.float32)
+        out[i] = (own + sibling[i].astype(jnp.float32)).astype(jnp.bfloat16)
+        sends.go(out.at[i], came.at[i], send_sems.at[4 + i], recv_sems.at[4 + i], me.peer(*d))
+
+
+def half_in(me, part, sibling, came, recv_sems):
+    arrived(sibling.at[3], recv_sems.at[3])
+    total = part[me.block, :, me.x].astype(jnp.float32) + sibling[3].astype(jnp.float32)
+    for i in (1, 2, 0):
+        arrived(came.at[i], recv_sems.at[4 + i])
+        total = total + came[i].astype(jnp.float32)
+    return total
+
+
+def half_scratch(tokens, width):
+    piece = (4, tokens // 32, width)
+    return [
+        pltpu.VMEM((4,) + piece, jnp.bfloat16),
+        pltpu.VMEM((3,) + piece, jnp.bfloat16),
+        pltpu.VMEM((3,) + piece, jnp.bfloat16),
+        SEM((7,)),
+        SEM((7,)),
+    ]
+
+
+def gain_row(gains_ref, kind):
+    rows = [jnp.sum(gains_ref[p, :, kind, :], axis=0, keepdims=True) for p in range(8)]
+    return jnp.concatenate(rows, axis=1)
+
+
+def allowed_keys(segcol, segrow, b, kb):
+    same = segcol[b] == segrow[:, 256 * kb : 256 * kb + 256]
+    if kb < b:
+        return same
+    rows = lax.broadcasted_iota(jnp.int32, (256, 256), 0)
+    return jnp.logical_and(same, lanes((256, 256)) <= rows)
+
+
+def norm_back(grad, vector, gain, scale):
+    weighted = grad * gain
+    inner = jnp.mean(weighted * vector, axis=-1, keepdims=True)
+    return scale * weighted - vector * (scale * scale * scale * inner)
+
+
+def permute_out(me, src_ref, dst_ref, send_sems, recv_sems, wait=False):
+    half = dst_ref.shape[1] // 2
+    for k in range(4):
+        src = src_ref.at[k]
+        dst = dst_ref.at[me.z % 2, pl.ds(half * me.x, half)]
+        mine = jnp.logical_and(me.x == me.z // 2, me.z == k)
+        spot = 2 * (me.z % 2) + me.x
+        copy = remote(src, dst, send_sems.at[k], recv_sems.at[spot], (me.z // 2, me.block, k))
+        if wait:
+            pl.when(jnp.logical_not(mine))(lambda copy=copy: copy.wait_send())
+            continue
+        pl.when(jnp.logical_not(mine))(lambda copy=copy: copy.start())
+        own = pltpu.make_async_copy(src, dst, recv_sems.at[spot])
+        pl.when(mine)(lambda own=own: own.start())
+
+
+def permuted_out(dst_ref, recv_sems):
+    half = dst_ref.shape[1] // 2
+    for j in (0, 1):
+        for to in (0, 1):
+            arrived(dst_ref.at[j, pl.ds(half * to, half)], recv_sems.at[2 * j + to])
+
+
+def total_row(share):
+    return jnp.sum(jnp.sum(share, axis=0), axis=0, keepdims=True)
+
+
+def layer_kernel(
+    x_ref, cot_ref, seg_ref, q_ref, k_ref, v_ref, g_ref, u_ref, o_ref, d_ref, gain_ref, hg_ref,
+    y_ref, gx_ref, dq_ref, dk_ref, dv_ref, dg_ref, du_ref, sums_ref, osum_ref, dsum_ref,
+    xf, cf, wf, of, df, guf, segs, gains, n1, nf, gf, pre, qkv, segcol, cos_s, sin_s, att, attlow,
+    totals, part, part2, part3, down, n2, gm, y_s, gi_s, mid, gmid,
+    hid, gboth, ga, gq, gk, gv, gpre, dd, dgu, do, dw,
+    d_came, d_buf, gu_came, gu_buf, gu_total, gu_sum, o_came, o_buf, w_came, w_buf, w_total, w_sum,
+    pack, packs, linep,
+    sib1, out1, came1, hs1, hr1, sib2, out2, came2, hs2, hr2, sib3, out3, came3, hs3, hr3,
+    sib4, out4, came4, hs4, hr4,
+    ps, pr, as_, ar, ws, wr, us, ur, gs, gr, zq, zo, zd, zg, rg, rd, ro, rw, cs, cr, ds, dr, ls,
+):
+    me = Place()
+    x, z, p = (me.x, me.z, me.head)
+    low, wide_t = (jnp.bfloat16, jnp.float32)
+    across = [((x + 1) % 2, me.block, me.ahead(turn)) for turn in TURNS]
+    meet([me.peer(*d) for d in PLANE[1:]] + [me.line(turn) for turn in TURNS] + across)
+    sends = Sends()
+
+    def local(src, dst, sem):
+        copy = pltpu.make_async_copy(src, dst, sem)
+        copy.start()
+        return copy
+
+    own_gain = local(gain_ref, gains.at[p, z], ls.at[0])
+    own_seg = local(seg_ref, segs.at[x], ls.at[1])
+    sends.go(seg_ref, segs.at[x], ls.at[2], ls.at[3], me.peer(1, 0, 0))
+    for turn in TURNS:
+        sends.go(gain_ref, gains.at[p, z], gs.at[turn], gr.at[turn], me.line(turn))
+    permute_in(me, x_ref, xf, ps.at[0], pr.at[0])
+    own_o = local(o_ref, of.at[z], ls.at[4])
+    own_d = local(d_ref, df.at[z], ls.at[5])
+    wide, narrow = (q_ref.shape[1] // 8, k_ref.shape[1] // 8)
+    cuts = ((q_ref, wide, 0), (k_ref, narrow, wide), (v_ref, narrow, wide + narrow))
+    for i, d in enumerate(PLANE):
+        t = me.index(*d)
+        for n, (ref, width, off) in enumerate(cuts):
+            src = ref.at[:, pl.ds(pl.multiple_of(t * width, 128), width)]
+            dst = wf.at[p, z, :, pl.ds(off, width)]
+            if i == 0:
+                local(src, dst, wr.at[n])
+            else:
+                sends.go(src, dst, ws.at[3 * i + n], wr.at[3 * i + n], me.peer(*d))
+    permuted_in(me, xf, pr.at[0])
+    spread_start(me, sends, me.shard(xf), xf, as_.at[0], ar.at[0])
+    for i, d in enumerate(PLANE):
+        t = me.index(*d)
+        for n, (ref, width, off) in enumerate(cuts):
+            arrived(wf.at[t, z, :, pl.ds(off, width)], wr.at[3 * i + n])
+    qkv_part = lambda k: wf.at[:, k]
+    o_part = lambda k: of.at[k]
+    d_part = lambda k: df.at[k]
+    gu_part = lambda k: guf.at[:, k]
+    line_spread(me, sends, qkv_part(z), qkv_part, zq)
+    permute_in(me, cot_ref, cf, ps.at[1], pr.at[1])
+    line_spread(me, sends, o_ref, o_part, zo)
+    ff = g_ref.shape[1] // 8
+    for i, d in enumerate(PLANE):
+        t = me.index(*d)
+        for n, ref in enumerate((g_ref, u_ref)):
+            src = ref.at[:, pl.ds(pl.multiple_of(t * ff, 128), ff)]
+            dst = guf.at[p, z, :, pl.ds(n * ff, ff)]
+            if i == 0:
+                local(src, dst, ur.at[n])
+            else:
+                sends.go(src, dst, us.at[2 * i + n], ur.at[2 * i + n], me.peer(*d))
+    own_gain.wait()
+    for turn in TURNS:
+        arrived(gains.at[p, me.behind(turn)], gr.at[turn])
+    for i, d in enumerate(PLANE[1:]):
+        sends.go(gains.at[p], gains.at[p], gs.at[4 + i], gr.at[4 + i], me.peer(*d))
+    own_seg.wait()
+    arrived(segs.at[(x + 1) % 2], ls.at[3])
+    head_dim = hg_ref.shape[1]
+    segrow = segs[z // 2, pl.ds(z % 2, 1), :]
+    tokens = segrow.shape[1]
+    column = jnp.transpose(jnp.broadcast_to(segrow.astype(wide_t), (8, tokens)))[:, :1]
+    segcol[...] = column.astype(jnp.int32).reshape(4, 256, 1)
+    half_lane = (lanes((1, head_dim)) % (head_dim // 2)).astype(wide_t)
+    inverse = jnp.exp(half_lane * (-2.0 * math.log(THETA) / head_dim))
+    steps = lax.broadcasted_iota(jnp.int32, (32, head_dim), 0).astype(wide_t) * inverse
+    cl, sl = (jnp.cos(steps), jnp.sin(steps))
+    ch, sh = (jnp.cos(steps * 32.0), jnp.sin(steps * 32.0))
+    doc_cos, doc_sin = ([], [])
+    for doc in range(DOCS):
+        start = jnp.sum((segrow < doc).astype(wide_t), axis=1, keepdims=True)
+        doc_cos.append(jnp.cos(start * inverse))
+        doc_sin.append(jnp.sin(start * inverse))
+    for b in range(4):
+        hi_c, hi_s = (ch[8 * b : 8 * b + 8][:, None, :], sh[8 * b : 8 * b + 8][:, None, :])
+        cos_at = (hi_c * cl[None] - hi_s * sl[None]).reshape(256, head_dim)
+        sin_at = (hi_s * cl[None] + hi_c * sl[None]).reshape(256, head_dim)
+        column = segcol[b]
+        cd, sd = (jnp.broadcast_to(v[0], (256, head_dim)) for v in (doc_cos, doc_sin))
+        for doc in range(1, DOCS):
+            cd = jnp.where(column == doc, doc_cos[doc], cd)
+            sd = jnp.where(column == doc, doc_sin[doc], sd)
+        cos_s[b] = cos_at * cd + sin_at * sd
+        sin_s[b] = sin_at * cd - cos_at * sd
+    for i, d in enumerate(PLANE[1:]):
+        arrived(gains.at[me.index(*d)], gr.at[4 + i])
+    gain_one, gain_two = (gain_row(gains, 0), gain_row(gains, 1))
+    line_forward(me, sends, qkv_part, zq)
+    spread_forward(me, sends, xf, as_.at[0], ar.at[0])
+    spread_finish(me, xf, ar.at[0])
+
+    @pl.loop(0, 4)
+    def _(b):
+        rows = xf[b].reshape(256, -1).astype(wide_t)
+        n1[b] = (rows * head_scale(rows) * gain_one).astype(low)
+
+    for i, d in enumerate(PLANE):
+        t = me.index(*d)
+        for n in (0, 1):
+            arrived(guf.at[t, z, :, pl.ds(n * ff, ff)], ur.at[2 * i + n])
+    line_spread(me, sends, gu_part(z), gu_part, zg)
+    line_spread(me, sends, d_ref, d_part, zd)
+    line_finish(me, qkv_part, zq)
+
+    @pl.loop(0, 4)
+    def _(b):
+        rows = mat(n1[b], wf[...].reshape(-1, wf.shape[3]))
+        pre[b] = rows
+        cosine, sine = (cos_s[b], sin_s[b])
+        for h in range(3):
+            v = rows[:, head_dim * h : head_dim * (h + 1)]
+            n = v * head_scale(v) * hg_ref[pl.ds(h // 2, 1), :]
+            qkv[b, :, pl.ds(head_dim * h, head_dim)] = (n * cosine + turned(n) * sine).astype(low)
+        qkv[b, :, pl.ds(3 * head_dim, head_dim)] = rows[:, 3 * head_dim :].astype(low)
+
+    own_o.wait()
+    line_forward(me, sends, o_part, zo)
+    top = lambda r: jnp.max(jnp.abs(hg_ref[pl.ds(r, 1), :]), axis=1, keepdims=True)
+    bound = math.sqrt(head_dim) * top(0) * top(1)
+    scale = head_dim ** (-0.5)
+    key_at, value_at = (pl.ds(2 * head_dim, head_dim), pl.ds(3 * head_dim, head_dim))
+
+    def weights_of(b, kb, query):
+        s = mat_right(query, qkv[kb, :, key_at]) * scale
+        return jnp.where(allowed_keys(segcol, segrow, b, kb), jnp.exp(s - bound), 0.0)
+
+    for b in range(4):
+
+        @pl.loop(0, 2)
+        def _(h, b=b):
+            at = pl.ds(pl.multiple_of(head_dim * h, head_dim), head_dim)
+            query = qkv[b, :, at]
+            total, mixed = (None, None)
+            for kb in range(b + 1):
+                w = weights_of(b, kb, query)
+                t = jnp.sum(w, axis=1, keepdims=True)
+                m = mat(w.astype(low), qkv[kb, :, value_at])
+                total = t if kb == 0 else total + t
+                mixed = m if kb == 0 else mixed + m
+            mixed = mixed / total
+            totals[b, h] = total
+            att[b, :, at] = mixed
+            attlow[b, :, at] = mixed.astype(low)
+
+        if b == 2:
+            permuted_in(me, cf, pr.at[1])
+            spread_start(me, sends, me.shard(cf), cf, as_.at[1], ar.at[1])
+    line_finish(me, o_part, zo)
+
+    @pl.loop(0, 4)
+    def _(b):
+        rows = mat(attlow[b], of[...].reshape(-1, of.shape[2])).astype(low)
+        part[b] = rows.reshape(part.shape[1:])
+        half_block(me, part, sib1, hs1, hr1, b)
+
+    for b in range(4):
+        half_block(me, part, sib1, hs1, hr1, b, sends)
+    half_out(me, sends, part, sib1, out1, came1, hs1, hr1)
+    spread_forward(me, sends, cf, as_.at[1], ar.at[1])
+    middle = xf[me.block, :, x].astype(wide_t) + half_in(me, part, sib1, came1, hr1)
+    mid[...] = middle
+    n2[...] = (middle * head_scale(middle) * gain_two).astype(low)
+    own_n = local(n2, me.shard(nf), ls.at[6])
+    spread_start(me, sends, n2, nf, as_.at[2], ar.at[2])
+    line_forward(me, sends, gu_part, zg)
+    line_forward(me, sends, d_part, zd)
+    spread_forward(me, sends, nf, as_.at[2], ar.at[2])
+    spread_finish(me, nf, ar.at[2])
+    own_n.wait()
+    spread_finish(me, cf, ar.at[1])
+    own_d.wait()
+    line_finish(me, gu_part, zg)
+    line_finish(me, d_part, zd)
+
+    @pl.loop(0, 4)
+    def _(b):
+        both = mat(nf[b].reshape(256, -1), guf[...].reshape(-1, 2 * ff))
+        gate, up = (both[:, :ff], both[:, ff:])
+        sig = 1.0 / (1.0 + jnp.exp(-gate))
+        silu = gate * sig
+        hidden = (silu * up).astype(low)
+        hid[b] = hidden
+        w_down = df[...].reshape(ff, -1)
+        grad = mat_right(cf[b].reshape(256, -1), w_down)
+        gboth[b, :, pl.ds(0, ff)] = (grad * up * sig * (1.0 + gate * (1.0 - sig))).astype(low)
+        gboth[b, :, pl.ds(ff, ff)] = (grad * silu).astype(low)
+        rows = mat_right(gboth[b], guf[...].reshape(-1, 2 * ff)).astype(low)
+        part2[b] = rows.reshape(part2.shape[1:])
+        half_block(me, part2, sib2, hs2, hr2, b)
+
+    for b in range(4):
+        half_block(me, part2, sib2, hs2, hr2, b, sends)
+    half_out(me, sends, part2, sib2, out2, came2, hs2, hr2)
+
+    @pl.loop(0, 4)
+    def _(b):
+        rows = nf[:, :, :, :, pl.ds(pl.multiple_of(256 * b, 256), 256)].reshape(-1, 256)
+        grad = mat_left(rows, gboth[...].reshape(-1, 2 * ff)).astype(low)
+        dgu[pl.ds(2 * b, 2)] = grad.reshape((2,) + dgu.shape[1:])
+
+    own_gu = lambda k: dgu.at[:, k]
+    reduce_start(me, sends, own_gu, gu_came, rg)
+    grad = half_in(me, part2, sib2, came2, hr2)
+    middle = mid[...]
+    r = head_scale(middle)
+    total = cf[me.block, :, x].astype(wide_t) + norm_back(grad, middle, gain_two, r)
+    gmid[...] = total
+    gm[...] = total.astype(low)
+    own_gm = local(gm, me.shard(gf), ls.at[7])
+    spread_start(me, sends, gm, gf, as_.at[3], ar.at[3])
+    share = total_row(grad * middle * r)
+    for i in range(8):
+        pack[pl.ds(8 + i, 1)] = share[:, 128 * i : 128 * i + 128]
+
+    @pl.loop(0, 4)
+    def _(b):
+        rows = mat(hid[b], df[...].reshape(ff, -1)).astype(low)
+        down[b] = rows.reshape(down.shape[1:])
+        half_block(me, down, sib3, hs3, hr3, b)
+
+    for b in range(4):
+        half_block(me, down, sib3, hs3, hr3, b, sends)
+    dd[...] = mat_left(hid[...].reshape(-1, ff), cf[...].reshape(tokens, -1)).astype(low).reshape(dd.shape)
+    own_dd = lambda k: dd.at[k]
+    reduce_start(me, sends, own_dd, d_came, rd)
+    half_out(me, sends, down, sib3, out3, came3, hs3, hr3)
+    reduce_join(me, sends, own_gu, gu_came, gu_buf, rg)
+    spread_forward(me, sends, gf, as_.at[3], ar.at[3])
+    spread_finish(me, gf, ar.at[3])
+    own_gm.wait()
+
+    gk[...] = jnp.zeros_like(gk)
+    gv[...] = jnp.zeros_like(gv)
+    for b in range(4):
+        ga[b] = mat_right(gf[b].reshape(256, -1), of[...].reshape(-1, of.shape[2])).astype(low)
+
+        @pl.loop(0, 2)
+        def _(h, b=b):
+            at = pl.ds(pl.multiple_of(head_dim * h, head_dim), head_dim)
+            query, grad = (qkv[b, :, at], ga[b, :, at])
+            delta = jnp.sum(grad.astype(wide_t) * att[b, :, at], axis=1, keepdims=True)
+            inv = 1.0 / totals[b, h]
+            grad_query = None
+            for kb in range(b + 1):
+                probs = weights_of(b, kb, query) * inv
+                gp = mat_right(grad, qkv[kb, :, value_at])
+                gsc = (probs * (gp - delta)).astype(low)
+                m = mat(gsc, qkv[kb, :, key_at])
+                grad_query = m if kb == 0 else grad_query + m
+                gk[kb] += mat_left(gsc, query)
+                gv[kb] += mat_left(probs.astype(low), grad)
+            gq[b, :, at] = grad_query
+
+        if b == 0:
+            reduce_join(me, sends, own_dd, d_came, d_buf, rd)
+        if b == 1:
+            y_s[...] = (mid[...] + half_in(me, down, sib3, came3, hr3)).astype(low)
+            permute_out(me, y_s, y_ref, cs.at[0], cr.at[0])
+    do[...] = mat_left(attlow[...].reshape(tokens, -1), gf[...].reshape(tokens, -1)).astype(low).reshape(do.shape)
+    own_do = lambda k: do.at[k]
+    reduce_start(me, sends, own_do, o_came, ro)
+    pack[pl.ds(16, 8)] = jnp.zeros((8, 128), wide_t)
+
+    @pl.loop(0, 4)
+    def _(b):
+        cosine, sine = (cos_s[b], sin_s[b])
+        for h in range(3):
+            at = pl.ds(head_dim * h, head_dim)
+            source = gq[b, :, at] if h < 2 else gk[b]
+            go = (source * scale).astype(low).astype(wide_t)
+            gh = go * cosine - turned(go * sine)
+            v = pre[b, :, at]
+            r = head_scale(v)
+            n = v * r
+            pack[pl.ds(16 + h // 2, 1)] += jnp.sum(gh * n, axis=0, keepdims=True)
+            gn = gh * hg_ref[pl.ds(h // 2, 1), :]
+            gpre[b, :, at] = (r * (gn - n * jnp.mean(gn * n, axis=-1, keepdims=True))).astype(low)
+        gpre[b, :, value_at] = gv[b].astype(low)
+        rows = mat_right(gpre[b], wf[...].reshape(-1, wf.shape[3])).astype(low)
+        part3[b] = rows.reshape(part3.shape[1:])
+        half_block(me, part3, sib4, hs4, hr4, b)
+
+    for b in range(4):
+        half_block(me, part3, sib4, hs4, hr4, b, sends)
+    half_out(me, sends, part3, sib4, out4, came4, hs4, hr4)
+
+    @pl.loop(0, 4)
+    def _(b):
+        rows = n1[:, :, pl.ds(pl.multiple_of(256 * b, 256), 256)].reshape(-1, 256)
+        grad = mat_left(rows, gpre[...].reshape(tokens, -1)).astype(low)
+        dw[pl.ds(2 * b, 2)] = grad.reshape((2,) + dw.shape[1:])
+
+    own_dw = lambda k: dw.at[:, k]
+    reduce_start(me, sends, own_dw, w_came, rw)
+    reduce_join(me, sends, own_do, o_came, o_buf, ro)
+    reduce_total(me, own_gu, gu_came, gu_total, rg)
+    gu_sum[...] = gu_total[...].astype(low)
+    for i, d in enumerate(PLANE):
+        t = me.index(*d)
+        for n, ref in enumerate((dg_ref, du_ref)):
+            src = gu_sum.at[t, :, pl.ds(n * ff, ff)]
+            dst = ref.at[:, pl.ds(pl.multiple_of(p * ff, 128), ff)]
+            if i == 0:
+                local(src, dst, dr.at[n])
+            else:
+                sends.go(src, dst, ds.at[2 * i + n], dr.at[2 * i + n], me.peer(*d))
+    reduce_total(me, own_dd, d_came, dsum_ref, rd)
+    grad = half_in(me, part3, sib4, came4, hr4)
+    rows = xf[me.block, :, x].astype(wide_t)
+    r = head_scale(rows)
+    gi_s[...] = (gmid[...] + norm_back(grad, rows, gain_one, r)).astype(low)
+    permute_out(me, gi_s, gx_ref, cs.at[1], cr.at[1])
+    share = total_row(grad * rows * r)
+    for i in range(8):
+        pack[pl.ds(i, 1)] = share[:, 128 * i : 128 * i + 128]
+    for i, d in enumerate(PLANE[1:]):
+        sends.go(pack, packs.at[i], gs.at[11 + i], gr.at[11 + i], me.peer(*d))
+    reduce_join(me, sends, own_dw, w_came, w_buf, rw)
+    reduce_total(me, own_do, o_came, osum_ref, ro)
+    total = pack[...]
+    for i in range(7):
+        arrived(packs.at[i], gr.at[11 + i])
+        total = total + packs[i]
+    packs[7] = total
+    for turn in TURNS:
+        sends.go(packs.at[7], linep.at[turn - 1], gs.at[17 + turn], gr.at[17 + turn], me.line(turn))
+    reduce_total(me, own_dw, w_came, w_total, rw)
+    w_sum[...] = w_total[...].astype(low)
+    backs = ((dq_ref, wide, 0), (dk_ref, narrow, wide), (dv_ref, narrow, wide + narrow))
+    for i, d in enumerate(PLANE):
+        t = me.index(*d)
+        for n, (ref, cols, off) in enumerate(backs):
+            src = w_sum.at[t, :, pl.ds(off, cols)]
+            dst = ref.at[:, pl.ds(pl.multiple_of(p * cols, 128), cols)]
+            if i == 0:
+                local(src, dst, dr.at[16 + n])
+            else:
+                s = 16 + 3 * i + n
+                sends.go(src, dst, ds.at[s], dr.at[s], me.peer(*d))
+    for turn in TURNS:
+        arrived(linep.at[turn - 1], gr.at[17 + turn])
+    sums_ref[...] = ((total + linep[0]) + linep[1]) + linep[2]
+    for i, d in enumerate(PLANE):
+        t = me.index(*d)
+        for n, ref in enumerate((dg_ref, du_ref)):
+            arrived(ref.at[:, pl.ds(pl.multiple_of(t * ff, 128), ff)], dr.at[2 * i + n])
+        for n, (ref, cols, off) in enumerate(backs):
+            arrived(ref.at[:, pl.ds(pl.multiple_of(t * cols, 128), cols)], dr.at[16 + 3 * i + n])
+    permuted_out(y_ref, cr.at[0])
+    permuted_out(gx_ref, cr.at[1])
+    permute_in(me, x_ref, xf, ps.at[0], pr.at[0], wait=True)
+    permute_in(me, cot_ref, cf, ps.at[1], pr.at[1], wait=True)
+    permute_out(me, y_s, y_ref, cs.at[0], cr.at[0], wait=True)
+    permute_out(me, gi_s, gx_ref, cs.at[1], cr.at[1], wait=True)
+    sends.drain()
+
+
+def layer_step(x, cot, seg, q, k, v, g, u, o, d, gain, head_gains):
+    tokens, width = (16 * x.shape[1], x.shape[2])
+    rows, low, wide = (q.shape[0], jnp.bfloat16, jnp.float32)
+    cols = (q.shape[1] + 2 * k.shape[1]) // 8
+    att_cols, head_dim = (q.shape[1] // 8, k.shape[1] // 8)
+    ff = g.shape[1] // 8
+    full = full_shape(tokens, width)
+    piece = (4, tokens // 32, width)
+    quarter = tokens // 4
+    shape, buf = (jax.ShapeDtypeStruct, pltpu.VMEM)
+    blocks = lambda n, kind: buf((4, quarter, n), kind)
+    return pl.pallas_call(
+        layer_kernel,
+        name="layer_step",
+        out_shape=(
+            shape(x.shape, low), shape(x.shape, low), shape(q.shape, low), shape(k.shape, low),
+            shape(v.shape, low), shape(g.shape, low), shape(u.shape, low), shape((24, 128), wide),
+            shape(o.shape, wide), shape(d.shape, wide),
+        ),
+        in_specs=[ANY] * 11 + [VMEM],
+        out_specs=(ANY,) * 7 + (VMEM,) * 3,
+        scratch_shapes=[
+            buf(full, low), buf(full, low), buf((8, 4, rows, cols), low), buf((4,) + o.shape, low),
+            buf((4,) + d.shape, low), buf((8, 4, rows, 2 * ff), low), buf((2,) + seg.shape, seg.dtype),
+            buf((8, 4, 8, 128), wide), blocks(width, low), buf(full, low), buf(full, low),
+            blocks(cols, wide), blocks(cols, low), blocks(1, jnp.int32), blocks(head_dim, wide),
+            blocks(head_dim, wide), blocks(att_cols, wide), blocks(att_cols, low),
+            buf((4, 2, quarter, 1), wide), buf(full, low), buf(full, low), buf(full, low), buf(full, low),
+            buf(piece, low), buf(piece, low), buf(piece, low), buf(piece, low), buf(piece, wide),
+            buf(piece, wide),
+            blocks(ff, low), blocks(2 * ff, low), blocks(att_cols, low), blocks(att_cols, wide),
+            blocks(head_dim, wide), blocks(head_dim, wide), blocks(cols, low),
+            buf((4,) + d.shape, low), buf((8, 4, rows, 2 * ff), low), buf((4,) + o.shape, low),
+            buf((8, 4, rows, cols), low),
+            buf((4,) + d.shape, low), buf(d.shape, low),
+            buf((4, 8, rows, 2 * ff), low), buf((8, rows, 2 * ff), low), buf((8, rows, 2 * ff), wide),
+            buf((8, rows, 2 * ff), low),
+            buf((4,) + o.shape, low), buf(o.shape, low),
+            buf((4, 8, rows, cols), low), buf((8, rows, cols), low), buf((8, rows, cols), wide),
+            buf((8, rows, cols), low),
+            buf((24, 128), wide), buf((8, 24, 128), wide), buf((3, 24, 128), wide),
+        ]
+        + half_scratch(tokens, width) * 4
+        + [SEM((2, 4)), SEM((2, 4)), SEM((4, 7)), SEM((4, 7)), SEM((24,)), SEM((24,)), SEM((16,)), SEM((16,))]
+        + [SEM((21,)), SEM((21,))]
+        + [SEM((2, 5))] * 4
+        + [SEM((2, 4))] * 4
+        + [SEM((2, 4)), SEM((2, 4)), SEM((40,)), SEM((40,)), SEM((8,))],
+        compiler_params=pltpu.CompilerParams(
+            collective_id=0, has_side_effects=True, vmem_limit_bytes=67043328
+        ),
+    )(x, cot, seg, q, k, v, g, u, o, d, gain, head_gains)
+
+
+def finish_kernel(*refs):
+    half = len(refs) // 2
+    for src, dst in zip(refs[:half], refs[half:]):
+        dst[...] = src[...].astype(dst.dtype)
+
+
+def finish_step(*arrays):
+    return pl.pallas_call(
+        finish_kernel,
+        name="finish_step",
+        out_shape=tuple(
+            jax.ShapeDtypeStruct(v.shape, v.dtype if i < 2 else jnp.float32) for i, v in enumerate(arrays)
+        ),
+        in_specs=[VMEM] * len(arrays),
+        out_specs=(VMEM,) * len(arrays),
+    )(*arrays)
+
+
+def plane_body(
+    inputs, segments, attn_gain, head_gains, query_weight, key_matrix, value_matrix, out_weight,
+    ffn_gain, gate_weight, up_weight, down_weight, cotangent,
+):
+    head_dim = head_gains.shape[1]
+    z = lax.axis_index("uly")
+    head = 4 * lax.axis_index("fsdp") + lax.axis_index("blk")
+    piece = attn_gain.shape[0]
+    pair = jnp.stack([attn_gain, ffn_gain]).astype(jnp.float32)
+    spot = (jnp.arange(128, dtype=jnp.int32) // piece == z)[None]
+    gains_own = jnp.where(spot, jnp.tile(pair, (1, 128 // piece)), 0.0)
+    gains_own = jnp.concatenate([gains_own, jnp.zeros((6, 128), jnp.float32)], axis=0)
+    outputs, grad_inputs, q_grad, k_grad, v_grad, g_grad, u_grad, sums, out_grad, down_grad = layer_step(
+        inputs, cotangent, segments, query_weight, key_matrix, value_matrix, gate_weight, up_weight,
+        out_weight, down_weight, gains_own, head_gains.astype(jnp.float32),
+    )
+    attn_gain_grad = lax.dynamic_slice(sums, (head, z * piece), (1, piece))[0]
+    ffn_gain_grad = lax.dynamic_slice(sums, (8 + head, z * piece), (1, piece))[0]
+    share = head_dim // 32
+    head_gain_grad = lax.dynamic_slice(sums, (16, (4 * head + z) * share), (2, share))
+    outputs, grad_inputs, q_grad, k_grad, v_grad, out_grad, g_grad, u_grad, down_grad = finish_step(
+        outputs, grad_inputs, q_grad, k_grad, v_grad, out_grad, g_grad, u_grad, down_grad
+    )
+    return (
+        outputs, grad_inputs, attn_gain_grad, head_gain_grad, q_grad, k_grad, v_grad, out_grad,
+        ffn_gain_grad, g_grad, u_grad, down_grad,
+    )
+
+
+def fits_plane(mesh, seq_count, heads):
+    shape = mesh.shape
+    return (shape["fsdp"], shape["blk"], shape["uly"]) == (2, 4, 4) and seq_count == 4 and heads == 8
+
+
 def solution(mesh):
-    return jax.shard_map(
-        body,
+    def step(*arrays):
+        seq_count = arrays[0].shape[0]
+        heads = arrays[5].shape[1] // arrays[3].shape[1]
+        chosen = plane_body if fits_plane(mesh, seq_count, heads) else body
+        return mapped(chosen)(*arrays)
+
+    mapped = functools.partial(
+        jax.shard_map,
         mesh=mesh,
         in_specs=(
             P("fsdp", ("blk", "uly"), None),
@@ -416,3 +1228,4 @@
         ),
         check_vma=False,
     )
+    return step

time: 1780 us -> 216 us (0.12)
  waiting for transfers between devices: 1380 us -> 0 us
  Pallas kernels: 0 us -> 209 us
  blocking collectives: 152 us -> 0 us
  starting transfers between devices: 88.4 us -> 0 us
  matrix products: 82.4 us -> 0 us
  local copies, waits for them, and re-layouts: 30.9 us -> 4.58 us
  other arithmetic: 22.1 us -> 0.59 us
    reduce_scatter x7 -> x0, waiting for transfers between devices: 1030 us -> none  [the longest x1 187 us: body(): lax.psum_scatter(query_grad, ('fsdp', 'blk', 'uly'), scatter_dimension=0,...]
    all_gather x7 -> x0, waiting for transfers between devices: 295 us -> none  [the longest x1 65.8 us: fetch_feedforward(): lax.all_gather(gate_weight, ('fsdp', 'blk', 'uly'), axis=0, tiled=True)]
    pallas_call x0 -> x2, Pallas kernels: none -> 209 us  [the longest x1 206 us: layer_step(): pl.pallas_call(layer_kernel, name='layer_step', out_shape=(shape(x.shape,...]
    dot_general x27 -> x0, matrix products: 82.4 us -> none  [the longest x1 6.6 us: body(): jnp.einsum('std,df->stf', normed_two, gate_full, preferred_element_type=j...]
    unnamed x2 -> x0, blocking collectives: 80.7 us -> none
    ppermute x10 -> x0, starting transfers between devices: 73.4 us -> none  [the longest x6 46.2 us: passed_along(): lax.ppermute(value, axis, [(source, source + steps) for source in range(f...]
    all_to_all x4 -> x0, blocking collectives: 71.7 us -> none  [the longest x1 30.7 us: body(): lax.all_to_all(grad_query_low, 'uly', split_axis=1, concat_axis=2, tiled=...]
    all_to_all x4 -> x0, waiting for transfers between devices: 35.1 us -> none  [the longest x1 15.9 us: body(): lax.all_to_all(query_rot.astype(jnp.bfloat16), 'uly', split_axis=2, conca...]
  transfers between devices with their start and end apart: 28 -> 0, of which waited for: 23 -> 0; matrix products, arithmetic and copies ran while one was open for 5% -> 0% of each run, Pallas kernels for 0% -> 0%
where the time goes in v3:
time: 216 us; the launch traced here: 215 us
  Pallas kernels  209 us (97%)
  local copies, waits for them, and re-layouts  4.58 us (2%)
    pallas_call x1, Pallas kernels, layer_step(): pl.pallas_call(layer_kernel, name='layer_step', out_shape=(shape(x.shape,...  206 us

profile of v3, /device:TPU:0, one launch (start us, length us, event | category | flops | bytes accessed | tf_op | source)
XLA Modules:
  0.0 215.2 jit_solution(5760877868404878316)
XLA Ops:
  0.7 0.0 copy-start
  0.7 0.0 copy-start.1
  0.7 0.6 copy-done
  1.3 0.0 copy-done.1
  1.3 0.0 copy-start.2
  1.4 0.6 copy-done.2
  2.0 0.6 convert_element_type.11.hg_ref
  2.6 0.1 tile.10
  2.7 0.6 concatenate.7.gain_ref
  3.3 206.5 %layer_step.1 = (bf16[2,64,1024]{2,1,0:T(8,128)(2,1)}, bf16[2,64,1024]{2,1,0:T(8,128)(2,1)}, bf16[32,2048]{1,0:T(8,128)(2,1)}, bf16[32,1024]{1,0:T(8,128)(2,1)},...) custom-call(bf16[2,64,1024]{2,1,0:T(8,128)(2,1)} %x_ref.1, ...), custom_call_target="tpu_custom_call" | custom-call | tf_op jit(solution)/shard_map/layer_step/pallas_call | solution.py:1095
  209.7 1.3 dynamic-slice_bitcast_fusion
  211.0 1.3 constant_dynamic-slice_fusion
  212.3 2.9 %finish_step.1 = (bf16[2,64,1024]{2,1,0:T(8,128)(2,1)}, bf16[2,64,1024]{2,1,0:T(8,128)(2,1)}, f32[32,2048]{1,0:T(8,128)}, f32[32,1024]{1,0:T(8,128)}, f32[32,102...) custom-call(bf16[2,64,1024]{2,1,0:T(8,128)(2,1)} %get-tuple-element.31.refs_, ...), custom_call_target="tpu_custom_call" | custom-call | tf_op jit(solution)/shard_map/finish_step/pallas_call | solution.py:1145
  (4 shorter events, 0.0 us)
Async XLA Ops:
  0.7 0.7 copy-start
  0.7 0.7 copy-start.1
  1.3 0.7 copy-start.2

commit v4 on v3

--- a/solution.py
+++ b/solution.py
@@ -476,8 +476,20 @@
         sends.go(src, me.shard(full), send_sems.at[i], recv_sems.at[i], me.peer(*d))
 
 
-def spread_forward(me, sends, full, send_sems, recv_sems):
-    for i in (1, 2, 0):
+def spread_piece(me, full, k, send_sems, recv_sems):
+    part = full.at[me.block, k, me.x]
+    for i, d in enumerate(FAR + [(0, 0, 1)]):
+        remote(part, part, send_sems.at[i], recv_sems.at[i], me.peer(*d)).start()
+
+
+def spread_pieces_sent(me, sends, full, send_sems, recv_sems):
+    part = me.shard(full)
+    for i, d in enumerate(FAR + [(0, 0, 1)]):
+        sends.pending.append((None, remote(part, part, send_sems.at[i], recv_sems.at[i], me.peer(*d))))
+
+
+def spread_forward(me, sends, full, send_sems, recv_sems, which=(1, 2, 0)):
+    for i in which:
         part = me.shard(full, *FAR[i])
         arrived(part, recv_sems.at[i])
         sends.go(part, part, send_sems.at[4 + i], recv_sems.at[4 + i], me.peer(0, 0, 1))
@@ -493,7 +505,7 @@
 
 
 def line_spread(me, sends, src, part, sems):
-    for dz in (1, 2):
+    for dz in (2, 1):
         sends.go_if(me.z < 4 - dz, src, part(me.z), sems.at[0, dz - 1], sems.at[1, dz - 1], me.line(dz))
         sends.go_if(me.z >= dz, src, part(me.z), sems.at[0, dz + 1], sems.at[1, dz + 1], me.line(4 - dz))
 
@@ -535,12 +547,12 @@
 def reduce_start(me, sends, own, came, sems):
     z = me.z
     outer, _ = outer_inner(me)
-    sends.go_if(z < 3, own((z + 1) % 4), came.at[0], sems.at[0, 0], sems.at[1, 0], me.line(1))
-    sends.go_if(z > 0, own((z + 3) % 4), came.at[1], sems.at[0, 1], sems.at[1, 1], me.line(3))
     nearer = line_to(me, 1 + z // 3)
     sends.go_if(outer, own((7 - z) % 4), came.at[3], sems.at[0, 3], sems.at[1, 3], nearer)
     far = (z + 2) % 4
     sends.go_if(outer, own(far), came.at[2], sems.at[0, 2], sems.at[1, 2], line_to(me, far))
+    sends.go_if(z < 3, own((z + 1) % 4), came.at[0], sems.at[0, 0], sems.at[1, 0], me.line(1))
+    sends.go_if(z > 0, own((z + 3) % 4), came.at[1], sems.at[0, 1], sems.at[1, 1], me.line(3))
 
 
 def reduce_join(me, sends, own, came, buf, sems):
@@ -602,9 +614,9 @@
         for to in (0, 1):
             src = src_ref.at[j, pl.ds(half * to, half)]
             dst = full_ref.at[me.block, me.z, to]
-            mine = jnp.logical_and(me.x == to, me.z == 2 * me.x + j)
+            mine = jnp.logical_and(me.x == to, me.z == 2 * j + me.x)
             copy = remote(
-                src, dst, send_sems.at[2 * j + to], recv_sems.at[me.z], (to, me.block, 2 * me.x + j)
+                src, dst, send_sems.at[2 * j + to], recv_sems.at[me.z], (to, me.block, 2 * j + me.x)
             )
             if wait:
                 pl.when(jnp.logical_not(mine))(lambda copy=copy: copy.wait_send())
@@ -686,10 +698,10 @@
     half = dst_ref.shape[1] // 2
     for k in range(4):
         src = src_ref.at[k]
-        dst = dst_ref.at[me.z % 2, pl.ds(half * me.x, half)]
-        mine = jnp.logical_and(me.x == me.z // 2, me.z == k)
-        spot = 2 * (me.z % 2) + me.x
-        copy = remote(src, dst, send_sems.at[k], recv_sems.at[spot], (me.z // 2, me.block, k))
+        dst = dst_ref.at[me.z // 2, pl.ds(half * me.x, half)]
+        mine = jnp.logical_and(me.x == me.z % 2, me.z == k)
+        spot = 2 * (me.z // 2) + me.x
+        copy = remote(src, dst, send_sems.at[k], recv_sems.at[spot], (me.z % 2, me.block, k))
         if wait:
             pl.when(jnp.logical_not(mine))(lambda copy=copy: copy.wait_send())
             continue
@@ -714,7 +726,7 @@
     y_ref, gx_ref, dq_ref, dk_ref, dv_ref, dg_ref, du_ref, sums_ref, osum_ref, dsum_ref,
     xf, cf, wf, of, df, guf, segs, gains, n1, nf, gf, pre, qkv, segcol, cos_s, sin_s, att, attlow,
     totals, part, part2, part3, down, n2, gm, y_s, gi_s, mid, gmid,
-    hid, gboth, ga, gq, gk, gv, gpre, dd, dgu, do, dw,
+    gates, hid, gboth, ga, gq, gk, gv, gpre, dd, dgu, do, dw,
     d_came, d_buf, gu_came, gu_buf, gu_total, gu_sum, o_came, o_buf, w_came, w_buf, w_total, w_sum,
     pack, packs, linep,
     sib1, out1, came1, hs1, hr1, sib2, out2, came2, hs2, hr2, sib3, out3, came3, hs3, hr3,
@@ -752,8 +764,8 @@
                 local(src, dst, wr.at[n])
             else:
                 sends.go(src, dst, ws.at[3 * i + n], wr.at[3 * i + n], me.peer(*d))
-    permuted_in(me, xf, pr.at[0])
-    spread_start(me, sends, me.shard(xf), xf, as_.at[0], ar.at[0])
+    arrived(xf.at[me.block, z, x], pr.at[0, z])
+    spread_piece(me, xf, z, as_.at[0], ar.at[0])
     for i, d in enumerate(PLANE):
         t = me.index(*d)
         for n, (ref, width, off) in enumerate(cuts):
@@ -763,6 +775,17 @@
     d_part = lambda k: df.at[k]
     gu_part = lambda k: guf.at[:, k]
     line_spread(me, sends, qkv_part(z), qkv_part, zq)
+    for turn in (1, 3, 2):
+        k = (z + turn) % 4
+        arrived(xf.at[me.block, k, x], pr.at[0, k])
+        spread_piece(me, xf, k, as_.at[0], ar.at[0])
+    spread_pieces_sent(me, sends, xf, as_.at[0], ar.at[0])
+    own_gain.wait()
+    for turn in TURNS:
+        arrived(gains.at[p, me.behind(turn)], gr.at[turn])
+    for i, d in enumerate(PLANE[1:]):
+        sends.go(gains.at[p], gains.at[p], gs.at[4 + i], gr.at[4 + i], me.peer(*d))
+    line_forward(me, sends, qkv_part, zq)
     permute_in(me, cot_ref, cf, ps.at[1], pr.at[1])
     line_spread(me, sends, o_ref, o_part, zo)
     ff = g_ref.shape[1] // 8
@@ -775,15 +798,10 @@
                 local(src, dst, ur.at[n])
             else:
                 sends.go(src, dst, us.at[2 * i + n], ur.at[2 * i + n], me.peer(*d))
-    own_gain.wait()
-    for turn in TURNS:
-        arrived(gains.at[p, me.behind(turn)], gr.at[turn])
-    for i, d in enumerate(PLANE[1:]):
-        sends.go(gains.at[p], gains.at[p], gs.at[4 + i], gr.at[4 + i], me.peer(*d))
     own_seg.wait()
     arrived(segs.at[(x + 1) % 2], ls.at[3])
     head_dim = hg_ref.shape[1]
-    segrow = segs[z // 2, pl.ds(z % 2, 1), :]
+    segrow = segs[z % 2, pl.ds(z // 2, 1), :]
     tokens = segrow.shape[1]
     column = jnp.transpose(jnp.broadcast_to(segrow.astype(wide_t), (8, tokens)))[:, :1]
     segcol[...] = column.astype(jnp.int32).reshape(4, 256, 1)
@@ -811,7 +829,6 @@
     for i, d in enumerate(PLANE[1:]):
         arrived(gains.at[me.index(*d)], gr.at[4 + i])
     gain_one, gain_two = (gain_row(gains, 0), gain_row(gains, 1))
-    line_forward(me, sends, qkv_part, zq)
     spread_forward(me, sends, xf, as_.at[0], ar.at[0])
     spread_finish(me, xf, ar.at[0])
 
@@ -820,12 +837,6 @@
         rows = xf[b].reshape(256, -1).astype(wide_t)
         n1[b] = (rows * head_scale(rows) * gain_one).astype(low)
 
-    for i, d in enumerate(PLANE):
-        t = me.index(*d)
-        for n in (0, 1):
-            arrived(guf.at[t, z, :, pl.ds(n * ff, ff)], ur.at[2 * i + n])
-    line_spread(me, sends, gu_part(z), gu_part, zg)
-    line_spread(me, sends, d_ref, d_part, zd)
     line_finish(me, qkv_part, zq)
 
     @pl.loop(0, 4)
@@ -839,8 +850,16 @@
             qkv[b, :, pl.ds(head_dim * h, head_dim)] = (n * cosine + turned(n) * sine).astype(low)
         qkv[b, :, pl.ds(3 * head_dim, head_dim)] = rows[:, 3 * head_dim :].astype(low)
 
+    permuted_in(me, cf, pr.at[1])
+    spread_start(me, sends, me.shard(cf), cf, as_.at[1], ar.at[1])
     own_o.wait()
     line_forward(me, sends, o_part, zo)
+    for i, d in enumerate(PLANE):
+        t = me.index(*d)
+        for n in (0, 1):
+            arrived(guf.at[t, z, :, pl.ds(n * ff, ff)], ur.at[2 * i + n])
+    line_spread(me, sends, gu_part(z), gu_part, zg)
+    line_spread(me, sends, d_ref, d_part, zd)
     top = lambda r: jnp.max(jnp.abs(hg_ref[pl.ds(r, 1), :]), axis=1, keepdims=True)
     bound = math.sqrt(head_dim) * top(0) * top(1)
     scale = head_dim ** (-0.5)
@@ -868,9 +887,6 @@
             att[b, :, at] = mixed
             attlow[b, :, at] = mixed.astype(low)
 
-        if b == 2:
-            permuted_in(me, cf, pr.at[1])
-            spread_start(me, sends, me.shard(cf), cf, as_.at[1], ar.at[1])
     line_finish(me, o_part, zo)
 
     @pl.loop(0, 4)
@@ -889,27 +905,35 @@
     own_n = local(n2, me.shard(nf), ls.at[6])
     spread_start(me, sends, n2, nf, as_.at[2], ar.at[2])
     line_forward(me, sends, gu_part, zg)
+    spread_forward(me, sends, nf, as_.at[2], ar.at[2], (1, 2))
     line_forward(me, sends, d_part, zd)
-    spread_forward(me, sends, nf, as_.at[2], ar.at[2])
+    spread_forward(me, sends, nf, as_.at[2], ar.at[2], (0,))
     spread_finish(me, nf, ar.at[2])
     own_n.wait()
-    spread_finish(me, cf, ar.at[1])
-    own_d.wait()
     line_finish(me, gu_part, zg)
-    line_finish(me, d_part, zd)
 
     @pl.loop(0, 4)
     def _(b):
         both = mat(nf[b].reshape(256, -1), guf[...].reshape(-1, 2 * ff))
+        gates[b] = both
+        gate, up = (both[:, :ff], both[:, ff:])
+        hid[b] = (gate / (1.0 + jnp.exp(-gate)) * up).astype(low)
+
+    spread_finish(me, cf, ar.at[1])
+    own_d.wait()
+    dd[...] = mat_left(hid[...].reshape(-1, ff), cf[...].reshape(tokens, -1)).astype(low).reshape(dd.shape)
+    own_dd = lambda k: dd.at[k]
+    reduce_start(me, sends, own_dd, d_came, rd)
+    line_finish(me, d_part, zd)
+
+    @pl.loop(0, 4)
+    def _(b):
+        both = gates[b]
         gate, up = (both[:, :ff], both[:, ff:])
         sig = 1.0 / (1.0 + jnp.exp(-gate))
-        silu = gate * sig
-        hidden = (silu * up).astype(low)
-        hid[b] = hidden
-        w_down = df[...].reshape(ff, -1)
-        grad = mat_right(cf[b].reshape(256, -1), w_down)
+        grad = mat_right(cf[b].reshape(256, -1), df[...].reshape(ff, -1))
         gboth[b, :, pl.ds(0, ff)] = (grad * up * sig * (1.0 + gate * (1.0 - sig))).astype(low)
-        gboth[b, :, pl.ds(ff, ff)] = (grad * silu).astype(low)
+        gboth[b, :, pl.ds(ff, ff)] = (grad * (gate * sig)).astype(low)
         rows = mat_right(gboth[b], guf[...].reshape(-1, 2 * ff)).astype(low)
         part2[b] = rows.reshape(part2.shape[1:])
         half_block(me, part2, sib2, hs2, hr2, b)
@@ -926,6 +950,7 @@
 
     own_gu = lambda k: dgu.at[:, k]
     reduce_start(me, sends, own_gu, gu_came, rg)
+    reduce_join(me, sends, own_dd, d_came, d_buf, rd)
     grad = half_in(me, part2, sib2, came2, hr2)
     middle = mid[...]
     r = head_scale(middle)
@@ -946,12 +971,10 @@
 
     for b in range(4):
         half_block(me, down, sib3, hs3, hr3, b, sends)
-    dd[...] = mat_left(hid[...].reshape(-1, ff), cf[...].reshape(tokens, -1)).astype(low).reshape(dd.shape)
-    own_dd = lambda k: dd.at[k]
-    reduce_start(me, sends, own_dd, d_came, rd)
     half_out(me, sends, down, sib3, out3, came3, hs3, hr3)
+    spread_forward(me, sends, gf, as_.at[3], ar.at[3], (1, 2))
     reduce_join(me, sends, own_gu, gu_came, gu_buf, rg)
-    spread_forward(me, sends, gf, as_.at[3], ar.at[3])
+    spread_forward(me, sends, gf, as_.at[3], ar.at[3], (0,))
     spread_finish(me, gf, ar.at[3])
     own_gm.wait()
 
@@ -977,9 +1000,7 @@
                 gv[kb] += mat_left(probs.astype(low), grad)
             gq[b, :, at] = grad_query
 
-        if b == 0:
-            reduce_join(me, sends, own_dd, d_came, d_buf, rd)
-        if b == 1:
+        if b == 2:
             y_s[...] = (mid[...] + half_in(me, down, sib3, came3, hr3)).astype(low)
             permute_out(me, y_s, y_ref, cs.at[0], cr.at[0])
     do[...] = mat_left(attlow[...].reshape(tokens, -1), gf[...].reshape(tokens, -1)).astype(low).reshape(do.shape)
@@ -1002,13 +1023,6 @@
             gn = gh * hg_ref[pl.ds(h // 2, 1), :]
             gpre[b, :, at] = (r * (gn - n * jnp.mean(gn * n, axis=-1, keepdims=True))).astype(low)
         gpre[b, :, value_at] = gv[b].astype(low)
-        rows = mat_right(gpre[b], wf[...].reshape(-1, wf.shape[3])).astype(low)
-        part3[b] = rows.reshape(part3.shape[1:])
-        half_block(me, part3, sib4, hs4, hr4, b)
-
-    for b in range(4):
-        half_block(me, part3, sib4, hs4, hr4, b, sends)
-    half_out(me, sends, part3, sib4, out4, came4, hs4, hr4)
 
     @pl.loop(0, 4)
     def _(b):
@@ -1018,6 +1032,16 @@
 
     own_dw = lambda k: dw.at[:, k]
     reduce_start(me, sends, own_dw, w_came, rw)
+
+    @pl.loop(0, 4)
+    def _(b):
+        rows = mat_right(gpre[b], wf[...].reshape(-1, wf.shape[3])).astype(low)
+        part3[b] = rows.reshape(part3.shape[1:])
+        half_block(me, part3, sib4, hs4, hr4, b)
+
+    for b in range(4):
+        half_block(me, part3, sib4, hs4, hr4, b, sends)
+    half_out(me, sends, part3, sib4, out4, came4, hs4, hr4)
     reduce_join(me, sends, own_do, o_came, o_buf, ro)
     reduce_total(me, own_gu, gu_came, gu_total, rg)
     gu_sum[...] = gu_total[...].astype(low)
@@ -1031,25 +1055,17 @@
             else:
                 sends.go(src, dst, ds.at[2 * i + n], dr.at[2 * i + n], me.peer(*d))
     reduce_total(me, own_dd, d_came, dsum_ref, rd)
+    reduce_join(me, sends, own_dw, w_came, w_buf, rw)
     grad = half_in(me, part3, sib4, came4, hr4)
     rows = xf[me.block, :, x].astype(wide_t)
     r = head_scale(rows)
-    gi_s[...] = (gmid[...] + norm_back(grad, rows, gain_one, r)).astype(low)
-    permute_out(me, gi_s, gx_ref, cs.at[1], cr.at[1])
     share = total_row(grad * rows * r)
     for i in range(8):
         pack[pl.ds(i, 1)] = share[:, 128 * i : 128 * i + 128]
-    for i, d in enumerate(PLANE[1:]):
-        sends.go(pack, packs.at[i], gs.at[11 + i], gr.at[11 + i], me.peer(*d))
-    reduce_join(me, sends, own_dw, w_came, w_buf, rw)
-    reduce_total(me, own_do, o_came, osum_ref, ro)
-    total = pack[...]
-    for i in range(7):
-        arrived(packs.at[i], gr.at[11 + i])
-        total = total + packs[i]
-    packs[7] = total
     for turn in TURNS:
-        sends.go(packs.at[7], linep.at[turn - 1], gs.at[17 + turn], gr.at[17 + turn], me.line(turn))
+        sends.go(pack, linep.at[turn - 1], gs.at[17 + turn], gr.at[17 + turn], me.line(turn))
+    gi_s[...] = (gmid[...] + norm_back(grad, rows, gain_one, r)).astype(low)
+    permute_out(me, gi_s, gx_ref, cs.at[1], cr.at[1])
     reduce_total(me, own_dw, w_came, w_total, rw)
     w_sum[...] = w_total[...].astype(low)
     backs = ((dq_ref, wide, 0), (dk_ref, narrow, wide), (dv_ref, narrow, wide + narrow))
@@ -1063,9 +1079,18 @@
             else:
                 s = 16 + 3 * i + n
                 sends.go(src, dst, ds.at[s], dr.at[s], me.peer(*d))
+    total = pack[...]
     for turn in TURNS:
         arrived(linep.at[turn - 1], gr.at[17 + turn])
-    sums_ref[...] = ((total + linep[0]) + linep[1]) + linep[2]
+        total = total + linep[turn - 1]
+    packs[7] = total
+    for i, d in enumerate(PLANE[1:]):
+        sends.go(packs.at[7], packs.at[i], gs.at[11 + i], gr.at[11 + i], me.peer(*d))
+    reduce_total(me, own_do, o_came, osum_ref, ro)
+    for i in range(7):
+        arrived(packs.at[i], gr.at[11 + i])
+        total = total + packs[i]
+    sums_ref[...] = total
     for i, d in enumerate(PLANE):
         t = me.index(*d)
         for n, ref in enumerate((dg_ref, du_ref)):
@@ -1111,7 +1136,7 @@
             buf((4, 2, quarter, 1), wide), buf(full, low), buf(full, low), buf(full, low), buf(full, low),
             buf(piece, low), buf(piece, low), buf(piece, low), buf(piece, low), buf(piece, wide),
             buf(piece, wide),
-            blocks(ff, low), blocks(2 * ff, low), blocks(att_cols, low), blocks(att_cols, wide),
+            blocks(2 * ff, wide), blocks(ff, low), blocks(2 * ff, low), blocks(att_cols, low), blocks(att_cols, wide),
             blocks(head_dim, wide), blocks(head_dim, wide), blocks(cols, low),
             buf((4,) + d.shape, low), buf((8, 4, rows, 2 * ff), low), buf((4,) + o.shape, low),
             buf((8, 4, rows, cols), low),
@@ -1126,7 +1151,7 @@
         + half_scratch(tokens, width) * 4
         + [SEM((2, 4)), SEM((2, 4)), SEM((4, 7)), SEM((4, 7)), SEM((24,)), SEM((24,)), SEM((16,)), SEM((16,))]
         + [SEM((21,)), SEM((21,))]
-        + [SEM((2, 5))] * 4
+        + [SEM((2, 6))] * 4
         + [SEM((2, 4))] * 4
         + [SEM((2, 4)), SEM((2, 4)), SEM((40,)), SEM((40,)), SEM((8,))],
         compiler_params=pltpu.CompilerParams(
@@ -1135,22 +1160,32 @@
     )(x, cot, seg, q, k, v, g, u, o, d, gain, head_gains)
 
 
-def finish_kernel(*refs):
+def finish_kernel(sums_ref, *refs):
     half = len(refs) // 2
-    for src, dst in zip(refs[:half], refs[half:]):
+    for src, dst in zip(refs[:half], refs[half : 2 * half]):
         dst[...] = src[...].astype(dst.dtype)
-
-
-def finish_step(*arrays):
+    cut_ref = refs[2 * half]
+    z = lax.axis_index("uly")
+    head = 4 * lax.axis_index("fsdp") + lax.axis_index("blk")
+    share = sums_ref.shape[1] // 4
+    gain_rows = [sums_ref[pl.ds(head, 1), :], sums_ref[pl.ds(8 + head, 1), :]]
+    gain_rows = pltpu.roll(jnp.concatenate(gain_rows + [jnp.zeros((6, 128), jnp.float32)], axis=0), 128 - share * z, 1)
+    head_rows = pltpu.roll(sums_ref[16:24, :], 128 - (4 * head + z) * (share // 8), 1)
+    cut_ref[0:8] = gain_rows
+    cut_ref[8:16] = head_rows
+
+
+def finish_step(sums, *arrays):
     return pl.pallas_call(
         finish_kernel,
         name="finish_step",
         out_shape=tuple(
             jax.ShapeDtypeStruct(v.shape, v.dtype if i < 2 else jnp.float32) for i, v in enumerate(arrays)
-        ),
-        in_specs=[VMEM] * len(arrays),
-        out_specs=(VMEM,) * len(arrays),
-    )(*arrays)
+        )
+        + (jax.ShapeDtypeStruct((16, 128), jnp.float32),),
+        in_specs=[VMEM] * (1 + len(arrays)),
+        out_specs=(VMEM,) * (1 + len(arrays)),
+    )(sums, *arrays)
 
 
 def plane_body(
@@ -1159,23 +1194,19 @@
 ):
     head_dim = head_gains.shape[1]
     z = lax.axis_index("uly")
-    head = 4 * lax.axis_index("fsdp") + lax.axis_index("blk")
     piece = attn_gain.shape[0]
     pair = jnp.stack([attn_gain, ffn_gain]).astype(jnp.float32)
     spot = (jnp.arange(128, dtype=jnp.int32) // piece == z)[None]
     gains_own = jnp.where(spot, jnp.tile(pair, (1, 128 // piece)), 0.0)
     gains_own = jnp.concatenate([gains_own, jnp.zeros((6, 128), jnp.float32)], axis=0)
     outputs, grad_inputs, q_grad, k_grad, v_grad, g_grad, u_grad, sums, out_grad, down_grad = layer_step(
-        inputs, cotangent, segments, query_weight, key_matrix, value_matrix, gate_weight, up_weight,
-        out_weight, down_weight, gains_own, head_gains.astype(jnp.float32),
-    )
-    attn_gain_grad = lax.dynamic_slice(sums, (head, z * piece), (1, piece))[0]
-    ffn_gain_grad = lax.dynamic_slice(sums, (8 + head, z * piece), (1, piece))[0]
-    share = head_dim // 32
-    head_gain_grad = lax.dynamic_slice(sums, (16, (4 * head + z) * share), (2, share))
-    outputs, grad_inputs, q_grad, k_grad, v_grad, out_grad, g_grad, u_grad, down_grad = finish_step(
-        outputs, grad_inputs, q_grad, k_grad, v_grad, out_grad, g_grad, u_grad, down_grad
-    )
+        inputs, cotangent, segments, query_weight, key_matrix, value_matrix, gate_weight, up_weight, out_weight, down_weight, gains_own, head_gains.astype(jnp.float32),
+    )
+    outputs, grad_inputs, q_grad, k_grad, v_grad, out_grad, g_grad, u_grad, down_grad, cut = finish_step(
+        sums, outputs, grad_inputs, q_grad, k_grad, v_grad, out_grad, g_grad, u_grad, down_grad
+    )
+    attn_gain_grad, ffn_gain_grad = (cut[0, :piece], cut[1, :piece])
+    head_gain_grad = cut[8:10, : head_dim // 32]
     return (
         outputs, grad_inputs, attn_gain_grad, head_gain_grad, q_grad, k_grad, v_grad, out_grad,
         ffn_gain_grad, g_grad, u_grad, down_grad,

time: 216 us -> 190 us (0.88)
  Pallas kernels: 209 us -> 183 us
    pallas_call x1, Pallas kernels: 206 us -> 180 us  [layer_step(): pl.pallas_call(layer_kernel, name='layer_step', out_shape=(shape(x.shape,...]
where the time goes in v4:
time: 190 us; the launch traced here: 189 us
  Pallas kernels  183 us (96%)
  local copies, waits for them, and re-layouts  4.5 us (2%)
    pallas_call x1, Pallas kernels, layer_step(): pl.pallas_call(layer_kernel, name='layer_step', out_shape=(shape(x.shape,...  180 us

profile of v4, /device:TPU:0, one launch (start us, length us, event | category | flops | bytes accessed | tf_op | source)
XLA Modules:
  0.0 189.3 jit_solution(14587241099278450886)
XLA Ops:
  0.7 0.0 copy-start
  0.7 0.0 copy-start.1
  0.7 0.6 copy-done
  1.3 0.0 copy-done.1
  1.3 0.0 copy-start.2
  1.3 0.6 copy-done.2
  2.0 0.6 convert_element_type.11.hg_ref
  2.6 0.1 tile.10
  2.6 0.6 concatenate.7.gain_ref
  3.2 180.5 %layer_step.1 = (bf16[2,64,1024]{2,1,0:T(8,128)(2,1)}, bf16[2,64,1024]{2,1,0:T(8,128)(2,1)}, bf16[32,2048]{1,0:T(8,128)(2,1)}, bf16[32,1024]{1,0:T(8,128)(2,1)},...) custom-call(bf16[2,64,1024]{2,1,0:T(8,128)(2,1)} %x_ref.1, ...), custom_call_target="tpu_custom_call" | custom-call | tf_op jit(solution)/shard_map/layer_step/pallas_call | solution.py:1120
  183.8 3.0 %finish_step.1 = (bf16[2,64,1024]{2,1,0:T(8,128)(2,1)}, bf16[2,64,1024]{2,1,0:T(8,128)(2,1)}, f32[32,2048]{1,0:T(8,128)}, f32[32,1024]{1,0:T(8,128)}, f32[32,102...) custom-call(f32[24,128]{1,0:T(8,128)} %get-tuple-element.32.sums_ref, ...), custom_call_target="tpu_custom_call" | custom-call | tf_op jit(solution)/shard_map/finish_step/pallas_call | solution.py:1179
  186.8 1.2 slice.10
  188.0 1.3 slice_bitcast_fusion
  (4 shorter events, 0.0 us)
Async XLA Ops:
  0.7 0.7 copy-start
  0.7 0.7 copy-start.1
  1.3 0.7 copy-start.2

commit v5 on v4

--- a/solution.py
+++ b/solution.py
@@ -471,33 +471,80 @@
                 pl.when(condition)(lambda copy=copy: copy.wait_send())
 
 
+WAYS = [(1, 0, 0), (0, 1, 0)]
+
+
 def spread_start(me, sends, src, full, send_sems, recv_sems):
-    for i, d in enumerate(FAR + [(0, 0, 1)]):
-        sends.go(src, me.shard(full), send_sems.at[i], recv_sems.at[i], me.peer(*d))
-
-
-def spread_piece(me, full, k, send_sems, recv_sems):
-    part = full.at[me.block, k, me.x]
-    for i, d in enumerate(FAR + [(0, 0, 1)]):
-        remote(part, part, send_sems.at[i], recv_sems.at[i], me.peer(*d)).start()
-
-
-def spread_pieces_sent(me, sends, full, send_sems, recv_sems):
-    part = me.shard(full)
-    for i, d in enumerate(FAR + [(0, 0, 1)]):
-        sends.pending.append((None, remote(part, part, send_sems.at[i], recv_sems.at[i], me.peer(*d))))
-
-
-def spread_forward(me, sends, full, send_sems, recv_sems, which=(1, 2, 0)):
-    for i in which:
-        part = me.shard(full, *FAR[i])
-        arrived(part, recv_sems.at[i])
-        sends.go(part, part, send_sems.at[4 + i], recv_sems.at[4 + i], me.peer(0, 0, 1))
+    for n, d, half in ((0, WAYS[0], 0), (1, WAYS[1], 1), (0, WAYS[0], 1), (1, WAYS[1], 0)):
+        rows, k = (pl.ds(2 * half, 2), 2 * n + half)
+        dst = me.shard(full).at[rows]
+        sends.go(src.at[rows], dst, send_sems.at[k], recv_sems.at[k], me.peer(*d))
+    sends.go(src, me.shard(full), send_sems.at[4], recv_sems.at[4], me.peer(0, 0, 1))
+
+
+def spread_relay(me, sends, full, send_sems, recv_sems):
+    for n in (0, 1):
+        rows = pl.ds(2 * n, 2)
+        part = me.shard(full, *WAYS[n]).at[rows]
+        arrived(part, recv_sems.at[3 * n])
+        sends.go(part, part, send_sems.at[5 + n], recv_sems.at[5 + n], me.peer(*WAYS[1 - n]))
+    for n in (0, 1):
+        rows = pl.ds(2 * (1 - n), 2)
+        part = me.shard(full, *WAYS[n])
+        arrived(part.at[rows], recv_sems.at[n + 1])
+        sends.go(part, part, send_sems.at[7 + n], recv_sems.at[7 + n], me.peer(0, 0, 1))
+
+
+def spread_far(me, sends, full, send_sems, recv_sems):
+    for n in (0, 1):
+        part = me.shard(full, 1, 1, 0).at[pl.ds(2 * n, 2)]
+        arrived(part, recv_sems.at[5 + n])
+        sends.go(part, part, send_sems.at[9 + n], recv_sems.at[9 + n], me.peer(0, 0, 1))
 
 
 def spread_finish(me, full, recv_sems):
-    for i, (dx, dy, _) in enumerate([(0, 0, 0)] + FAR):
-        arrived(me.shard(full, dx, dy, 1), recv_sems.at[3 + i])
+    arrived(me.shard(full, 0, 0, 1), recv_sems.at[4])
+    for n in (0, 1):
+        arrived(me.shard(full, *WAYS[n][:2], 1), recv_sems.at[7 + n])
+        arrived(me.shard(full, 1, 1, 1).at[pl.ds(2 * n, 2)], recv_sems.at[9 + n])
+
+
+PIECES = (0, 1, 3, 2)
+
+
+def piece_start(me, sends, full, turn, send_sems, recv_sems):
+    part = full.at[me.block, (me.z + turn) % 4, me.x]
+    for n, d in enumerate(WAYS + [(0, 0, 1)]):
+        k = 4 * n + turn
+        sends.go(part, part, send_sems.at[k], recv_sems.at[k], me.peer(*d))
+
+
+def piece_relay(me, sends, full, send_sems, recv_sems):
+    for turn in PIECES:
+        n = int(turn > 1)
+        for way in (n, 1 - n):
+            x, y, c = me.coords(*WAYS[way])
+            part = full.at[2 * y + c, (me.z + turn) % 4, x]
+            k = 4 * way + turn
+            arrived(part, recv_sems.at[k])
+            if way == n:
+                sends.go(part, part, send_sems.at[12 + turn], recv_sems.at[12 + turn], me.peer(*WAYS[1 - n]))
+            sends.go(part, part, send_sems.at[16 + k], recv_sems.at[16 + k], me.peer(0, 0, 1))
+
+
+def piece_far(me, sends, full, send_sems, recv_sems):
+    for turn in PIECES:
+        x, y, c = me.coords(1, 1, 0)
+        part = full.at[2 * y + c, (me.z + turn) % 4, x]
+        arrived(part, recv_sems.at[12 + turn])
+        sends.go(part, part, send_sems.at[24 + turn], recv_sems.at[24 + turn], me.peer(0, 0, 1))
+
+
+def piece_finish(me, full, recv_sems):
+    for n, (dx, dy) in enumerate(((0, 0), (1, 0), (0, 1), (1, 1))):
+        x, y, c = me.coords(dx, dy, 1)
+        for turn in PIECES:
+            arrived(full.at[2 * y + c, (me.z + turn) % 4, x], recv_sems.at[(8, 16, 20, 24)[n] + turn])
 
 
 def full_shape(tokens, width):
@@ -508,6 +555,19 @@
     for dz in (2, 1):
         sends.go_if(me.z < 4 - dz, src, part(me.z), sems.at[0, dz - 1], sems.at[1, dz - 1], me.line(dz))
         sends.go_if(me.z >= dz, src, part(me.z), sems.at[0, dz + 1], sems.at[1, dz + 1], me.line(4 - dz))
+
+
+def line_spread_first(me, sends, src, part, sems, second=False):
+    outer, inner = outer_inner(me)
+    for dz in (2, 1):
+        for up in (True, False):
+            fits = me.z < 4 - dz if up else me.z >= dz
+            outward = me.z == 2 if up else me.z == 1
+            early = jnp.logical_or(outer, outward) if dz == 1 else outer
+            now = jnp.logical_not(early) if second else early
+            k = dz - 1 if up else dz + 1
+            target = me.line(dz) if up else me.line(4 - dz)
+            sends.go_if(jnp.logical_and(fits, now), src, part(me.z), sems.at[0, k], sems.at[1, k], target)
 
 
 def line_forward(me, sends, part, sems):
@@ -646,22 +706,49 @@
             sends.pending.append((other, copy))
 
 
+HALVES = (slice(0, 2), slice(2, 4))
+
+
+def half_own(me, part, i, dims):
+    x, y, c = me.coords(*(FAR + [(0, 0, 0)])[i])
+    ref, sibling = part
+    return ref[2 * y + c, dims, x].astype(jnp.float32) + sibling[i, dims].astype(jnp.float32)
+
+
 def half_out(me, sends, part, sibling, out, came, send_sems, recv_sems):
-    for i, d in enumerate(FAR):
-        x, y, c = me.coords(*d)
-        arrived(sibling.at[i], recv_sems.at[i])
-        own = part[2 * y + c, :, x].astype(jnp.float32)
-        out[i] = (own + sibling[i].astype(jnp.float32)).astype(jnp.bfloat16)
-        sends.go(out.at[i], came.at[i], send_sems.at[4 + i], recv_sems.at[4 + i], me.peer(*d))
+    low, both = (out.dtype, (part, sibling))
+    near = (me.peer(1, 0, 0), me.peer(0, 1, 0))
+    arrived(sibling.at[0], recv_sems.at[0])
+    out[0] = half_own(me, both, 0, slice(None)).astype(low)
+    for n, dims in enumerate(HALVES):
+        half = pl.ds(2 * n, 2)
+        sends.go(out.at[0, half], came.at[0, half], send_sems.at[4 + n], recv_sems.at[4 + n], near[n])
+    for n, dims in enumerate(HALVES):
+        arrived(sibling.at[1 + n], recv_sems.at[1 + n])
+        out[1 + n, dims] = half_own(me, both, 1 + n, dims).astype(low)
+        half = pl.ds(2 * n, 2)
+        k = 6 + 2 * n
+        sends.go(out.at[1 + n, half], came.at[1 + n, half], send_sems.at[k], recv_sems.at[k], near[n])
+
+
+def half_relay(me, sends, part, sibling, out, came, send_sems, recv_sems):
+    low, both = (out.dtype, (part, sibling))
+    near = (me.peer(1, 0, 0), me.peer(0, 1, 0))
+    for n in (0, 1):
+        dims, half, k = (HALVES[1 - n], pl.ds(2 * (1 - n), 2), 7 + 2 * n)
+        arrived(came.at[0, half], recv_sems.at[5 - n])
+        total = half_own(me, both, 1 + n, dims) + came[0, dims].astype(jnp.float32)
+        out[1 + n, dims] = total.astype(low)
+        sends.go(out.at[1 + n, half], came.at[1 + n, half], send_sems.at[k], recv_sems.at[k], near[n])
 
 
 def half_in(me, part, sibling, came, recv_sems):
     arrived(sibling.at[3], recv_sems.at[3])
-    total = part[me.block, :, me.x].astype(jnp.float32) + sibling[3].astype(jnp.float32)
-    for i in (1, 2, 0):
-        arrived(came.at[i], recv_sems.at[4 + i])
-        total = total + came[i].astype(jnp.float32)
-    return total
+    for n, half in ((0, 0), (1, 1), (0, 1), (1, 0)):
+        k = 6 + 2 * n + (half != n)
+        arrived(came.at[1 + n, pl.ds(2 * half, 2)], recv_sems.at[k])
+    total = half_own(me, (part, sibling), 3, slice(None))
+    return total + came[1].astype(jnp.float32) + came[2].astype(jnp.float32)
 
 
 def half_scratch(tokens, width):
@@ -670,8 +757,8 @@
         pltpu.VMEM((4,) + piece, jnp.bfloat16),
         pltpu.VMEM((3,) + piece, jnp.bfloat16),
         pltpu.VMEM((3,) + piece, jnp.bfloat16),
-        SEM((7,)),
-        SEM((7,)),
+        SEM((10,)),
+        SEM((10,)),
     ]
 
 
@@ -725,20 +812,19 @@
     x_ref, cot_ref, seg_ref, q_ref, k_ref, v_ref, g_ref, u_ref, o_ref, d_ref, gain_ref, hg_ref,
     y_ref, gx_ref, dq_ref, dk_ref, dv_ref, dg_ref, du_ref, sums_ref, osum_ref, dsum_ref,
     xf, cf, wf, of, df, guf, segs, gains, n1, nf, gf, pre, qkv, segcol, cos_s, sin_s, att, attlow,
-    totals, part, part2, part3, down, n2, gm, y_s, gi_s, mid, gmid,
+    totals, kept, part, part2, down, n2, gm, y_s, gi_s, mid, gmid,
     gates, hid, gboth, ga, gq, gk, gv, gpre, dd, dgu, do, dw,
     d_came, d_buf, gu_came, gu_buf, gu_total, gu_sum, o_came, o_buf, w_came, w_buf, w_total, w_sum,
     pack, packs, linep,
     sib1, out1, came1, hs1, hr1, sib2, out2, came2, hs2, hr2, sib3, out3, came3, hs3, hr3,
-    sib4, out4, came4, hs4, hr4,
-    ps, pr, as_, ar, ws, wr, us, ur, gs, gr, zq, zo, zd, zg, rg, rd, ro, rw, cs, cr, ds, dr, ls,
+    ps, pr, as_, ar, xas, xar, ws, wr, us, ur, gs, gr, zq, zo, zd, zg, zu, rg, rd, ro, rw, cs, cr, ds, dr, ls,
 ):
     me = Place()
     x, z, p = (me.x, me.z, me.head)
     low, wide_t = (jnp.bfloat16, jnp.float32)
     across = [((x + 1) % 2, me.block, me.ahead(turn)) for turn in TURNS]
     meet([me.peer(*d) for d in PLANE[1:]] + [me.line(turn) for turn in TURNS] + across)
-    sends = Sends()
+    sends, early = (Sends(), Sends())
 
     def local(src, dst, sem):
         copy = pltpu.make_async_copy(src, dst, sem)
@@ -764,8 +850,9 @@
                 local(src, dst, wr.at[n])
             else:
                 sends.go(src, dst, ws.at[3 * i + n], wr.at[3 * i + n], me.peer(*d))
+    ff = g_ref.shape[1] // 8
     arrived(xf.at[me.block, z, x], pr.at[0, z])
-    spread_piece(me, xf, z, as_.at[0], ar.at[0])
+    piece_start(me, sends, xf, 0, xas, xar)
     for i, d in enumerate(PLANE):
         t = me.index(*d)
         for n, (ref, width, off) in enumerate(cuts):
@@ -773,13 +860,15 @@
     qkv_part = lambda k: wf.at[:, k]
     o_part = lambda k: of.at[k]
     d_part = lambda k: df.at[k]
-    gu_part = lambda k: guf.at[:, k]
-    line_spread(me, sends, qkv_part(z), qkv_part, zq)
+    gate_part = lambda k: guf.at[:, k, :, pl.ds(0, ff)]
+    up_part = lambda k: guf.at[:, k, :, pl.ds(ff, ff)]
+    line_spread_first(me, sends, qkv_part(z), qkv_part, zq)
     for turn in (1, 3, 2):
         k = (z + turn) % 4
         arrived(xf.at[me.block, k, x], pr.at[0, k])
-        spread_piece(me, xf, k, as_.at[0], ar.at[0])
-    spread_pieces_sent(me, sends, xf, as_.at[0], ar.at[0])
+        piece_start(me, sends, xf, turn, xas, xar)
+    line_spread_first(me, sends, qkv_part(z), qkv_part, zq, second=True)
+    piece_relay(me, sends, xf, xas, xar)
     own_gain.wait()
     for turn in TURNS:
         arrived(gains.at[p, me.behind(turn)], gr.at[turn])
@@ -788,7 +877,6 @@
     line_forward(me, sends, qkv_part, zq)
     permute_in(me, cot_ref, cf, ps.at[1], pr.at[1])
     line_spread(me, sends, o_ref, o_part, zo)
-    ff = g_ref.shape[1] // 8
     for i, d in enumerate(PLANE):
         t = me.index(*d)
         for n, ref in enumerate((g_ref, u_ref)):
@@ -826,11 +914,11 @@
             sd = jnp.where(column == doc, doc_sin[doc], sd)
         cos_s[b] = cos_at * cd + sin_at * sd
         sin_s[b] = sin_at * cd - cos_at * sd
+    piece_far(me, sends, xf, xas, xar)
     for i, d in enumerate(PLANE[1:]):
         arrived(gains.at[me.index(*d)], gr.at[4 + i])
     gain_one, gain_two = (gain_row(gains, 0), gain_row(gains, 1))
-    spread_forward(me, sends, xf, as_.at[0], ar.at[0])
-    spread_finish(me, xf, ar.at[0])
+    piece_finish(me, xf, xar)
 
     @pl.loop(0, 4)
     def _(b):
@@ -839,6 +927,14 @@
 
     line_finish(me, qkv_part, zq)
 
+    own_o.wait()
+    line_forward(me, sends, o_part, zo)
+    for i, d in enumerate(PLANE):
+        t = me.index(*d)
+        for n in (0, 1):
+            arrived(guf.at[t, z, :, pl.ds(n * ff, ff)], ur.at[2 * i + n])
+    line_spread(me, sends, gate_part(z), gate_part, zg)
+    line_spread(me, sends, up_part(z), up_part, zu)
     @pl.loop(0, 4)
     def _(b):
         rows = mat(n1[b], wf[...].reshape(-1, wf.shape[3]))
@@ -852,14 +948,6 @@
 
     permuted_in(me, cf, pr.at[1])
     spread_start(me, sends, me.shard(cf), cf, as_.at[1], ar.at[1])
-    own_o.wait()
-    line_forward(me, sends, o_part, zo)
-    for i, d in enumerate(PLANE):
-        t = me.index(*d)
-        for n in (0, 1):
-            arrived(guf.at[t, z, :, pl.ds(n * ff, ff)], ur.at[2 * i + n])
-    line_spread(me, sends, gu_part(z), gu_part, zg)
-    line_spread(me, sends, d_ref, d_part, zd)
     top = lambda r: jnp.max(jnp.abs(hg_ref[pl.ds(r, 1), :]), axis=1, keepdims=True)
     bound = math.sqrt(head_dim) * top(0) * top(1)
     scale = head_dim ** (-0.5)
@@ -879,6 +967,7 @@
             for kb in range(b + 1):
                 w = weights_of(b, kb, query)
                 t = jnp.sum(w, axis=1, keepdims=True)
+                kept[h, b * (b + 1) // 2 + kb] = w.astype(low)
                 m = mat(w.astype(low), qkv[kb, :, value_at])
                 total = t if kb == 0 else total + t
                 mixed = m if kb == 0 else mixed + m
@@ -896,21 +985,25 @@
         half_block(me, part, sib1, hs1, hr1, b)
 
     for b in range(4):
-        half_block(me, part, sib1, hs1, hr1, b, sends)
-    half_out(me, sends, part, sib1, out1, came1, hs1, hr1)
-    spread_forward(me, sends, cf, as_.at[1], ar.at[1])
+        half_block(me, part, sib1, hs1, hr1, b, early)
+    half_out(me, early, part, sib1, out1, came1, hs1, hr1)
+    line_forward(me, sends, gate_part, zg)
+    half_relay(me, early, part, sib1, out1, came1, hs1, hr1)
+    spread_relay(me, sends, cf, as_.at[1], ar.at[1])
     middle = xf[me.block, :, x].astype(wide_t) + half_in(me, part, sib1, came1, hr1)
     mid[...] = middle
     n2[...] = (middle * head_scale(middle) * gain_two).astype(low)
     own_n = local(n2, me.shard(nf), ls.at[6])
     spread_start(me, sends, n2, nf, as_.at[2], ar.at[2])
-    line_forward(me, sends, gu_part, zg)
-    spread_forward(me, sends, nf, as_.at[2], ar.at[2], (1, 2))
+    line_forward(me, sends, up_part, zu)
+    line_spread(me, sends, d_ref, d_part, zd)
+    spread_relay(me, sends, nf, as_.at[2], ar.at[2])
     line_forward(me, sends, d_part, zd)
-    spread_forward(me, sends, nf, as_.at[2], ar.at[2], (0,))
+    spread_far(me, sends, nf, as_.at[2], ar.at[2])
     spread_finish(me, nf, ar.at[2])
     own_n.wait()
-    line_finish(me, gu_part, zg)
+    line_finish(me, gate_part, zg)
+    line_finish(me, up_part, zu)
 
     @pl.loop(0, 4)
     def _(b):
@@ -919,6 +1012,7 @@
         gate, up = (both[:, :ff], both[:, ff:])
         hid[b] = (gate / (1.0 + jnp.exp(-gate)) * up).astype(low)
 
+    spread_far(me, sends, cf, as_.at[1], ar.at[1])
     spread_finish(me, cf, ar.at[1])
     own_d.wait()
     dd[...] = mat_left(hid[...].reshape(-1, ff), cf[...].reshape(tokens, -1)).astype(low).reshape(dd.shape)
@@ -950,6 +1044,7 @@
 
     own_gu = lambda k: dgu.at[:, k]
     reduce_start(me, sends, own_gu, gu_came, rg)
+    half_relay(me, sends, part2, sib2, out2, came2, hs2, hr2)
     reduce_join(me, sends, own_dd, d_came, d_buf, rd)
     grad = half_in(me, part2, sib2, came2, hr2)
     middle = mid[...]
@@ -971,13 +1066,14 @@
 
     for b in range(4):
         half_block(me, down, sib3, hs3, hr3, b, sends)
+    spread_relay(me, sends, gf, as_.at[3], ar.at[3])
     half_out(me, sends, down, sib3, out3, came3, hs3, hr3)
-    spread_forward(me, sends, gf, as_.at[3], ar.at[3], (1, 2))
     reduce_join(me, sends, own_gu, gu_came, gu_buf, rg)
-    spread_forward(me, sends, gf, as_.at[3], ar.at[3], (0,))
+    spread_far(me, sends, gf, as_.at[3], ar.at[3])
     spread_finish(me, gf, ar.at[3])
     own_gm.wait()
 
+    half_relay(me, sends, down, sib3, out3, came3, hs3, hr3)
     gk[...] = jnp.zeros_like(gk)
     gv[...] = jnp.zeros_like(gv)
     for b in range(4):
@@ -987,17 +1083,19 @@
         def _(h, b=b):
             at = pl.ds(pl.multiple_of(head_dim * h, head_dim), head_dim)
             query, grad = (qkv[b, :, at], ga[b, :, at])
-            delta = jnp.sum(grad.astype(wide_t) * att[b, :, at], axis=1, keepdims=True)
             inv = 1.0 / totals[b, h]
+            scaled = grad.astype(wide_t) * inv
+            delta = jnp.sum(scaled * att[b, :, at], axis=1, keepdims=True)
+            scaled = scaled.astype(low)
             grad_query = None
             for kb in range(b + 1):
-                probs = weights_of(b, kb, query) * inv
-                gp = mat_right(grad, qkv[kb, :, value_at])
-                gsc = (probs * (gp - delta)).astype(low)
+                w = kept[h, b * (b + 1) // 2 + kb]
+                gp = mat_right(scaled, qkv[kb, :, value_at])
+                gsc = (w.astype(wide_t) * (gp - delta)).astype(low)
                 m = mat(gsc, qkv[kb, :, key_at])
                 grad_query = m if kb == 0 else grad_query + m
                 gk[kb] += mat_left(gsc, query)
-                gv[kb] += mat_left(probs.astype(low), grad)
+                gv[kb] += mat_left(w, scaled)
             gq[b, :, at] = grad_query
 
         if b == 2:
@@ -1024,6 +1122,17 @@
             gpre[b, :, at] = (r * (gn - n * jnp.mean(gn * n, axis=-1, keepdims=True))).astype(low)
         gpre[b, :, value_at] = gv[b].astype(low)
 
+    early.drain()
+
+    @pl.loop(0, 4)
+    def _(b):
+        rows = mat_right(gpre[b], wf[...].reshape(-1, wf.shape[3])).astype(low)
+        part[b] = rows.reshape(part.shape[1:])
+        half_block(me, part, sib1, hs1, hr1, b)
+
+    for b in range(4):
+        half_block(me, part, sib1, hs1, hr1, b, sends)
+    half_out(me, sends, part, sib1, out1, came1, hs1, hr1)
     @pl.loop(0, 4)
     def _(b):
         rows = n1[:, :, pl.ds(pl.multiple_of(256 * b, 256), 256)].reshape(-1, 256)
@@ -1032,16 +1141,7 @@
 
     own_dw = lambda k: dw.at[:, k]
     reduce_start(me, sends, own_dw, w_came, rw)
-
-    @pl.loop(0, 4)
-    def _(b):
-        rows = mat_right(gpre[b], wf[...].reshape(-1, wf.shape[3])).astype(low)
-        part3[b] = rows.reshape(part3.shape[1:])
-        half_block(me, part3, sib4, hs4, hr4, b)
-
-    for b in range(4):
-        half_block(me, part3, sib4, hs4, hr4, b, sends)
-    half_out(me, sends, part3, sib4, out4, came4, hs4, hr4)
+    half_relay(me, sends, part, sib1, out1, came1, hs1, hr1)
     reduce_join(me, sends, own_do, o_came, o_buf, ro)
     reduce_total(me, own_gu, gu_came, gu_total, rg)
     gu_sum[...] = gu_total[...].astype(low)
@@ -1056,15 +1156,22 @@
                 sends.go(src, dst, ds.at[2 * i + n], dr.at[2 * i + n], me.peer(*d))
     reduce_total(me, own_dd, d_came, dsum_ref, rd)
     reduce_join(me, sends, own_dw, w_came, w_buf, rw)
-    grad = half_in(me, part3, sib4, came4, hr4)
+    grad = half_in(me, part, sib1, came1, hr1)
     rows = xf[me.block, :, x].astype(wide_t)
     r = head_scale(rows)
     share = total_row(grad * rows * r)
     for i in range(8):
         pack[pl.ds(i, 1)] = share[:, 128 * i : 128 * i + 128]
+    for i, d in enumerate(PLANE[1:]):
+        sends.go(pack, packs.at[i], gs.at[11 + i], gr.at[11 + i], me.peer(*d))
+    gi_s[...] = (gmid[...] + norm_back(grad, rows, gain_one, r)).astype(low)
+    total = pack[...]
+    for i in range(7):
+        arrived(packs.at[i], gr.at[11 + i])
+        total = total + packs[i]
+    packs[7] = total
     for turn in TURNS:
-        sends.go(pack, linep.at[turn - 1], gs.at[17 + turn], gr.at[17 + turn], me.line(turn))
-    gi_s[...] = (gmid[...] + norm_back(grad, rows, gain_one, r)).astype(low)
+        sends.go(packs.at[7], linep.at[turn - 1], gs.at[17 + turn], gr.at[17 + turn], me.line(turn))
     permute_out(me, gi_s, gx_ref, cs.at[1], cr.at[1])
     reduce_total(me, own_dw, w_came, w_total, rw)
     w_sum[...] = w_total[...].astype(low)
@@ -1079,17 +1186,10 @@
             else:
                 s = 16 + 3 * i + n
                 sends.go(src, dst, ds.at[s], dr.at[s], me.peer(*d))
-    total = pack[...]
+    reduce_total(me, own_do, o_came, osum_ref, ro)
     for turn in TURNS:
         arrived(linep.at[turn - 1], gr.at[17 + turn])
         total = total + linep[turn - 1]
-    packs[7] = total
-    for i, d in enumerate(PLANE[1:]):
-        sends.go(packs.at[7], packs.at[i], gs.at[11 + i], gr.at[11 + i], me.peer(*d))
-    reduce_total(me, own_do, o_came, osum_ref, ro)
-    for i in range(7):
-        arrived(packs.at[i], gr.at[11 + i])
-        total = total + packs[i]
     sums_ref[...] = total
     for i, d in enumerate(PLANE):
         t = me.index(*d)
@@ -1133,7 +1233,7 @@
             buf((8, 4, 8, 128), wide), blocks(width, low), buf(full, low), buf(full, low),
             blocks(cols, wide), blocks(cols, low), blocks(1, jnp.int32), blocks(head_dim, wide),
             blocks(head_dim, wide), blocks(att_cols, wide), blocks(att_cols, low),
-            buf((4, 2, quarter, 1), wide), buf(full, low), buf(full, low), buf(full, low), buf(full, low),
+            buf((4, 2, quarter, 1), wide), buf((2, 10, quarter, quarter), low), buf(full, low), buf(full, low), buf(full, low),
             buf(piece, low), buf(piece, low), buf(piece, low), buf(piece, low), buf(piece, wide),
             buf(piece, wide),
             blocks(2 * ff, wide), blocks(ff, low), blocks(2 * ff, low), blocks(att_cols, low), blocks(att_cols, wide),
@@ -1148,10 +1248,10 @@
             buf((8, rows, cols), low),
             buf((24, 128), wide), buf((8, 24, 128), wide), buf((3, 24, 128), wide),
         ]
-        + half_scratch(tokens, width) * 4
-        + [SEM((2, 4)), SEM((2, 4)), SEM((4, 7)), SEM((4, 7)), SEM((24,)), SEM((24,)), SEM((16,)), SEM((16,))]
+        + half_scratch(tokens, width) * 3
+        + [SEM((2, 4)), SEM((2, 4)), SEM((4, 11)), SEM((4, 11)), SEM((28,)), SEM((28,)), SEM((24,)), SEM((24,)), SEM((16,)), SEM((16,))]
         + [SEM((21,)), SEM((21,))]
-        + [SEM((2, 6))] * 4
+        + [SEM((2, 5))] * 5
         + [SEM((2, 4))] * 4
         + [SEM((2, 4)), SEM((2, 4)), SEM((40,)), SEM((40,)), SEM((8,))],
         compiler_params=pltpu.CompilerParams(

time: 190 us -> 180 us (0.947)
  Pallas kernels: 183 us -> 174 us
    pallas_call x1, Pallas kernels: 180 us -> 171 us  [layer_step(): pl.pallas_call(layer_kernel, name='layer_step', out_shape=(shape(x.shape,...]
where the time goes in v5:
time: 180 us
  Pallas kernels  174 us (97%)
  local copies, waits for them, and re-layouts  4.5 us (2%)
    pallas_call x1, Pallas kernels, layer_step(): pl.pallas_call(layer_kernel, name='layer_step', out_shape=(shape(x.shape,...  171 us

profile of v5, /device:TPU:0, one launch (start us, length us, event | category | flops | bytes accessed | tf_op | source)
XLA Modules:
  0.0 179.7 jit_solution(7002390983756509831)
XLA Ops:
  0.7 0.0 copy-start
  0.7 0.0 copy-start.1
  0.7 0.6 copy-done
  1.3 0.0 copy-done.1
  1.3 0.0 copy-start.2
  1.3 0.6 copy-done.2
  2.0 0.6 convert_element_type.11.hg_ref
  2.6 0.1 tile.10
  2.6 0.6 concatenate.7.gain_ref
  3.2 171.0 %layer_step.1 = (bf16[2,64,1024]{2,1,0:T(8,128)(2,1)}, bf16[2,64,1024]{2,1,0:T(8,128)(2,1)}, bf16[32,2048]{1,0:T(8,128)(2,1)}, bf16[32,1024]{1,0:T(8,128)(2,1)},...) custom-call(bf16[2,64,1024]{2,1,0:T(8,128)(2,1)} %x_ref.1, ...), custom_call_target="tpu_custom_call" | custom-call | tf_op jit(solution)/shard_map/layer_step/pallas_call | solution.py:1220
  174.2 3.0 %finish_step.1 = (bf16[2,64,1024]{2,1,0:T(8,128)(2,1)}, bf16[2,64,1024]{2,1,0:T(8,128)(2,1)}, f32[32,2048]{1,0:T(8,128)}, f32[32,1024]{1,0:T(8,128)}, f32[32,102...) custom-call(f32[24,128]{1,0:T(8,128)} %get-tuple-element.32.sums_ref, ...), custom_call_target="tpu_custom_call" | custom-call | tf_op jit(solution)/shard_map/finish_step/pallas_call | solution.py:1279
  177.2 1.2 slice.10
  178.5 1.3 slice_bitcast_fusion
  (4 shorter events, 0.0 us)
Async XLA Ops:
  0.7 0.7 copy-start
  0.7 0.7 copy-start.1
  1.3 0.7 copy-start.2

commit v6 on v5

--- a/solution.py
+++ b/solution.py
@@ -519,8 +519,8 @@
         sends.go(part, part, send_sems.at[k], recv_sems.at[k], me.peer(*d))
 
 
-def piece_relay(me, sends, full, send_sems, recv_sems):
-    for turn in PIECES:
+def piece_relay(me, sends, full, send_sems, recv_sems, turns):
+    for turn in turns:
         n = int(turn > 1)
         for way in (n, 1 - n):
             x, y, c = me.coords(*WAYS[way])
@@ -604,15 +604,17 @@
     return (outer, jnp.logical_not(outer))
 
 
-def reduce_start(me, sends, own, came, sems):
+def reduce_start(me, sends, own, came, sems, joins=True, rest=True):
     z = me.z
     outer, _ = outer_inner(me)
-    nearer = line_to(me, 1 + z // 3)
-    sends.go_if(outer, own((7 - z) % 4), came.at[3], sems.at[0, 3], sems.at[1, 3], nearer)
-    far = (z + 2) % 4
-    sends.go_if(outer, own(far), came.at[2], sems.at[0, 2], sems.at[1, 2], line_to(me, far))
-    sends.go_if(z < 3, own((z + 1) % 4), came.at[0], sems.at[0, 0], sems.at[1, 0], me.line(1))
-    sends.go_if(z > 0, own((z + 3) % 4), came.at[1], sems.at[0, 1], sems.at[1, 1], me.line(3))
+    if joins:
+        nearer = line_to(me, 1 + z // 3)
+        sends.go_if(outer, own((7 - z) % 4), came.at[3], sems.at[0, 3], sems.at[1, 3], nearer)
+    if rest:
+        far = (z + 2) % 4
+        sends.go_if(outer, own(far), came.at[2], sems.at[0, 2], sems.at[1, 2], line_to(me, far))
+        sends.go_if(z < 3, own((z + 1) % 4), came.at[0], sems.at[0, 0], sems.at[1, 0], me.line(1))
+        sends.go_if(z > 0, own((z + 3) % 4), came.at[1], sems.at[0, 1], sems.at[1, 1], me.line(3))
 
 
 def reduce_join(me, sends, own, came, buf, sems):
@@ -809,15 +811,15 @@
 
 
 def layer_kernel(
-    x_ref, cot_ref, seg_ref, q_ref, k_ref, v_ref, g_ref, u_ref, o_ref, d_ref, gain_ref, hg_ref,
-    y_ref, gx_ref, dq_ref, dk_ref, dv_ref, dg_ref, du_ref, sums_ref, osum_ref, dsum_ref,
+    x_ref, cot_ref, seg_ref, q_ref, k_ref, v_ref, g_ref, u_ref, o_ref, d_ref, ag_ref, fg_ref, hg_in,
+    y_ref, gx_ref, dq_ref, dk_ref, dv_ref, dg_ref, du_ref, sums_ref, osum_out, dsum_out,
     xf, cf, wf, of, df, guf, segs, gains, n1, nf, gf, pre, qkv, segcol, cos_s, sin_s, att, attlow,
     totals, kept, part, part2, down, n2, gm, y_s, gi_s, mid, gmid,
     gates, hid, gboth, ga, gq, gk, gv, gpre, dd, dgu, do, dw,
     d_came, d_buf, gu_came, gu_buf, gu_total, gu_sum, o_came, o_buf, w_came, w_buf, w_total, w_sum,
     pack, packs, linep,
     sib1, out1, came1, hs1, hr1, sib2, out2, came2, hs2, hr2, sib3, out3, came3, hs3, hr3,
-    ps, pr, as_, ar, xas, xar, ws, wr, us, ur, gs, gr, zq, zo, zd, zg, zu, rg, rd, ro, rw, cs, cr, ds, dr, ls,
+    ps, pr, as_, ar, xas, xar, ws, wr, us, ur, gs, gr, zq, zo, zd, zg, zu, rg, rd, ro, rw, cs, cr, ds, dr, ls, raw1, raw2, hg_low, hg_ref, osum_ref, dsum_ref,
 ):
     me = Place()
     x, z, p = (me.x, me.z, me.head)
@@ -831,12 +833,12 @@
         copy.start()
         return copy
 
-    own_gain = local(gain_ref, gains.at[p, z], ls.at[0])
+    own_raw = [local(ref, dst, ls.at[6 + i]) for i, (ref, dst) in enumerate(((ag_ref, raw1), (fg_ref, raw2)))]
+    own_head = local(hg_in, hg_low, ls.at[0])
     own_seg = local(seg_ref, segs.at[x], ls.at[1])
     sends.go(seg_ref, segs.at[x], ls.at[2], ls.at[3], me.peer(1, 0, 0))
-    for turn in TURNS:
-        sends.go(gain_ref, gains.at[p, z], gs.at[turn], gr.at[turn], me.line(turn))
     permute_in(me, x_ref, xf, ps.at[0], pr.at[0])
+    permute_in(me, cot_ref, cf, ps.at[1], pr.at[1])
     own_o = local(o_ref, of.at[z], ls.at[4])
     own_d = local(d_ref, df.at[z], ls.at[5])
     wide, narrow = (q_ref.shape[1] // 8, k_ref.shape[1] // 8)
@@ -851,8 +853,18 @@
             else:
                 sends.go(src, dst, ws.at[3 * i + n], wr.at[3 * i + n], me.peer(*d))
     ff = g_ref.shape[1] // 8
+    for copy in own_raw + [own_head]:
+        copy.wait()
+    hg_ref[...] = hg_low[...].astype(wide_t)
+    piece = raw1.shape[1]
+    rows = [raw1[...].astype(wide_t), raw2[...].astype(wide_t), jnp.zeros((6, piece), wide_t)]
+    rows = [jnp.concatenate(rows, axis=0), jnp.zeros((8, 128 - piece), wide_t)]
+    rows = jnp.concatenate(rows, axis=1)
+    gains[p, z] = pltpu.roll(rows, piece * z, 1)
     arrived(xf.at[me.block, z, x], pr.at[0, z])
     piece_start(me, sends, xf, 0, xas, xar)
+    for turn in TURNS:
+        sends.go(gains.at[p, z], gains.at[p, z], gs.at[turn], gr.at[turn], me.line(turn))
     for i, d in enumerate(PLANE):
         t = me.index(*d)
         for n, (ref, width, off) in enumerate(cuts):
@@ -868,15 +880,14 @@
         arrived(xf.at[me.block, k, x], pr.at[0, k])
         piece_start(me, sends, xf, turn, xas, xar)
     line_spread_first(me, sends, qkv_part(z), qkv_part, zq, second=True)
-    piece_relay(me, sends, xf, xas, xar)
-    own_gain.wait()
+    line_spread(me, sends, o_ref, o_part, zo)
+    piece_relay(me, sends, xf, xas, xar, PIECES[:2])
+    line_forward(me, sends, qkv_part, zq)
+    piece_relay(me, sends, xf, xas, xar, PIECES[2:])
     for turn in TURNS:
         arrived(gains.at[p, me.behind(turn)], gr.at[turn])
     for i, d in enumerate(PLANE[1:]):
         sends.go(gains.at[p], gains.at[p], gs.at[4 + i], gr.at[4 + i], me.peer(*d))
-    line_forward(me, sends, qkv_part, zq)
-    permute_in(me, cot_ref, cf, ps.at[1], pr.at[1])
-    line_spread(me, sends, o_ref, o_part, zo)
     for i, d in enumerate(PLANE):
         t = me.index(*d)
         for n, ref in enumerate((g_ref, u_ref)):
@@ -886,6 +897,8 @@
                 local(src, dst, ur.at[n])
             else:
                 sends.go(src, dst, us.at[2 * i + n], ur.at[2 * i + n], me.peer(*d))
+    permuted_in(me, cf, pr.at[1])
+    spread_start(me, sends, me.shard(cf), cf, as_.at[1], ar.at[1])
     own_seg.wait()
     arrived(segs.at[(x + 1) % 2], ls.at[3])
     head_dim = hg_ref.shape[1]
@@ -935,6 +948,7 @@
             arrived(guf.at[t, z, :, pl.ds(n * ff, ff)], ur.at[2 * i + n])
     line_spread(me, sends, gate_part(z), gate_part, zg)
     line_spread(me, sends, up_part(z), up_part, zu)
+    spread_relay(me, sends, cf, as_.at[1], ar.at[1])
     @pl.loop(0, 4)
     def _(b):
         rows = mat(n1[b], wf[...].reshape(-1, wf.shape[3]))
@@ -946,8 +960,6 @@
             qkv[b, :, pl.ds(head_dim * h, head_dim)] = (n * cosine + turned(n) * sine).astype(low)
         qkv[b, :, pl.ds(3 * head_dim, head_dim)] = rows[:, 3 * head_dim :].astype(low)
 
-    permuted_in(me, cf, pr.at[1])
-    spread_start(me, sends, me.shard(cf), cf, as_.at[1], ar.at[1])
     top = lambda r: jnp.max(jnp.abs(hg_ref[pl.ds(r, 1), :]), axis=1, keepdims=True)
     bound = math.sqrt(head_dim) * top(0) * top(1)
     scale = head_dim ** (-0.5)
@@ -989,11 +1001,10 @@
     half_out(me, early, part, sib1, out1, came1, hs1, hr1)
     line_forward(me, sends, gate_part, zg)
     half_relay(me, early, part, sib1, out1, came1, hs1, hr1)
-    spread_relay(me, sends, cf, as_.at[1], ar.at[1])
     middle = xf[me.block, :, x].astype(wide_t) + half_in(me, part, sib1, came1, hr1)
     mid[...] = middle
     n2[...] = (middle * head_scale(middle) * gain_two).astype(low)
-    own_n = local(n2, me.shard(nf), ls.at[6])
+    own_n = local(n2, me.shard(nf), ls.at[8])
     spread_start(me, sends, n2, nf, as_.at[2], ar.at[2])
     line_forward(me, sends, up_part, zu)
     line_spread(me, sends, d_ref, d_part, zd)
@@ -1052,7 +1063,7 @@
     total = cf[me.block, :, x].astype(wide_t) + norm_back(grad, middle, gain_two, r)
     gmid[...] = total
     gm[...] = total.astype(low)
-    own_gm = local(gm, me.shard(gf), ls.at[7])
+    own_gm = local(gm, me.shard(gf), ls.at[9])
     spread_start(me, sends, gm, gf, as_.at[3], ar.at[3])
     share = total_row(grad * middle * r)
     for i in range(8):
@@ -1137,10 +1148,14 @@
     def _(b):
         rows = n1[:, :, pl.ds(pl.multiple_of(256 * b, 256), 256)].reshape(-1, 256)
         grad = mat_left(rows, gpre[...].reshape(tokens, -1)).astype(low)
-        dw[pl.ds(2 * b, 2)] = grad.reshape((2,) + dw.shape[1:])
-
-    own_dw = lambda k: dw.at[:, k]
-    reduce_start(me, sends, own_dw, w_came, rw)
+        grad = grad.reshape((2,) + dw.shape[2:-1] + (2 * dw.shape[-1],))
+        for n in (0, 1):
+            dw[n, pl.ds(2 * b, 2)] = grad[..., n * dw.shape[-1] : (n + 1) * dw.shape[-1]]
+
+    own_dw = [lambda k, n=n: dw.at[n, :, k] for n in (0, 1)]
+    for joins in (True, False):
+        for n in (0, 1):
+            reduce_start(me, sends, own_dw[n], w_came.at[n], rw.at[n], joins, not joins)
     half_relay(me, sends, part, sib1, out1, came1, hs1, hr1)
     reduce_join(me, sends, own_do, o_came, o_buf, ro)
     reduce_total(me, own_gu, gu_came, gu_total, rg)
@@ -1155,7 +1170,9 @@
             else:
                 sends.go(src, dst, ds.at[2 * i + n], dr.at[2 * i + n], me.peer(*d))
     reduce_total(me, own_dd, d_came, dsum_ref, rd)
-    reduce_join(me, sends, own_dw, w_came, w_buf, rw)
+    dsum_copy = local(dsum_ref, dsum_out, ls.at[6])
+    for n in (0, 1):
+        reduce_join(me, sends, own_dw[n], w_came.at[n], w_buf.at[n], rw.at[n])
     grad = half_in(me, part, sib1, came1, hr1)
     rows = xf[me.block, :, x].astype(wide_t)
     r = head_scale(rows)
@@ -1173,20 +1190,22 @@
     for turn in TURNS:
         sends.go(packs.at[7], linep.at[turn - 1], gs.at[17 + turn], gr.at[17 + turn], me.line(turn))
     permute_out(me, gi_s, gx_ref, cs.at[1], cr.at[1])
-    reduce_total(me, own_dw, w_came, w_total, rw)
-    w_sum[...] = w_total[...].astype(low)
-    backs = ((dq_ref, wide, 0), (dk_ref, narrow, wide), (dv_ref, narrow, wide + narrow))
-    for i, d in enumerate(PLANE):
-        t = me.index(*d)
-        for n, (ref, cols, off) in enumerate(backs):
-            src = w_sum.at[t, :, pl.ds(off, cols)]
-            dst = ref.at[:, pl.ds(pl.multiple_of(p * cols, 128), cols)]
-            if i == 0:
-                local(src, dst, dr.at[16 + n])
-            else:
-                s = 16 + 3 * i + n
-                sends.go(src, dst, ds.at[s], dr.at[s], me.peer(*d))
+    backs = (((dq_ref, wide, 0),), ((dk_ref, narrow, 0), (dv_ref, narrow, narrow)))
+    for block in (0, 1):
+        reduce_total(me, own_dw[block], w_came.at[block], w_total, rw.at[block])
+        w_sum[block] = w_total[...].astype(low)
+        for i, d in enumerate(PLANE):
+            t = me.index(*d)
+            for n, (ref, cols, off) in enumerate(backs[block]):
+                src = w_sum.at[block, t, :, pl.ds(off, cols)]
+                dst = ref.at[:, pl.ds(pl.multiple_of(p * cols, 128), cols)]
+                k = 16 + 3 * i + block + n
+                if i == 0:
+                    local(src, dst, dr.at[k])
+                else:
+                    sends.go(src, dst, ds.at[k], dr.at[k], me.peer(*d))
     reduce_total(me, own_do, o_came, osum_ref, ro)
+    osum_copy = local(osum_ref, osum_out, ls.at[7])
     for turn in TURNS:
         arrived(linep.at[turn - 1], gr.at[17 + turn])
         total = total + linep[turn - 1]
@@ -1195,8 +1214,10 @@
         t = me.index(*d)
         for n, ref in enumerate((dg_ref, du_ref)):
             arrived(ref.at[:, pl.ds(pl.multiple_of(t * ff, 128), ff)], dr.at[2 * i + n])
-        for n, (ref, cols, off) in enumerate(backs):
+        for n, (ref, cols, off) in enumerate(backs[0] + backs[1]):
             arrived(ref.at[:, pl.ds(pl.multiple_of(t * cols, 128), cols)], dr.at[16 + 3 * i + n])
+    dsum_copy.wait()
+    osum_copy.wait()
     permuted_out(y_ref, cr.at[0])
     permuted_out(gx_ref, cr.at[1])
     permute_in(me, x_ref, xf, ps.at[0], pr.at[0], wait=True)
@@ -1206,7 +1227,7 @@
     sends.drain()
 
 
-def layer_step(x, cot, seg, q, k, v, g, u, o, d, gain, head_gains):
+def layer_step(x, cot, seg, q, k, v, g, u, o, d, gain, gain_two, head_gains):
     tokens, width = (16 * x.shape[1], x.shape[2])
     rows, low, wide = (q.shape[0], jnp.bfloat16, jnp.float32)
     cols = (q.shape[1] + 2 * k.shape[1]) // 8
@@ -1225,8 +1246,8 @@
             shape(v.shape, low), shape(g.shape, low), shape(u.shape, low), shape((24, 128), wide),
             shape(o.shape, wide), shape(d.shape, wide),
         ),
-        in_specs=[ANY] * 11 + [VMEM],
-        out_specs=(ANY,) * 7 + (VMEM,) * 3,
+        in_specs=[ANY] * 13,
+        out_specs=(ANY,) * 7 + (VMEM, ANY, ANY),
         scratch_shapes=[
             buf(full, low), buf(full, low), buf((8, 4, rows, cols), low), buf((4,) + o.shape, low),
             buf((4,) + d.shape, low), buf((8, 4, rows, 2 * ff), low), buf((2,) + seg.shape, seg.dtype),
@@ -1239,52 +1260,55 @@
             blocks(2 * ff, wide), blocks(ff, low), blocks(2 * ff, low), blocks(att_cols, low), blocks(att_cols, wide),
             blocks(head_dim, wide), blocks(head_dim, wide), blocks(cols, low),
             buf((4,) + d.shape, low), buf((8, 4, rows, 2 * ff), low), buf((4,) + o.shape, low),
-            buf((8, 4, rows, cols), low),
+            buf((2, 8, 4, rows, cols // 2), low),
             buf((4,) + d.shape, low), buf(d.shape, low),
             buf((4, 8, rows, 2 * ff), low), buf((8, rows, 2 * ff), low), buf((8, rows, 2 * ff), wide),
             buf((8, rows, 2 * ff), low),
             buf((4,) + o.shape, low), buf(o.shape, low),
-            buf((4, 8, rows, cols), low), buf((8, rows, cols), low), buf((8, rows, cols), wide),
-            buf((8, rows, cols), low),
+            buf((2, 4, 8, rows, cols // 2), low), buf((2, 8, rows, cols // 2), low),
+            buf((8, rows, cols // 2), wide), buf((2, 8, rows, cols // 2), low),
             buf((24, 128), wide), buf((8, 24, 128), wide), buf((3, 24, 128), wide),
         ]
         + half_scratch(tokens, width) * 3
         + [SEM((2, 4)), SEM((2, 4)), SEM((4, 11)), SEM((4, 11)), SEM((28,)), SEM((28,)), SEM((24,)), SEM((24,)), SEM((16,)), SEM((16,))]
         + [SEM((21,)), SEM((21,))]
         + [SEM((2, 5))] * 5
-        + [SEM((2, 4))] * 4
-        + [SEM((2, 4)), SEM((2, 4)), SEM((40,)), SEM((40,)), SEM((8,))],
+        + [SEM((2, 4))] * 3
+        + [SEM((2, 2, 4))]
+        + [SEM((2, 4)), SEM((2, 4)), SEM((40,)), SEM((40,)), SEM((10,)),
+            buf(gain.shape, low), buf(gain.shape, low), buf(head_gains.shape, low), buf(head_gains.shape, wide),
+            buf(o.shape, wide), buf(d.shape, wide)],
         compiler_params=pltpu.CompilerParams(
             collective_id=0, has_side_effects=True, vmem_limit_bytes=67043328
         ),
-    )(x, cot, seg, q, k, v, g, u, o, d, gain, head_gains)
+    )(x, cot, seg, q, k, v, g, u, o, d, gain, gain_two, head_gains)
 
 
 def finish_kernel(sums_ref, *refs):
-    half = len(refs) // 2
+    half = (len(refs) - 3) // 2
     for src, dst in zip(refs[:half], refs[half : 2 * half]):
         dst[...] = src[...].astype(dst.dtype)
-    cut_ref = refs[2 * half]
+    attn_ref, ffn_ref, head_ref = refs[2 * half :]
     z = lax.axis_index("uly")
     head = 4 * lax.axis_index("fsdp") + lax.axis_index("blk")
-    share = sums_ref.shape[1] // 4
-    gain_rows = [sums_ref[pl.ds(head, 1), :], sums_ref[pl.ds(8 + head, 1), :]]
-    gain_rows = pltpu.roll(jnp.concatenate(gain_rows + [jnp.zeros((6, 128), jnp.float32)], axis=0), 128 - share * z, 1)
-    head_rows = pltpu.roll(sums_ref[16:24, :], 128 - (4 * head + z) * (share // 8), 1)
-    cut_ref[0:8] = gain_rows
-    cut_ref[8:16] = head_rows
-
-
-def finish_step(sums, *arrays):
+    piece, share = (attn_ref.shape[1], head_ref.shape[1])
+    rows = [sums_ref[pl.ds(head, 1), :], sums_ref[pl.ds(8 + head, 1), :], jnp.zeros((6, 128), jnp.float32)]
+    rows = pltpu.roll(jnp.concatenate(rows, axis=0), 128 - piece * z, 1)
+    attn_ref[...] = rows[0:1, :piece]
+    ffn_ref[...] = rows[1:2, :piece]
+    head_ref[...] = pltpu.roll(sums_ref[16:24, :], 128 - (4 * head + z) * share, 1)[0:2, :share]
+
+
+def finish_step(piece, share, sums, *arrays):
     return pl.pallas_call(
         finish_kernel,
         name="finish_step",
         out_shape=tuple(
             jax.ShapeDtypeStruct(v.shape, v.dtype if i < 2 else jnp.float32) for i, v in enumerate(arrays)
         )
-        + (jax.ShapeDtypeStruct((16, 128), jnp.float32),),
+        + tuple(jax.ShapeDtypeStruct(v, jnp.float32) for v in ((1, piece), (1, piece), (2, share))),
         in_specs=[VMEM] * (1 + len(arrays)),
-        out_specs=(VMEM,) * (1 + len(arrays)),
+        out_specs=(VMEM,) * (3 + len(arrays)),
     )(sums, *arrays)
 
 
@@ -1292,24 +1316,20 @@
     inputs, segments, attn_gain, head_gains, query_weight, key_matrix, value_matrix, out_weight,
     ffn_gain, gate_weight, up_weight, down_weight, cotangent,
 ):
-    head_dim = head_gains.shape[1]
-    z = lax.axis_index("uly")
-    piece = attn_gain.shape[0]
-    pair = jnp.stack([attn_gain, ffn_gain]).astype(jnp.float32)
-    spot = (jnp.arange(128, dtype=jnp.int32) // piece == z)[None]
-    gains_own = jnp.where(spot, jnp.tile(pair, (1, 128 // piece)), 0.0)
-    gains_own = jnp.concatenate([gains_own, jnp.zeros((6, 128), jnp.float32)], axis=0)
     outputs, grad_inputs, q_grad, k_grad, v_grad, g_grad, u_grad, sums, out_grad, down_grad = layer_step(
-        inputs, cotangent, segments, query_weight, key_matrix, value_matrix, gate_weight, up_weight, out_weight, down_weight, gains_own, head_gains.astype(jnp.float32),
-    )
-    outputs, grad_inputs, q_grad, k_grad, v_grad, out_grad, g_grad, u_grad, down_grad, cut = finish_step(
-        sums, outputs, grad_inputs, q_grad, k_grad, v_grad, out_grad, g_grad, u_grad, down_grad
-    )
-    attn_gain_grad, ffn_gain_grad = (cut[0, :piece], cut[1, :piece])
-    head_gain_grad = cut[8:10, : head_dim // 32]
+        inputs, cotangent, segments, query_weight, key_matrix, value_matrix, gate_weight, up_weight,
+        out_weight, down_weight, attn_gain[None], ffn_gain[None], head_gains,
+    )
+    (
+        outputs, grad_inputs, q_grad, k_grad, v_grad, out_grad, g_grad, u_grad, down_grad, attn_gain_grad,
+        ffn_gain_grad, head_gain_grad,
+    ) = finish_step(
+        attn_gain.shape[0], head_gains.shape[1] // 32, sums, outputs, grad_inputs, q_grad, k_grad, v_grad,
+        out_grad, g_grad, u_grad, down_grad,
+    )
     return (
-        outputs, grad_inputs, attn_gain_grad, head_gain_grad, q_grad, k_grad, v_grad, out_grad,
-        ffn_gain_grad, g_grad, u_grad, down_grad,
+        outputs, grad_inputs, attn_gain_grad[0], head_gain_grad, q_grad, k_grad, v_grad, out_grad,
+        ffn_gain_grad[0], g_grad, u_grad, down_grad,
     )
 
 

time: 180 us -> 174 us (0.967)
  local copies, waits for them, and re-layouts: 4.5 us -> 0 us
where the time goes in v6:
time: 174 us
  Pallas kernels  173 us (99%)
    pallas_call x1, Pallas kernels, layer_step(): pl.pallas_call(layer_kernel, name='layer_step', out_shape=(shape(x.shape,...  170 us

profile of v6, /device:TPU:0, one launch (start us, length us, event | category | flops | bytes accessed | tf_op | source)
XLA Modules:
  0.0 173.5 jit_solution(3728937740762953405)
XLA Ops:
  0.6 169.7 %layer_step.1 = (bf16[2,64,1024]{2,1,0:T(8,128)(2,1)}, bf16[2,64,1024]{2,1,0:T(8,128)(2,1)}, bf16[32,2048]{1,0:T(8,128)(2,1)}, bf16[32,1024]{1,0:T(8,128)(2,1)},...) custom-call(bf16[2,64,1024]{2,1,0:T(8,128)(2,1)} %x_ref.1, ...), custom_call_target="tpu_custom_call" | custom-call | tf_op jit(solution)/shard_map/layer_step/pallas_call | solution.py:1241
  170.4 3.0 %finish_step.1 = (bf16[2,64,1024]{2,1,0:T(8,128)(2,1)}, bf16[2,64,1024]{2,1,0:T(8,128)(2,1)}, f32[32,2048]{1,0:T(8,128)}, f32[32,1024]{1,0:T(8,128)}, f32[32,102...) custom-call(f32[24,128]{1,0:T(8,128)} %get-tuple-element.34.sums_ref, ...), custom_call_target="tpu_custom_call" | custom-call | tf_op jit(solution)/shard_map/finish_step/pallas_call | solution.py:1303

commit v7 on v6

--- a/solution.py
+++ b/solution.py
@@ -557,17 +557,43 @@
         sends.go_if(me.z >= dz, src, part(me.z), sems.at[0, dz + 1], sems.at[1, dz + 1], me.line(4 - dz))
 
 
-def line_spread_first(me, sends, src, part, sems, second=False):
-    outer, inner = outer_inner(me)
-    for dz in (2, 1):
-        for up in (True, False):
-            fits = me.z < 4 - dz if up else me.z >= dz
-            outward = me.z == 2 if up else me.z == 1
-            early = jnp.logical_or(outer, outward) if dz == 1 else outer
-            now = jnp.logical_not(early) if second else early
-            k = dz - 1 if up else dz + 1
-            target = me.line(dz) if up else me.line(4 - dz)
-            sends.go_if(jnp.logical_and(fits, now), src, part(me.z), sems.at[0, k], sems.at[1, k], target)
+def relay_spread(me, sends, src, part, sems):
+    outer, _ = outer_inner(me)
+    mine = part(me.z)
+    for up, far in ((True, me.z == 0), (False, me.z == 3)):
+        k = 1 if up else 3
+        sends.go_if(far, src, mine, sems.at[0, k], sems.at[1, k], me.line(2))
+        near = me.z < 3 if up else me.z > 0
+        k = 0 if up else 2
+        sends.go_if(near, src, mine, sems.at[0, k], sems.at[1, k], me.line(1 if up else 3))
+
+
+def relay_forward(me, sends, part, sems):
+    _, inner = outer_inner(me)
+    ref = part((7 - me.z) % 4)
+    pl.when(me.z == 1)(lambda: arrived(ref, sems.at[1, 2]))
+    pl.when(me.z == 2)(lambda: arrived(ref, sems.at[1, 0]))
+    target = (me.x, me.block, (3 * me.z + 1) % 4)
+    for z, k in ((1, 3), (2, 1)):
+        sends.go_if(me.z == z, ref, ref, sems.at[0, k], sems.at[1, k], target)
+    line_forward(me, sends, part, sems)
+
+
+def relay_finish(me, part, sems):
+    z = me.z
+    low, high = (part((z + 3) % 4), part((z + 1) % 4))
+    pl.when(jnp.logical_or(z == 1, z == 3))(lambda: arrived(low, sems.at[1, 0]))
+    pl.when(jnp.logical_or(z == 0, z == 2))(lambda: arrived(high, sems.at[1, 2]))
+
+    @pl.when(z == 3)
+    def _():
+        arrived(part((z + 2) % 4), sems.at[1, 1])
+        arrived(high, sems.at[1, 4])
+
+    @pl.when(z == 0)
+    def _():
+        arrived(part((z + 2) % 4), sems.at[1, 3])
+        arrived(low, sems.at[1, 4])
 
 
 def line_forward(me, sends, part, sems):
@@ -874,12 +900,11 @@
     d_part = lambda k: df.at[k]
     gate_part = lambda k: guf.at[:, k, :, pl.ds(0, ff)]
     up_part = lambda k: guf.at[:, k, :, pl.ds(ff, ff)]
-    line_spread_first(me, sends, qkv_part(z), qkv_part, zq)
+    line_spread(me, sends, qkv_part(z), qkv_part, zq)
     for turn in (1, 3, 2):
         k = (z + turn) % 4
         arrived(xf.at[me.block, k, x], pr.at[0, k])
         piece_start(me, sends, xf, turn, xas, xar)
-    line_spread_first(me, sends, qkv_part(z), qkv_part, zq, second=True)
     line_spread(me, sends, o_ref, o_part, zo)
     piece_relay(me, sends, xf, xas, xar, PIECES[:2])
     line_forward(me, sends, qkv_part, zq)
@@ -946,7 +971,7 @@
         t = me.index(*d)
         for n in (0, 1):
             arrived(guf.at[t, z, :, pl.ds(n * ff, ff)], ur.at[2 * i + n])
-    line_spread(me, sends, gate_part(z), gate_part, zg)
+    relay_spread(me, sends, gate_part(z), gate_part, zg)
     line_spread(me, sends, up_part(z), up_part, zu)
     spread_relay(me, sends, cf, as_.at[1], ar.at[1])
     @pl.loop(0, 4)
@@ -999,7 +1024,7 @@
     for b in range(4):
         half_block(me, part, sib1, hs1, hr1, b, early)
     half_out(me, early, part, sib1, out1, came1, hs1, hr1)
-    line_forward(me, sends, gate_part, zg)
+    relay_forward(me, sends, gate_part, zg)
     half_relay(me, early, part, sib1, out1, came1, hs1, hr1)
     middle = xf[me.block, :, x].astype(wide_t) + half_in(me, part, sib1, came1, hr1)
     mid[...] = middle
@@ -1013,7 +1038,7 @@
     spread_far(me, sends, nf, as_.at[2], ar.at[2])
     spread_finish(me, nf, ar.at[2])
     own_n.wait()
-    line_finish(me, gate_part, zg)
+    relay_finish(me, gate_part, zg)
     line_finish(me, up_part, zu)
 
     @pl.loop(0, 4)

time: 174 us -> 173 us (level)
  no operation moved by 1% of the time
where the time goes in v7:
time: 173 us
  Pallas kernels  172 us (99%)
    pallas_call x1, Pallas kernels, layer_step(): pl.pallas_call(layer_kernel, name='layer_step', out_shape=(shape(x.shape,...  169 us

profile of v7, /device:TPU:0, one launch (start us, length us, event | category | flops | bytes accessed | tf_op | source)
XLA Modules:
  0.0 173.1 jit_solution(3998455337511913689)
XLA Ops:
  0.6 169.2 %layer_step.1 = (bf16[2,64,1024]{2,1,0:T(8,128)(2,1)}, bf16[2,64,1024]{2,1,0:T(8,128)(2,1)}, bf16[32,2048]{1,0:T(8,128)(2,1)}, bf16[32,1024]{1,0:T(8,128)(2,1)},...) custom-call(bf16[2,64,1024]{2,1,0:T(8,128)(2,1)} %x_ref.1, ...), custom_call_target="tpu_custom_call" | custom-call | tf_op jit(solution)/shard_map/layer_step/pallas_call | solution.py:1266
  169.9 3.0 %finish_step.1 = (bf16[2,64,1024]{2,1,0:T(8,128)(2,1)}, bf16[2,64,1024]{2,1,0:T(8,128)(2,1)}, f32[32,2048]{1,0:T(8,128)}, f32[32,1024]{1,0:T(8,128)}, f32[32,102...) custom-call(f32[24,128]{1,0:T(8,128)} %get-tuple-element.34.sums_ref, ...), custom_call_target="tpu_custom_call" | custom-call | tf_op jit(solution)/shard_map/finish_step/pallas_call | solution.py:1328

commit v8 on v7

--- a/solution.py
+++ b/solution.py
@@ -1207,6 +1207,7 @@
     for i, d in enumerate(PLANE[1:]):
         sends.go(pack, packs.at[i], gs.at[11 + i], gr.at[11 + i], me.peer(*d))
     gi_s[...] = (gmid[...] + norm_back(grad, rows, gain_one, r)).astype(low)
+    permute_out(me, gi_s, gx_ref, cs.at[1], cr.at[1])
     total = pack[...]
     for i in range(7):
         arrived(packs.at[i], gr.at[11 + i])
@@ -1214,7 +1215,6 @@
     packs[7] = total
     for turn in TURNS:
         sends.go(packs.at[7], linep.at[turn - 1], gs.at[17 + turn], gr.at[17 + turn], me.line(turn))
-    permute_out(me, gi_s, gx_ref, cs.at[1], cr.at[1])
     backs = (((dq_ref, wide, 0),), ((dk_ref, narrow, 0), (dv_ref, narrow, narrow)))
     for block in (0, 1):
         reduce_total(me, own_dw[block], w_came.at[block], w_total, rw.at[block])

time: 173 us -> 173 us (level)
  no operation moved by 1% of the time
where the time goes in v8:
time: 173 us
  Pallas kernels  172 us (99%)
    pallas_call x1, Pallas kernels, layer_step(): pl.pallas_call(layer_kernel, name='layer_step', out_shape=(shape(x.shape,...  169 us

profile of v8, /device:TPU:0, one launch (start us, length us, event | category | flops | bytes accessed | tf_op | source)
XLA Modules:
  0.0 172.6 jit_solution(8230850412730320661)
XLA Ops:
  0.6 168.8 %layer_step.1 = (bf16[2,64,1024]{2,1,0:T(8,128)(2,1)}, bf16[2,64,1024]{2,1,0:T(8,128)(2,1)}, bf16[32,2048]{1,0:T(8,128)(2,1)}, bf16[32,1024]{1,0:T(8,128)(2,1)},...) custom-call(bf16[2,64,1024]{2,1,0:T(8,128)(2,1)} %x_ref.1, ...), custom_call_target="tpu_custom_call" | custom-call | tf_op jit(solution)/shard_map/layer_step/pallas_call | solution.py:1266
  169.4 3.0 %finish_step.1 = (bf16[2,64,1024]{2,1,0:T(8,128)(2,1)}, bf16[2,64,1024]{2,1,0:T(8,128)(2,1)}, f32[32,2048]{1,0:T(8,128)}, f32[32,1024]{1,0:T(8,128)}, f32[32,102...) custom-call(f32[24,128]{1,0:T(8,128)} %get-tuple-element.34.sums_ref, ...), custom_call_target="tpu_custom_call" | custom-call | tf_op jit(solution)/shard_map/finish_step/pallas_call | solution.py:1328
